TPU v7x, 256 devices: a whole 4x4x8 slice. The times are simulated.
256 devices in a mesh: depth: 64 (over x, z, core), tile: 4 (over y).
Axes of the slice: x: 4, y: 4, z: 8, core: 2. Of those that a mesh axis runs over, the one named last changes fastest.
Arguments:
- brick_image: float32 [64, 4, 512, 512], P('depth', None, 'tile'), may hold values from 0 to 0.08
- order: int32 [64], replicated, may hold values from 0 to 63, each once
- active: int32 [64, 4], replicated, may hold values 0 or 1
Outputs:
- final_image: float32 [4, 512, 512], replicated
All inputs are finite; a program needn't handle non-finite values.
Results may differ from a plain program's by a relative error of at most 0.00002.
Values sent between devices are 32-bit elements; how exact they have to be, the bound alone decides.
No kernel may reach another device: no remote copies, remote signals or barrier semaphores. Data moves between devices by JAX's collectives and lax.ppermute only.
A program may use at most 64 MiB of HBM per device.

v0:
```python
import jax
import jax.numpy as jnp
from jax import lax
from jax.sharding import Mesh
from jax.sharding import PartitionSpec as P

DEPTH = ("depth_0", "depth_1", "depth_2")


def in_order(pieces, dim):
    dims = list(pieces.shape[1:])
    dims[dim] *= pieces.shape[0]
    return jnp.moveaxis(pieces, 0, dim).reshape(dims)


def sent_to_all(shard, axis):
    count = lax.axis_size(axis)
    return lax.all_to_all(
        jnp.broadcast_to(shard[None], (count, *shard.shape)), axis, 0, 0, tiled=True
    )


def collect(shard, axis, dim):
    return in_order(sent_to_all(shard, axis), dim)


def stacked_from(shard, axes, turns):
    pieces = shard[None]
    for k in turns:
        pieces = lax.all_gather(pieces, axes[k], axis=0, tiled=True)
    held = [lax.axis_size(axes[k]) for k in reversed(turns)]
    pieces = pieces.reshape(*held, *shard.shape)
    turned = sorted(range(len(turns)), key=lambda place: turns[len(turns) - 1 - place])
    return pieces.transpose(*turned, *range(len(turns), pieces.ndim)).reshape(-1, *shard.shape)


def whole_of(shard, axes, turns, dim):
    return in_order(stacked_from(shard, axes, turns), dim)


def composite_over(near_part, far_part):
    return near_part + (1.0 - near_part[:, 3:4]) * far_part


def shards(brick_image, order, active):
    rank_count = lax.axis_size(DEPTH)
    own_rank = lax.axis_index(DEPTH)
    own_tile = lax.axis_index("tile")
    own_block = brick_image[0]
    channels, tile_rows, columns = own_block.shape
    pixels = tile_rows * columns
    piece_len = pixels // rank_count
    own_flag = active[own_rank, own_tile].astype(jnp.float32)
    outgoing = (own_block * own_flag).reshape(1, channels, rank_count, piece_len)
    layers = lax.all_to_all(outgoing, DEPTH, split_axis=2, concat_axis=0, tiled=True)[:, :, 0, :][
        order
    ]
    for level in range(rank_count.bit_length() - 1):
        layers = composite_over(layers[0::2], layers[1::2])
    composite = layers[0]
    grouped = collect(composite[:, None, :], "tile", 1)
    gathered = whole_of(grouped, DEPTH, (0, 1, 2), 2)
    final_image = gathered.reshape(channels, -1, columns)
    return final_image


def solution(mesh):
    split = Mesh(
        mesh.devices.reshape(4, 8, 2, mesh.shape["tile"]), ("depth_0", "depth_1", "depth_2", "tile")
    )
    return jax.shard_map(
        shards,
        mesh=split,
        in_specs=(P(DEPTH, None, "tile", None), P(), P()),
        out_specs=P(),
        check_vma=False,
    )
```

profile of v0, /device:TPU:1, one launch (start us, length us, event | category | flops | bytes accessed | tf_op | source)
XLA Modules:
  0.0 153.9 jit_solution(17242035934742367514)
XLA Ops:
  6.5 1.3 dynamic_slice.3
  8.4 0.0 copy-start
  8.5 1.3 broadcast_multiply_fusion
  9.8 0.3 mul.86
  10.2 1.6 %copy.9 = f32[1,4,64,1024]{3,1,0,2:T(4,128)} copy(f32[1,4,64,1024]{3,2,1,0:T(8,128)S(1)} %mul.86) | data formatting | bytes 2097152 | tf_op jit(solution)/shard_map/mul | solution.py:54
  11.8 13.0 %all-to-all-start = ((f32[1,4,64,1024]{3,1,0,2:T(4,128)}), f32[1,4,64,1024]{3,1,0,2:T(4,128)S(1)}, u32[]{:S(2)}, u32[]{:S(2)}) async-start(f32[1,4,64,1024]{3,1,0,2:T(4,128)} %copy.9), calls=%async_computation | async-start | bytes 2097152 | tf_op jit(solution)/shard_map/all_to_all | solution.py:55
  24.8 0.0 all-gather.4.cloned.1.call-start
  24.8 0.0 copy-done
  24.9 28.4 %all-to-all-done = f32[1,4,64,1024]{3,1,0,2:T(4,128)S(1)} async-done(((f32[1,4,64,1024]{3,1,0,2:T(4,128)}), f32[1,4,64,1024]{3,1,0,2:T(4,128)S(1)}, u32[]{:S(2)}, u32[]{:S(2)}) %all-to-all-start) | async-done | bytes 1048608 | tf_op jit(solution)/shard_map/all_to_all | solution.py:55
  53.3 1.2 gather_fusion
  54.5 0.2 slice_subtract_fusion
  54.8 0.2 multiply_add_fusion
  55.0 0.1 slice_subtract_fusion.1
  55.1 0.1 multiply_add_fusion.1
  55.3 0.1 multiply_add_fusion.2
  55.6 8.5 %all_to_all.20 = f32[4,4,1,1024]{3,1,2,0:T(4,128)S(1)} all-to-all(f32[4,4,1,1024]{3,1,2,0:T(4,128)S(1)} %broadcast_in_dim.12), channel_id=1, replica_groups=mesh['depth_0'=4,'depth_1'=8,'depth_2'=2,'tile'=4] {'tile'}, dimensions={0} | all-to-all | bytes 131072 | tf_op jit(solution)/shard_map/all_to_all | solution.py:18
  64.1 10.6 %all-gather = f32[16,4,1,1024]{3,1,2,0:T(4,128)} all-gather(f32[4,4,1,1024]{3,1,2,0:T(4,128)S(1)} %copy.10), channel_id=2, replica_groups=mesh['depth_0'=4,'depth_1'=8,'depth_2'=2,'tile'=4] {'depth_0'}, dimensions={0}, use_global_device_ids=true | all-gather | bytes 327680 | tf_op jit(solution)/shard_map/all_gather | solution.py:30
  74.6 0.0 all-gather.4.cloned.1.call-update
  74.7 0.0 all-gather.6.cloned.1.call-start
  74.7 35.6 %all-gather.4.cloned.1.call-done = f32[32,4,4,1024]{3,2,1,0:T(4,128)} async-done(((f32[4,4,4,1024]{3,2,1,0:T(4,128)}), f32[32,4,4,1024]{3,2,1,0:T(4,128)}) %all-gather.4.cloned.1.call-update) | async-done | bytes 2097168 | tf_op jit(solution)/shard_map/all_gather | solution.py:30
  110.3 0.0 all-gather.6.cloned.1.call-update
  110.4 24.3 %all-gather.6.cloned.1.call-done = f32[64,4,4,1024]{3,2,1,0:T(4,128)} async-done(((f32[32,4,4,1024]{3,2,1,0:T(4,128)}), f32[64,4,4,1024]{3,2,1,0:T(4,128)}) %all-gather.6.cloned.1.call-update) | async-done | bytes 4194320 | tf_op jit(solution)/shard_map/all_gather | solution.py:30
  134.6 3.1 %copy.11 = f32[4,8,2,4,4,1024]{5,4,3,2,1,0:T(4,128)S(1)} copy(f32[4,8,2,4,4,1024]{5,4,3,0,1,2:T(4,128)} %bitcast.38) | data formatting | bytes 8388608 | tf_op jit(solution)/shard_map/transpose | solution.py:34
  137.8 4.4 %copy.12 = f32[4,4,64,1024]{3,2,1,0:T(8,128)} copy(f32[4,4,64,1024]{3,1,0,2:T(4,128)S(1)} %bitcast.36) | data formatting | bytes 8388608 | tf_op jit(solution)/shard_map/transpose | solution.py:13
  142.1 4.9 %reshape_reshape.3 = f32[4,512,512]{2,1,0:T(8,128)} reshape(f32[4,4,64,1024]{3,2,1,0:T(8,128)} %copy.12) | data formatting | bytes 8388608 | tf_op jit(solution)/shard_map/reshape;reshape | solution.py:63
  (21 shorter events, 0.3 us)
Async XLA Ops:
  8.4 16.4 %copy-start = (s32[64]{0:T(128)S(1)}, s32[64]{0:T(128)}, u32[]{:S(2)}) copy-start(s32[64]{0:T(128)} %param.4) | copy-start | bytes 772
  11.8 41.5 %all-to-all-start = ((f32[1,4,64,1024]{3,1,0,2:T(4,128)}), f32[1,4,64,1024]{3,1,0,2:T(4,128)S(1)}, u32[]{:S(2)}, u32[]{:S(2)}) async-start(f32[1,4,64,1024]{3,1,0,2:T(4,128)} %copy.9), calls=%async_computation | async-start | bytes 2097152 | tf_op jit(solution)/shard_map/all_to_all | solution.py:55
  24.8 85.5 %all-gather.4.cloned.1.call-start = ((), (), s32[]{:S(2)}) async-start(), calls=%async_computation.2 | async-start | bytes 2359296 | tf_op jit(solution)/shard_map/all_gather | solution.py:30
  74.7 60.0 %all-gather.6.cloned.1.call-start = ((), (), s32[]{:S(2)}) async-start(), calls=%async_computation.3 | async-start | bytes 6291456 | tf_op jit(solution)/shard_map/all_gather | solution.py:30
Sparse Core Ops, SparseCore 0:
  74.8 35.4 all-gather.3
  112.1 22.4 all-gather.5
where the time goes:
time: 154 us
  waiting for transfers between devices  88.4 us (57%)
  blocking collectives  19 us (12%)
  local copies, waits for them, and re-layouts  17.1 us (11%)
  between operations  14.3 us (9%)
  starting transfers between devices  13.1 us (9%)
  other arithmetic  2.12 us (1%)
    all_gather x2, waiting for transfers between devices, stacked_from(): pieces = lax.all_gather(pieces, axes[k], axis=0, tiled=True)  59.9 us
    all_to_all x1, waiting for transfers between devices, shards(): lax.all_to_all(outgoing, DEPTH, split_axis=2, concat_axis=0, tiled=True)  28.4 us
    all_to_all x1, starting transfers between devices, shards(): lax.all_to_all(outgoing, DEPTH, split_axis=2, concat_axis=0, tiled=True)  13 us
    all_gather x1, blocking collectives, stacked_from(): pieces = lax.all_gather(pieces, axes[k], axis=0, tiled=True)  10.6 us
    all_to_all x1, blocking collectives, sent_to_all(): lax.all_to_all(jnp.broadcast_to(shard[None], (count, *shard.shape)), axis...  8.46 us
    another operation x1, local copies, waits for them, and re-layouts, shards(): final_image = gathered.reshape(channels, -1, columns)  4.92 us
    transpose x2, local copies, waits for them, and re-layouts, in_order(): return jnp.moveaxis(pieces, 0, dim).reshape(dims)  4.41 us
    transpose x1, local copies, waits for them, and re-layouts, stacked_from(): pieces.transpose(*turned, *range(len(turns), pieces.ndim))  3.15 us
  transfers between devices with their start and end apart: 3, of which 3 were waited for; matrix products, arithmetic and copies ran while one was open for 0% of the time, Pallas kernels for 0%

commit v1 on v0

v1 whole, which is shorter than its diff:
```python
import jax
import jax.numpy as jnp
from jax import lax
from jax.experimental import pallas as pl
from jax.experimental.pallas import tpu as pltpu
from jax.sharding import Mesh
from jax.sharding import PartitionSpec as P

X, Z, C, Y = "depth_0", "depth_1", "depth_2", "tile"
DEPTH = (X, Z, C)
PLANE = (X, C, Y)
STEPS = (0, -1, 1, -2)
MIB = 1 << 20


def params(limit):
    return pltpu.CompilerParams(vmem_limit_bytes=limit)


def shifted_z(value, by):
    n = lax.axis_size(Z)
    return lax.ppermute(value, Z, [(k, (k + by) % n) for k in range(n)])


def shifted_plane(value, by, second):
    nx, nc, ny = (lax.axis_size(a) for a in PLANE)
    pairs = []
    for x in range(nx):
        for y in range(ny):
            for c in range(nc):
                along_x = (c == 0) != second
                tx, ty = ((x + by) % nx, y) if along_x else (x, (y + by) % ny)
                pairs.append(((x * nc + c) * ny + y, (tx * nc + c) * ny + ty))
    return lax.ppermute(value, PLANE, pairs)


def other_core(value):
    return lax.ppermute(value, C, [(0, 1), (1, 0)])


def composite_kernel(order_ref, flag_ref, layers_ref, out_ref):
    count = layers_ref.shape[0]

    def step(k, accumulated):
        brick = order_ref[k]
        flag = flag_ref[brick].astype(jnp.float32)
        return tuple(
            a + (1.0 - accumulated[3]) * (layers_ref[brick, ch] * flag)
            for ch, a in enumerate(accumulated)
        )

    zero = jnp.zeros(layers_ref.shape[2:], jnp.float32)
    done = lax.fori_loop(0, count, step, (zero,) * 4, unroll=8)
    for ch in range(4):
        out_ref[ch] = done[ch]


def z_block_kernel(near_ref, far_ref, out_ref):
    z = lax.axis_index(Z)
    for slot, step in enumerate(STEPS):
        for ref, extra in ((near_ref, 0), (far_ref, 4)):
            place = lax.rem(z + step + extra + 8, 8)
            out_ref[:, pl.ds(pl.multiple_of(place * 8, 8), 8), :] = ref[slot]


def image_kernel(*refs):
    out_ref, sem = refs[-2:]
    parts = refs[:-2]
    half = len(parts) // 2
    x, c, y = (lax.axis_index(a) for a in PLANE)
    copies = []
    for which, ref in enumerate(parts):
        core = c if which < half else 1 - c
        kind = which % half
        second = (0, -1, 1, -2, -2)[kind]
        firsts = STEPS if kind < 3 else (STEPS[:2] if kind == 3 else STEPS[2:])
        for slot, first in enumerate(firsts):
            bx = lax.rem(x + jnp.where(core == 0, first, second) + 4, 4)
            by = lax.rem(y + jnp.where(core == 0, second, first) + 4, 4)
            row = pl.multiple_of(by * 128 + core * 64, 64)
            col = pl.multiple_of(bx * 128, 128)
            copy = pltpu.make_async_copy(
                ref.at[slot],
                out_ref.at[:, pl.ds(row, 64), pl.ds(col, 128)],
                sem.at[len(copies)],
            )
            copy.start()
            copies.append(copy)
    for copy in copies:
        copy.wait()


def shards(brick_image, order, active):
    flags = lax.dynamic_slice_in_dim(active, lax.axis_index(Y), 1, axis=1)[:, 0]
    own = brick_image[0]
    tiles = own.reshape(4, 2, 8, 8, 4, 128)
    outgoing = tiles.transpose(4, 2, 1, 0, 3, 5).reshape(64, 4, 8, 128)
    layers = lax.all_to_all(outgoing, DEPTH, split_axis=0, concat_axis=0, tiled=True)
    smem = pl.BlockSpec(memory_space=pltpu.SMEM)
    vmem = pl.BlockSpec(memory_space=pltpu.VMEM)
    anywhere = pl.BlockSpec(memory_space=pl.ANY)
    piece = pl.pallas_call(
        composite_kernel,
        out_shape=jax.ShapeDtypeStruct((4, 8, 128), jnp.float32),
        in_specs=[smem, smem, vmem],
        out_specs=vmem,
        compiler_params=params(4 * MIB),
        name="composite",
    )(order, flags, layers)

    near = jnp.stack([piece, *(shifted_z(piece, -s) for s in STEPS[1:])])
    far = shifted_z(near, 4)
    block = pl.pallas_call(
        z_block_kernel,
        out_shape=jax.ShapeDtypeStruct((4, 64, 128), jnp.float32),
        in_specs=[vmem, vmem],
        out_specs=vmem,
        compiler_params=params(4 * MIB),
        name="z_block",
    )(near, far)

    line = jnp.stack([block, *(shifted_plane(block, -s, False) for s in STEPS[1:])])
    before = shifted_plane(line, 1, True)
    after = shifted_plane(line, -1, True)
    across_a = shifted_plane(before[:2], 1, True)
    across_b = shifted_plane(after[2:], -1, True)
    held = (line, before, after, across_a, across_b)
    parts = (*held, *(other_core(part) for part in held))
    return pl.pallas_call(
        image_kernel,
        out_shape=jax.ShapeDtypeStruct((4, 512, 512), jnp.float32),
        in_specs=[anywhere] * len(parts),
        out_specs=anywhere,
        scratch_shapes=[pltpu.SemaphoreType.DMA((32,))],
        compiler_params=params(8 * MIB),
        name="image",
    )(*parts)


def solution(mesh):
    split = Mesh(mesh.devices.reshape(4, 8, 2, mesh.shape["tile"]), (X, Z, C, Y))
    return jax.shard_map(
        shards,
        mesh=split,
        in_specs=(P(DEPTH, None, Y, None), P(), P()),
        out_specs=P(),
        check_vma=False,
    )
```

time: 154 us -> 96.5 us (0.63)
  waiting for transfers between devices: 88.4 us -> 44.7 us
  starting transfers between devices: 13.1 us -> 45.9 us
  blocking collectives: 19 us -> 0 us
  local copies, waits for them, and re-layouts: 17.1 us -> 2.41 us
  between operations: 14.3 us -> 0.09 us
  Pallas kernels: 0 us -> 3.06 us
  other arithmetic: 2.12 us -> 0.05 us
    all_gather x2 -> x0, waiting for transfers between devices: 59.9 us -> none  [stacked_from(): pieces = lax.all_gather(pieces, axes[k], axis=0, tiled=True)]
    ppermute x0 -> x16, starting transfers between devices: none -> 33 us  [the longest x5 15.6 us: other_core(): return lax.ppermute(value, C, [(0, 1), (1, 0)])]
    ppermute x0 -> x16, waiting for transfers between devices: none -> 16.2 us  [the longest x4 7.91 us: shifted_z(): return lax.ppermute(value, Z, [(k, (k + by) % n) for k in range(n)])]
    all_gather x1 -> x0, blocking collectives: 10.6 us -> none  [stacked_from(): pieces = lax.all_gather(pieces, axes[k], axis=0, tiled=True)]
    all_to_all x1 -> x0, blocking collectives: 8.46 us -> none  [sent_to_all(): lax.all_to_all(jnp.broadcast_to(shard[None], (count, *shard.shape)), axis...]
    transpose x3 -> x0, local copies, waits for them, and re-layouts: 7.56 us -> none  [the longest x2 4.41 us: in_order(): return jnp.moveaxis(pieces, 0, dim).reshape(dims)]
    pallas_call x0 -> x3, Pallas kernels: none -> 3.06 us  [the longest x1 2.26 us: shards(): pl.pallas_call(image_kernel, out_shape=jax.ShapeDtypeStruct((4, 512, 512)...]
    another operation x1, local copies, waits for them, and re-layouts: 4.92 us -> 2.36 us  [shards(): tiles = own.reshape(4, 2, 8, 8, 4, 128)]
  transfers between devices with their start and end apart: 3 -> 17, of which waited for: 3 -> 9; matrix products, arithmetic and copies ran while one was open for 0% -> 0% of each run, Pallas kernels for 0% -> 0%
where the time goes in v1:
time: 96.5 us; the launch traced here: 96.3 us
  starting transfers between devices  45.9 us (48%)
  waiting for transfers between devices  44.7 us (46%)
  Pallas kernels  3.06 us (3%)
  local copies, waits for them, and re-layouts  2.41 us (2%)
    all_to_all x1, waiting for transfers between devices, shards(): lax.all_to_all(outgoing, DEPTH, split_axis=0, concat_axis=0, tiled=True)  28.5 us
    ppermute x5, starting transfers between devices, other_core(): return lax.ppermute(value, C, [(0, 1), (1, 0)])  15.6 us
    all_to_all x1, starting transfers between devices, shards(): lax.all_to_all(outgoing, DEPTH, split_axis=0, concat_axis=0, tiled=True)  13 us
    ppermute x7, starting transfers between devices, shifted_plane(): return lax.ppermute(value, PLANE, pairs)  11.4 us
    ppermute x4, waiting for transfers between devices, shifted_z(): return lax.ppermute(value, Z, [(k, (k + by) % n) for k in range(n)])  7.91 us
    ppermute x7, waiting for transfers between devices, shifted_plane(): return lax.ppermute(value, PLANE, pairs)  7.16 us
    ppermute x4, starting transfers between devices, shifted_z(): return lax.ppermute(value, Z, [(k, (k + by) % n) for k in range(n)])  5.95 us
    another operation x1, local copies, waits for them, and re-layouts, shards(): tiles = own.reshape(4, 2, 8, 8, 4, 128)  2.36 us
  transfers between devices with their start and end apart: 17, of which 9 were waited for; matrix products, arithmetic and copies ran while one was open for 0% of the time, Pallas kernels for 0%

profile of v1, /device:TPU:1, one launch (start us, length us, event | category | flops | bytes accessed | tf_op | source)
XLA Modules:
  0.0 96.3 jit_solution(16001978518376153889)
XLA Ops:
  0.0 0.0 copy-start
  0.0 0.0 copy-start.1
  0.0 2.4 %copy.4 = f32[4,2,8,8,4,128]{5,3,0,1,2,4:T(8,128)} copy(f32[4,2,8,8,4,128]{5,3,4,2,1,0:T(8,128)} %bitcast.16) | data formatting | bytes 2097152 | tf_op jit(solution)/shard_map/reshape;squeeze | solution.py:96
  2.4 13.0 %all-to-all-start = ((f32[64,4,8,128]{3,2,1,0:T(8,128)}), f32[64,4,8,128]{3,2,1,0:T(8,128)S(1)}, u32[]{:S(2)}, u32[]{:S(2)}) async-start(f32[64,4,8,128]{3,2,1,0:T(8,128)} %bitcast.3), calls=%async_computation | async-start | bytes 2097152 | tf_op jit(solution)/shard_map/all_to_all | solution.py:98
  15.4 0.0 copy-done
  15.4 28.5 %all-to-all-done.layers_ref = f32[64,4,8,128]{3,2,1,0:T(8,128)S(1)} async-done(((f32[64,4,8,128]{3,2,1,0:T(8,128)}), f32[64,4,8,128]{3,2,1,0:T(8,128)S(1)}, u32[]{:S(2)}, u32[]{:S(2)}) %all-to-all-start) | async-done | bytes 1048608 | tf_op jit(solution)/shard_map/all_to_all | solution.py:98
  43.9 0.0 copy-done.1
  43.9 0.8 composite.1
  44.7 0.1 collective-permute-start.2
  44.8 3.0 %collective-permute-start.1 = (f32[4,8,128]{2,1,0:T(8,128)S(1)}, f32[4,8,128]{2,1,0:T(8,128)S(1)}, u32[]{:S(2)}, u32[]{:S(2)}) collective-permute-start(f32[4,8,128]{2,1,0:T(8,128)S(1)} %composite.1), channel_id=1, source_target_pairs={{0,56},{8,0},{16,8},{24,16},{32,24},{40,32},{48,40},{56,48},{1,57}... | collective-permute-start | bytes 49160 | tf_op jit(solution)/shard_map/ppermute | solution.py:22
  47.7 0.0 collective-permute-start
  47.7 1.7 %collective-permute-done.2 = f32[4,8,128]{2,1,0:T(8,128)S(1)} collective-permute-done((f32[4,8,128]{2,1,0:T(8,128)S(1)}, f32[4,8,128]{2,1,0:T(8,128)S(1)}, u32[]{:S(2)}, u32[]{:S(2)}) %collective-permute-start.2) | collective-permute-done | bytes 16416 | tf_op jit(solution)/shard_map/ppermute | solution.py:22
  49.4 0.0 collective-permute-done.1
  49.4 2.1 %collective-permute-done = f32[4,8,128]{2,1,0:T(8,128)S(1)} collective-permute-done((f32[4,8,128]{2,1,0:T(8,128)S(1)}, f32[4,8,128]{2,1,0:T(8,128)S(1)}, u32[]{:S(2)}, u32[]{:S(2)}) %collective-permute-start) | collective-permute-done | bytes 16416 | tf_op jit(solution)/shard_map/ppermute | solution.py:22
  51.5 2.9 %collective-permute-start.3 = (f32[4,4,8,128]{3,2,1,0:T(8,128)S(1)}, f32[4,4,8,128]{3,2,1,0:T(8,128)S(1)}, u32[]{:S(2)}, u32[]{:S(2)}) collective-permute-start(f32[4,4,8,128]{3,2,1,0:T(8,128)S(1)} %pad_maximum_fusion.1.near_ref), channel_id=1, source_target_pairs={{0,32},{8,40},{16,48},{24,56},{32,0},{40,8},{48,16},{56,24},{1,33}... | collective-permute-start | bytes 196616 | tf_op jit(solution)/shard_map/ppermute | solution.py:22
  54.4 4.1 %collective-permute-done.3.far_ref = f32[4,4,8,128]{3,2,1,0:T(8,128)S(1)} collective-permute-done((f32[4,4,8,128]{3,2,1,0:T(8,128)S(1)}, f32[4,4,8,128]{3,2,1,0:T(8,128)S(1)}, u32[]{:S(2)}, u32[]{:S(2)}) %collective-permute-start.3) | collective-permute-done | bytes 65568 | tf_op jit(solution)/shard_map/ppermute | solution.py:22
  58.6 3.0 %collective-permute-start.6 = (f32[4,64,128]{2,1,0:T(8,128)S(1)}, f32[4,64,128]{2,1,0:T(8,128)S(1)}, u32[]{:S(2)}, u32[]{:S(2)}) collective-permute-start(f32[4,64,128]{2,1,0:T(8,128)S(1)} %z_block.1), channel_id=1, source_target_pairs={{0,128},{4,6},{1,129},{5,7},{2,130},{6,4},{3,131},{7,5},{64,192},{... | collective-permute-start | bytes 393224 | tf_op jit(solution)/shard_map/ppermute | solution.py:34
  61.6 0.8 collective-permute-start.5
  62.3 0.7 collective-permute-start.4
  63.0 0.9 collective-permute-done.6
  64.0 1.7 %collective-permute-done.5 = f32[4,64,128]{2,1,0:T(8,128)S(1)} collective-permute-done((f32[4,64,128]{2,1,0:T(8,128)S(1)}, f32[4,64,128]{2,1,0:T(8,128)S(1)}, u32[]{:S(2)}, u32[]{:S(2)}) %collective-permute-start.5) | collective-permute-done | bytes 131104 | tf_op jit(solution)/shard_map/ppermute | solution.py:34
  65.7 1.9 %collective-permute-done.4 = f32[4,64,128]{2,1,0:T(8,128)S(1)} collective-permute-done((f32[4,64,128]{2,1,0:T(8,128)S(1)}, f32[4,64,128]{2,1,0:T(8,128)S(1)}, u32[]{:S(2)}, u32[]{:S(2)}) %collective-permute-start.4) | collective-permute-done | bytes 131104 | tf_op jit(solution)/shard_map/ppermute | solution.py:34
  67.7 3.3 %collective-permute-start.8 = (f32[4,4,64,128]{3,2,1,0:T(8,128)S(1)}, f32[4,4,64,128]{3,2,1,0:T(8,128)S(1)}, u32[]{:S(2)}, u32[]{:S(2)}) collective-permute-start(f32[4,4,64,128]{3,2,1,0:T(8,128)S(1)} %pad_maximum_fusion.refs_0_), channel_id=1, source_target_pairs={{0,3},{4,196},{1,0},{5,197},{2,1},{6,198},{3,2},{7,199},{64,67},{6... | collective-permute-start | bytes 1572872 | tf_op jit(solution)/shard_map/ppermute | solution.py:34
  71.1 0.0 collective-permute-start.7
  71.1 3.6 %collective-permute-start.11 = (f32[4,4,64,128]{3,2,1,0:T(8,128)S(1)}, f32[4,4,64,128]{3,2,1,0:T(8,128)S(1)}, u32[]{:S(2)}, u32[]{:S(2)}) collective-permute-start(f32[4,4,64,128]{3,2,1,0:T(8,128)S(1)} %pad_maximum_fusion.refs_0_), channel_id=1, source_target_pairs={{0,4},{4,0},{1,5},{5,1},{2,6},{6,2},{3,7},{7,3},{8,12},{12,8},{9,1... | collective-permute-start | bytes 1572872 | tf_op jit(solution)/shard_map/ppermute | solution.py:38
  74.7 2.5 %collective-permute-done.8.refs_2_ = f32[4,4,64,128]{3,2,1,0:T(8,128)S(1)} collective-permute-done((f32[4,4,64,128]{3,2,1,0:T(8,128)S(1)}, f32[4,4,64,128]{3,2,1,0:T(8,128)S(1)}, u32[]{:S(2)}, u32[]{:S(2)}) %collective-permute-start.8) | collective-permute-done | bytes 524320 | tf_op jit(solution)/shard_map/ppermute | solution.py:34
  77.2 3.5 %collective-permute-start.10 = (f32[2,4,64,128]{3,2,1,0:T(8,128)S(1)}, f32[2,4,64,128]{3,2,1,0:T(8,128)S(1)}, u32[]{:S(2)}, u32[]{:S(2)}) collective-permute-start(f32[2,4,64,128]{3,2,1,0:T(8,128)S(1)} %slice.9), channel_id=1, source_target_pairs={{0,3},{4,196},{1,0},{5,197},{2,1},{6,198},{3,2},{7,199},{64,67},{6... | collective-permute-start | bytes 786440 | tf_op jit(solution)/shard_map/ppermute | solution.py:34
  80.7 0.0 collective-permute-done.7.refs_1_
  80.7 0.1 collective-permute-start.9
  80.8 4.5 %collective-permute-start.13 = (f32[4,4,64,128]{3,2,1,0:T(8,128)S(1)}, f32[4,4,64,128]{3,2,1,0:T(8,128)S(1)}, u32[]{:S(2)}, u32[]{:S(2)}) collective-permute-start(f32[4,4,64,128]{3,2,1,0:T(8,128)S(1)} %collective-permute-done.8.refs_2_), channel_id=1, source_target_pairs={{0,4},{4,0},{1,5},{5,1},{2,6},{6,2},{3,7},{7,3},{8,12},{12,8},{9,1... | collective-permute-start | bytes 1572872 | tf_op jit(solution)/shard_map/ppermute | solution.py:38
  85.4 0.1 collective-permute-start.12
  85.5 0.0 collective-permute-done.10.refs_4_
  85.5 3.6 %collective-permute-start.15 = (f32[2,4,64,128]{3,2,1,0:T(8,128)S(1)}, f32[2,4,64,128]{3,2,1,0:T(8,128)S(1)}, u32[]{:S(2)}, u32[]{:S(2)}) collective-permute-start(f32[2,4,64,128]{3,2,1,0:T(8,128)S(1)} %collective-permute-done.10.refs_4_), channel_id=1, source_target_pairs={{0,4},{4,0},{1,5},{5,1},{2,6},{6,2},{3,7},{7,3},{8,12},{12,8},{9,1... | collective-permute-start | bytes 786440 | tf_op jit(solution)/shard_map/ppermute | solution.py:38
  89.0 0.0 collective-permute-done.9.refs_3_
  89.0 3.8 %collective-permute-start.14 = (f32[2,4,64,128]{3,2,1,0:T(8,128)S(1)}, f32[2,4,64,128]{3,2,1,0:T(8,128)S(1)}, u32[]{:S(2)}, u32[]{:S(2)}) collective-permute-start(f32[2,4,64,128]{3,2,1,0:T(8,128)S(1)} %collective-permute-done.9.refs_3_), channel_id=1, source_target_pairs={{0,4},{4,0},{1,5},{5,1},{2,6},{6,2},{3,7},{7,3},{8,12},{12,8},{9,1... | collective-permute-start | bytes 786440 | tf_op jit(solution)/shard_map/ppermute | solution.py:38
  92.8 0.0 collective-permute-done.11.refs_5_
  92.8 0.0 collective-permute-done.15.refs_9_
  92.8 0.0 collective-permute-done.13.refs_7_
  92.8 1.1 %collective-permute-done.14.refs_8_ = f32[2,4,64,128]{3,2,1,0:T(8,128)S(1)} collective-permute-done((f32[2,4,64,128]{3,2,1,0:T(8,128)S(1)}, f32[2,4,64,128]{3,2,1,0:T(8,128)S(1)}, u32[]{:S(2)}, u32[]{:S(2)}) %collective-permute-start.14) | collective-permute-done | bytes 262176 | tf_op jit(solution)/shard_map/ppermute | solution.py:38
  94.0 0.0 collective-permute-done.12.refs_6_
  94.0 2.3 %image.1 = f32[4,512,512]{2,1,0:T(8,128)} custom-call(f32[4,4,64,128]{3,2,1,0:T(8,128)S(1)} %pad_maximum_fusion.refs_0_, f32[4,4,64,128]{3,2,1,0:T(8,128)S(1)} %collective-permute-done.7.refs_1_, f32[4,4,64,128]{3,2,1,0:T(8,128)S(1)} %collective-permute-done.8.refs_2_, f32[2,4,64,128]{3,2,1,0:T(8,128)S(1)} %collective-permute-done.9.refs_3_, ...), custom_call_target="tpu_custom_call" | custom-call | tf_op jit(solution)/shard_map/image/pallas_call | solution.py:129
  (6 shorter events, 0.1 us)
Async XLA Ops:
  0.0 15.4 %copy-start = (s32[64,4]{0,1:T(4,128)S(1)}, s32[64,4]{0,1:T(4,128)}, u32[]{:S(2)}) copy-start(s32[64,4]{0,1:T(4,128)} %param.5) | copy-start | bytes 3076
  0.0 43.9 %copy-start.1 = (s32[64]{0:T(128)S(1)}, s32[64]{0:T(128)}, u32[]{:S(2)}) copy-start(s32[64]{0:T(128)} %order_ref.1) | copy-start | bytes 772
  2.4 41.5 %all-to-all-start = ((f32[64,4,8,128]{3,2,1,0:T(8,128)}), f32[64,4,8,128]{3,2,1,0:T(8,128)S(1)}, u32[]{:S(2)}, u32[]{:S(2)}) async-start(f32[64,4,8,128]{3,2,1,0:T(8,128)} %bitcast.3), calls=%async_computation | async-start | bytes 2097152 | tf_op jit(solution)/shard_map/all_to_all | solution.py:98
  44.7 4.8 %collective-permute-start.2 = (f32[4,8,128]{2,1,0:T(8,128)S(1)}, f32[4,8,128]{2,1,0:T(8,128)S(1)}, u32[]{:S(2)}, u32[]{:S(2)}) collective-permute-start(f32[4,8,128]{2,1,0:T(8,128)S(1)} %composite.1), channel_id=1, source_target_pairs={{0,16},{8,24},{16,32},{24,40},{32,48},{40,56},{48,0},{56,8},{1,17}... | collective-permute-start | bytes 49160 | tf_op jit(solution)/shard_map/ppermute | solution.py:22
  44.8 4.7 %collective-permute-start.1 = (f32[4,8,128]{2,1,0:T(8,128)S(1)}, f32[4,8,128]{2,1,0:T(8,128)S(1)}, u32[]{:S(2)}, u32[]{:S(2)}) collective-permute-start(f32[4,8,128]{2,1,0:T(8,128)S(1)} %composite.1), channel_id=1, source_target_pairs={{0,56},{8,0},{16,8},{24,16},{32,24},{40,32},{48,40},{56,48},{1,57}... | collective-permute-start | bytes 49160 | tf_op jit(solution)/shard_map/ppermute | solution.py:22
  47.7 3.8 %collective-permute-start = (f32[4,8,128]{2,1,0:T(8,128)S(1)}, f32[4,8,128]{2,1,0:T(8,128)S(1)}, u32[]{:S(2)}, u32[]{:S(2)}) collective-permute-start(f32[4,8,128]{2,1,0:T(8,128)S(1)} %composite.1), channel_id=1, source_target_pairs={{0,8},{8,16},{16,24},{24,32},{32,40},{40,48},{48,56},{56,0},{1,9},... | collective-permute-start | bytes 49160 | tf_op jit(solution)/shard_map/ppermute | solution.py:22
  51.5 7.0 %collective-permute-start.3 = (f32[4,4,8,128]{3,2,1,0:T(8,128)S(1)}, f32[4,4,8,128]{3,2,1,0:T(8,128)S(1)}, u32[]{:S(2)}, u32[]{:S(2)}) collective-permute-start(f32[4,4,8,128]{3,2,1,0:T(8,128)S(1)} %pad_maximum_fusion.1.near_ref), channel_id=1, source_target_pairs={{0,32},{8,40},{16,48},{24,56},{32,0},{40,8},{48,16},{56,24},{1,33}... | collective-permute-start | bytes 196616 | tf_op jit(solution)/shard_map/ppermute | solution.py:22
  58.6 5.4 %collective-permute-start.6 = (f32[4,64,128]{2,1,0:T(8,128)S(1)}, f32[4,64,128]{2,1,0:T(8,128)S(1)}, u32[]{:S(2)}, u32[]{:S(2)}) collective-permute-start(f32[4,64,128]{2,1,0:T(8,128)S(1)} %z_block.1), channel_id=1, source_target_pairs={{0,128},{4,6},{1,129},{5,7},{2,130},{6,4},{3,131},{7,5},{64,192},{... | collective-permute-start | bytes 393224 | tf_op jit(solution)/shard_map/ppermute | solution.py:34
  61.6 4.2 %collective-permute-start.5 = (f32[4,64,128]{2,1,0:T(8,128)S(1)}, f32[4,64,128]{2,1,0:T(8,128)S(1)}, u32[]{:S(2)}, u32[]{:S(2)}) collective-permute-start(f32[4,64,128]{2,1,0:T(8,128)S(1)} %z_block.1), channel_id=1, source_target_pairs={{0,192},{4,7},{1,193},{5,4},{2,194},{6,5},{3,195},{7,6},{64,0},{68... | collective-permute-start | bytes 393224 | tf_op jit(solution)/shard_map/ppermute | solution.py:34
  62.3 5.3 %collective-permute-start.4 = (f32[4,64,128]{2,1,0:T(8,128)S(1)}, f32[4,64,128]{2,1,0:T(8,128)S(1)}, u32[]{:S(2)}, u32[]{:S(2)}) collective-permute-start(f32[4,64,128]{2,1,0:T(8,128)S(1)} %z_block.1), channel_id=1, source_target_pairs={{0,64},{4,5},{1,65},{5,6},{2,66},{6,7},{3,67},{7,4},{64,128},{68,6... | collective-permute-start | bytes 393224 | tf_op jit(solution)/shard_map/ppermute | solution.py:34
  67.7 9.5 %collective-permute-start.8 = (f32[4,4,64,128]{3,2,1,0:T(8,128)S(1)}, f32[4,4,64,128]{3,2,1,0:T(8,128)S(1)}, u32[]{:S(2)}, u32[]{:S(2)}) collective-permute-start(f32[4,4,64,128]{3,2,1,0:T(8,128)S(1)} %pad_maximum_fusion.refs_0_), channel_id=1, source_target_pairs={{0,3},{4,196},{1,0},{5,197},{2,1},{6,198},{3,2},{7,199},{64,67},{6... | collective-permute-start | bytes 1572872 | tf_op jit(solution)/shard_map/ppermute | solution.py:34
  71.1 9.6 %collective-permute-start.7 = (f32[4,4,64,128]{3,2,1,0:T(8,128)S(1)}, f32[4,4,64,128]{3,2,1,0:T(8,128)S(1)}, u32[]{:S(2)}, u32[]{:S(2)}) collective-permute-start(f32[4,4,64,128]{3,2,1,0:T(8,128)S(1)} %pad_maximum_fusion.refs_0_), channel_id=1, source_target_pairs={{0,1},{4,68},{1,2},{5,69},{2,3},{6,70},{3,0},{7,71},{64,65},{68,13... | collective-permute-start | bytes 1572872 | tf_op jit(solution)/shard_map/ppermute | solution.py:34
  71.1 21.8 %collective-permute-start.11 = (f32[4,4,64,128]{3,2,1,0:T(8,128)S(1)}, f32[4,4,64,128]{3,2,1,0:T(8,128)S(1)}, u32[]{:S(2)}, u32[]{:S(2)}) collective-permute-start(f32[4,4,64,128]{3,2,1,0:T(8,128)S(1)} %pad_maximum_fusion.refs_0_), channel_id=1, source_target_pairs={{0,4},{4,0},{1,5},{5,1},{2,6},{6,2},{3,7},{7,3},{8,12},{12,8},{9,1... | collective-permute-start | bytes 1572872 | tf_op jit(solution)/shard_map/ppermute | solution.py:38
  77.2 8.3 %collective-permute-start.10 = (f32[2,4,64,128]{3,2,1,0:T(8,128)S(1)}, f32[2,4,64,128]{3,2,1,0:T(8,128)S(1)}, u32[]{:S(2)}, u32[]{:S(2)}) collective-permute-start(f32[2,4,64,128]{3,2,1,0:T(8,128)S(1)} %slice.9), channel_id=1, source_target_pairs={{0,3},{4,196},{1,0},{5,197},{2,1},{6,198},{3,2},{7,199},{64,67},{6... | collective-permute-start | bytes 786440 | tf_op jit(solution)/shard_map/ppermute | solution.py:34
  80.7 8.3 %collective-permute-start.9 = (f32[2,4,64,128]{3,2,1,0:T(8,128)S(1)}, f32[2,4,64,128]{3,2,1,0:T(8,128)S(1)}, u32[]{:S(2)}, u32[]{:S(2)}) collective-permute-start(f32[2,4,64,128]{3,2,1,0:T(8,128)S(1)} %slice.8), channel_id=1, source_target_pairs={{0,1},{4,68},{1,2},{5,69},{2,3},{6,70},{3,0},{7,71},{64,65},{68,13... | collective-permute-start | bytes 786440 | tf_op jit(solution)/shard_map/ppermute | solution.py:34
  80.8 12.0 %collective-permute-start.13 = (f32[4,4,64,128]{3,2,1,0:T(8,128)S(1)}, f32[4,4,64,128]{3,2,1,0:T(8,128)S(1)}, u32[]{:S(2)}, u32[]{:S(2)}) collective-permute-start(f32[4,4,64,128]{3,2,1,0:T(8,128)S(1)} %collective-permute-done.8.refs_2_), channel_id=1, source_target_pairs={{0,4},{4,0},{1,5},{5,1},{2,6},{6,2},{3,7},{7,3},{8,12},{12,8},{9,1... | collective-permute-start | bytes 1572872 | tf_op jit(solution)/shard_map/ppermute | solution.py:38
  85.4 8.6 %collective-permute-start.12 = (f32[4,4,64,128]{3,2,1,0:T(8,128)S(1)}, f32[4,4,64,128]{3,2,1,0:T(8,128)S(1)}, u32[]{:S(2)}, u32[]{:S(2)}) collective-permute-start(f32[4,4,64,128]{3,2,1,0:T(8,128)S(1)} %collective-permute-done.7.refs_1_), channel_id=1, source_target_pairs={{0,4},{4,0},{1,5},{5,1},{2,6},{6,2},{3,7},{7,3},{8,12},{12,8},{9,1... | collective-permute-start | bytes 1572872 | tf_op jit(solution)/shard_map/ppermute | solution.py:38
  85.5 7.4 %collective-permute-start.15 = (f32[2,4,64,128]{3,2,1,0:T(8,128)S(1)}, f32[2,4,64,128]{3,2,1,0:T(8,128)S(1)}, u32[]{:S(2)}, u32[]{:S(2)}) collective-permute-start(f32[2,4,64,128]{3,2,1,0:T(8,128)S(1)} %collective-permute-done.10.refs_4_), channel_id=1, source_target_pairs={{0,4},{4,0},{1,5},{5,1},{2,6},{6,2},{3,7},{7,3},{8,12},{12,8},{9,1... | collective-permute-start | bytes 786440 | tf_op jit(solution)/shard_map/ppermute | solution.py:38
  89.0 5.0 %collective-permute-start.14 = (f32[2,4,64,128]{3,2,1,0:T(8,128)S(1)}, f32[2,4,64,128]{3,2,1,0:T(8,128)S(1)}, u32[]{:S(2)}, u32[]{:S(2)}) collective-permute-start(f32[2,4,64,128]{3,2,1,0:T(8,128)S(1)} %collective-permute-done.9.refs_3_), channel_id=1, source_target_pairs={{0,4},{4,0},{1,5},{5,1},{2,6},{6,2},{3,7},{7,3},{8,12},{12,8},{9,1... | collective-permute-start | bytes 786440 | tf_op jit(solution)/shard_map/ppermute | solution.py:38

commit v2 on v1

v2 whole, which is shorter than its diff:
```python
import jax
import jax.numpy as jnp
from jax import lax
from jax.experimental import pallas as pl
from jax.experimental.pallas import tpu as pltpu
from jax.sharding import Mesh
from jax.sharding import PartitionSpec as P

X, Z, C, Y = "depth_0", "depth_1", "depth_2", "tile"
DEPTH = (X, Z, C)
PLANE = (X, C, Y)
STEPS = (0, -1, 1, -2)
MIB = 1 << 20


def params(limit):
    return pltpu.CompilerParams(vmem_limit_bytes=limit)


def shifted_plane(value, by, second):
    nx, nc, ny = (lax.axis_size(a) for a in PLANE)
    pairs = []
    for x in range(nx):
        for y in range(ny):
            for c in range(nc):
                along_x = (c == 0) != second
                tx, ty = ((x + by) % nx, y) if along_x else (x, (y + by) % ny)
                pairs.append(((x * nc + c) * ny + y, (tx * nc + c) * ny + ty))
    return lax.ppermute(value, PLANE, pairs)


def other_core(value):
    return lax.ppermute(value, C, [(0, 1), (1, 0)])


def composite_kernel(order_ref, active_ref, layers_ref, out_ref):
    count = layers_ref.shape[0]
    tile = lax.axis_index(Y)

    def step(k, accumulated):
        brick = order_ref[k]
        flag = active_ref[tile, brick].astype(jnp.float32)
        return tuple(
            a + (1.0 - accumulated[3]) * (layers_ref[brick, ch] * flag)
            for ch, a in enumerate(accumulated)
        )

    zero = jnp.zeros(layers_ref.shape[2:], jnp.float32)
    done = lax.fori_loop(0, count, step, (zero,) * 4, unroll=8)
    for copy in range(out_ref.shape[0]):
        for ch in range(4):
            out_ref[copy, ch] = done[ch]


def outgoing_kernel(own_ref, out_ref):
    for x in range(4):
        for z in range(8):
            for c in range(2):
                for ch in range(4):
                    row = c * 64 + z * 8
                    out_ref[(x * 8 + z) * 2 + c, ch] = own_ref[
                        ch, row : row + 8, x * 128 : x * 128 + 128
                    ]


def z_block_kernel(pieces_ref, out_ref):
    for z in range(8):
        out_ref[:, z * 8 : z * 8 + 8, :] = pieces_ref[z]


def place_blocks(parts, out_ref, sem):
    x, c, y = (lax.axis_index(a) for a in PLANE)
    copies = []
    for ref, other, firsts, second in parts:
        core = 1 - c if other else c
        for slot, first in enumerate(firsts):
            bx = lax.rem(x + jnp.where(core == 0, first, second) + 4, 4)
            by = lax.rem(y + jnp.where(core == 0, second, first) + 4, 4)
            row = pl.multiple_of(by * 128 + core * 64, 64)
            col = pl.multiple_of(bx * 128, 128)
            copies.append(
                pltpu.make_async_copy(
                    ref.at[slot],
                    out_ref.at[:, pl.ds(row, 64), pl.ds(col, 128)],
                    sem.at[len(copies)],
                )
            )
    for copy in copies:
        copy.start()
    for copy in copies:
        copy.wait()


def image_call(parts, image, name):
    layout = [p[1:] for p in parts]
    blocks = sum(len(p[2]) for p in parts)
    anywhere = pl.BlockSpec(memory_space=pl.ANY)

    def kernel(*refs):
        out_ref, sem = refs[-2:]
        place_blocks([(ref, *how) for ref, how in zip(refs, layout)], out_ref, sem)

    given = [p[0] for p in parts] + ([] if image is None else [image])
    return pl.pallas_call(
        kernel,
        out_shape=jax.ShapeDtypeStruct((4, 512, 512), jnp.float32),
        in_specs=[anywhere] * len(given),
        out_specs=anywhere,
        scratch_shapes=[pltpu.SemaphoreType.DMA((blocks,))],
        input_output_aliases={} if image is None else {len(parts): 0},
        compiler_params=params(8 * MIB),
        name=name,
    )(*given)


def shards(brick_image, order, active):
    own = brick_image[0]
    smem = pl.BlockSpec(memory_space=pltpu.SMEM)
    vmem = pl.BlockSpec(memory_space=pltpu.VMEM)
    outgoing = pl.pallas_call(
        outgoing_kernel,
        out_shape=jax.ShapeDtypeStruct((64, 4, 8, 128), jnp.float32),
        in_specs=[vmem],
        out_specs=vmem,
        compiler_params=params(4 * MIB),
        name="outgoing",
    )(own)
    layers = lax.all_to_all(outgoing, DEPTH, split_axis=0, concat_axis=0, tiled=True)
    piece = pl.pallas_call(
        composite_kernel,
        out_shape=jax.ShapeDtypeStruct((8, 4, 8, 128), jnp.float32),
        in_specs=[smem, smem, vmem],
        out_specs=vmem,
        compiler_params=params(4 * MIB),
        name="composite",
    )(order, active.T, layers)

    pieces = lax.all_to_all(piece, Z, split_axis=0, concat_axis=0, tiled=True)
    block = pl.pallas_call(
        z_block_kernel,
        out_shape=jax.ShapeDtypeStruct((4, 64, 128), jnp.float32),
        in_specs=[vmem],
        out_specs=vmem,
        compiler_params=params(4 * MIB),
        name="z_block",
    )(pieces)

    head = jnp.stack([block, shifted_plane(block, 1, False)])
    tail = jnp.stack([shifted_plane(block, -1, False), shifted_plane(block, 2, False)])
    head_before = shifted_plane(head, 1, True)
    tail_after = shifted_plane(tail, -1, True)
    tail_before = shifted_plane(tail, 1, True)
    head_after = shifted_plane(head, -1, True)
    head_across = shifted_plane(head_before, 1, True)
    tail_across = shifted_plane(tail_after, -1, True)
    held = (
        (head, STEPS[:2], 0),
        (tail, STEPS[2:], 0),
        (head_before, STEPS[:2], -1),
        (tail_after, STEPS[2:], 1),
        (tail_before, STEPS[2:], -1),
        (head_after, STEPS[:2], 1),
        (head_across, STEPS[:2], -2),
        (tail_across, STEPS[2:], -2),
    )
    mine = [(part, False, *how) for part, *how in held]
    others = [(other_core(part), True, *how) for part, *how in held]
    image = image_call(mine[:6] + others[:2], None, "image_early")
    return image_call(mine[6:] + others[2:], image, "image_late")


def solution(mesh):
    split = Mesh(mesh.devices.reshape(4, 8, 2, mesh.shape["tile"]), (X, Z, C, Y))
    return jax.shard_map(
        shards,
        mesh=split,
        in_specs=(P(DEPTH, None, Y, None), P(), P()),
        out_specs=P(),
        check_vma=False,
    )
```

time: 96.5 us -> 86.5 us (0.90)
  blocking collectives: 0 us -> 52.9 us
  waiting for transfers between devices: 44.7 us -> 2.94 us
  starting transfers between devices: 45.9 us -> 25.3 us
  local copies, waits for them, and re-layouts: 2.41 us -> 1.25 us
    all_to_all x0 -> x2, blocking collectives: none -> 52.9 us  [the longest x1 41.3 us: shards(): lax.all_to_all(outgoing, DEPTH, split_axis=0, concat_axis=0, tiled=True)]
    all_to_all x1 -> x0, waiting for transfers between devices: 28.5 us -> none  [shards(): lax.all_to_all(outgoing, DEPTH, split_axis=0, concat_axis=0, tiled=True)]
    all_to_all x1 -> x0, starting transfers between devices: 13 us -> none  [shards(): lax.all_to_all(outgoing, DEPTH, split_axis=0, concat_axis=0, tiled=True)]
    ppermute x4 -> x0, waiting for transfers between devices: 7.91 us -> none  [shifted_z(): return lax.ppermute(value, Z, [(k, (k + by) % n) for k in range(n)])]
    ppermute x4 -> x0, starting transfers between devices: 5.95 us -> none  [shifted_z(): return lax.ppermute(value, Z, [(k, (k + by) % n) for k in range(n)])]
    ppermute x7 -> x9, waiting for transfers between devices: 7.16 us -> 2.88 us  [shifted_plane(): return lax.ppermute(value, PLANE, pairs)]
    another operation x1 -> x0, local copies, waits for them, and re-layouts: 2.36 us -> none  [shards(): tiles = own.reshape(4, 2, 8, 8, 4, 128)]
    ppermute x7 -> x9, starting transfers between devices: 11.4 us -> 9.18 us  [shifted_plane(): return lax.ppermute(value, PLANE, pairs)]
  transfers between devices with their start and end apart: 17 -> 17, of which waited for: 9 -> 3; matrix products, arithmetic and copies ran while one was open for 0% -> 0% of each run, Pallas kernels for 0% -> 2%
where the time goes in v2:
time: 86.5 us; the launch traced here: 86.3 us
  blocking collectives  52.9 us (61%)
  starting transfers between devices  25.3 us (29%)
  Pallas kernels  3.81 us (4%)
  waiting for transfers between devices  2.94 us (3%)
  local copies, waits for them, and re-layouts  1.25 us (1%)
    all_to_all x1, blocking collectives, shards(): lax.all_to_all(outgoing, DEPTH, split_axis=0, concat_axis=0, tiled=True)  41.3 us
    ppermute x8, starting transfers between devices, other_core(): return lax.ppermute(value, C, [(0, 1), (1, 0)])  16.2 us
    all_to_all x1, blocking collectives, shards(): pieces = lax.all_to_all(piece, Z, split_axis=0, concat_axis=0, tiled=True)  11.6 us
    ppermute x9, starting transfers between devices, shifted_plane(): return lax.ppermute(value, PLANE, pairs)  9.18 us
    ppermute x9, waiting for transfers between devices, shifted_plane(): return lax.ppermute(value, PLANE, pairs)  2.88 us
    pallas_call x2, Pallas kernels, image_call(): pl.pallas_call(kernel, out_shape=jax.ShapeDtypeStruct((4, 512, 512), jnp....  2.87 us
  transfers between devices with their start and end apart: 17, of which 3 were waited for; matrix products, arithmetic and copies ran while one was open for 0% of the time, Pallas kernels for 2%

profile of v2, /device:TPU:1, one launch (start us, length us, event | category | flops | bytes accessed | tf_op | source)
XLA Modules:
  0.0 86.3 jit_solution(5212391583988014062)
XLA Ops:
  0.0 0.0 copy-start.2
  0.0 0.0 copy-start
  0.0 1.2 %copy-done = f32[1,4,128,512]{3,2,1,0:T(8,128)S(1)} copy-done((f32[1,4,128,512]{3,2,1,0:T(8,128)S(1)}, f32[1,4,128,512]{3,2,1,0:T(8,128)}, u32[]{:S(2)}) %copy-start) | copy-done | bytes 1048600
  1.2 0.0 copy-start.1
  1.2 0.1 outgoing.1
  1.3 41.3 %all_to_all.10.layers_ref = f32[64,4,8,128]{3,2,1,0:T(8,128)S(1)} all-to-all(f32[64,4,8,128]{3,2,1,0:T(8,128)S(1)} %outgoing.1), channel_id=1, replica_groups=mesh['depth_0'=4,'depth_1'=8,'depth_2'=2,'tile'=4] {'depth_0','depth_1',..., dimensions={0} | all-to-all | bytes 2097152 | tf_op jit(solution)/shard_map/all_to_all | solution.py:128
  42.6 0.0 copy-done.2
  42.6 0.0 copy-done.1
  42.6 0.9 composite.1
  43.5 11.6 %all_to_all.11.pieces_ref = f32[8,4,8,128]{3,2,1,0:T(8,128)S(1)} all-to-all(f32[8,4,8,128]{3,2,1,0:T(8,128)S(1)} %composite.1), channel_id=1, replica_groups=mesh['depth_0'=4,'depth_1'=8,'depth_2'=2,'tile'=4] {'depth_1'}, dimensions={0} | all-to-all | bytes 262144 | tf_op jit(solution)/shard_map/all_to_all | solution.py:138
  55.1 1.4 %collective-permute-start = (f32[4,64,128]{2,1,0:T(8,128)S(1)}, f32[4,64,128]{2,1,0:T(8,128)S(1)}, u32[]{:S(2)}, u32[]{:S(2)}) collective-permute-start(f32[4,64,128]{2,1,0:T(8,128)S(1)} %z_block.1), channel_id=1, source_target_pairs={{0,64},{4,5},{1,65},{5,6},{2,66},{6,7},{3,67},{7,4},{64,128},{68,6... | collective-permute-start | bytes 393224 | tf_op jit(solution)/shard_map/ppermute | solution.py:29
  56.5 2.6 %collective-permute-start.4 = (f32[4,64,128]{2,1,0:T(8,128)S(1)}, f32[4,64,128]{2,1,0:T(8,128)S(1)}, u32[]{:S(2)}, u32[]{:S(2)}) collective-permute-start(f32[4,64,128]{2,1,0:T(8,128)S(1)} %z_block.1), channel_id=1, source_target_pairs={{0,128},{4,6},{1,129},{5,7},{2,130},{6,4},{3,131},{7,5},{64,192},{... | collective-permute-start | bytes 393224 | tf_op jit(solution)/shard_map/ppermute | solution.py:29
  59.1 1.1 %collective-permute-start.3 = (f32[4,64,128]{2,1,0:T(8,128)S(1)}, f32[4,64,128]{2,1,0:T(8,128)S(1)}, u32[]{:S(2)}, u32[]{:S(2)}) collective-permute-start(f32[4,64,128]{2,1,0:T(8,128)S(1)} %z_block.1), channel_id=1, source_target_pairs={{0,192},{4,7},{1,193},{5,4},{2,194},{6,5},{3,195},{7,6},{64,0},{68... | collective-permute-start | bytes 393224 | tf_op jit(solution)/shard_map/ppermute | solution.py:29
  60.2 0.1 collective-permute-done
  60.3 4.8 %collective-permute-start.15 = (f32[2,4,64,128]{3,2,1,0:T(8,128)S(1)}, f32[2,4,64,128]{3,2,1,0:T(8,128)S(1)}, u32[]{:S(2)}, u32[]{:S(2)}) collective-permute-start(f32[2,4,64,128]{3,2,1,0:T(8,128)S(1)} %pad_maximum_fusion.refs_0_), channel_id=1, source_target_pairs={{0,4},{4,0},{1,5},{5,1},{2,6},{6,2},{3,7},{7,3},{8,12},{12,8},{9,1... | collective-permute-start | bytes 786440 | tf_op jit(solution)/shard_map/ppermute | solution.py:33
  65.1 0.0 collective-permute-start.11
  65.1 1.5 %collective-permute-start.1 = (f32[2,4,64,128]{3,2,1,0:T(8,128)S(1)}, f32[2,4,64,128]{3,2,1,0:T(8,128)S(1)}, u32[]{:S(2)}, u32[]{:S(2)}) collective-permute-start(f32[2,4,64,128]{3,2,1,0:T(8,128)S(1)} %pad_maximum_fusion.refs_0_), channel_id=1, source_target_pairs={{0,1},{4,68},{1,2},{5,69},{2,3},{6,70},{3,0},{7,71},{64,65},{68,13... | collective-permute-start | bytes 786440 | tf_op jit(solution)/shard_map/ppermute | solution.py:29
  66.6 0.0 collective-permute-done.4
  66.6 0.0 collective-permute-done.3
  66.6 1.3 %collective-permute-start.5 = (f32[2,4,64,128]{3,2,1,0:T(8,128)S(1)}, f32[2,4,64,128]{3,2,1,0:T(8,128)S(1)}, u32[]{:S(2)}, u32[]{:S(2)}) collective-permute-start(f32[2,4,64,128]{3,2,1,0:T(8,128)S(1)} %pad_maximum_fusion.1.refs_1_), channel_id=1, source_target_pairs={{0,3},{4,196},{1,0},{5,197},{2,1},{6,198},{3,2},{7,199},{64,67},{6... | collective-permute-start | bytes 786440 | tf_op jit(solution)/shard_map/ppermute | solution.py:29
  67.9 3.7 %collective-permute-start.16 = (f32[2,4,64,128]{3,2,1,0:T(8,128)S(1)}, f32[2,4,64,128]{3,2,1,0:T(8,128)S(1)}, u32[]{:S(2)}, u32[]{:S(2)}) collective-permute-start(f32[2,4,64,128]{3,2,1,0:T(8,128)S(1)} %pad_maximum_fusion.1.refs_1_), channel_id=1, source_target_pairs={{0,4},{4,0},{1,5},{5,1},{2,6},{6,2},{3,7},{7,3},{8,12},{12,8},{9,1... | collective-permute-start | bytes 786440 | tf_op jit(solution)/shard_map/ppermute | solution.py:33
  71.5 0.0 collective-permute-done.15.refs_6_
  71.5 0.0 collective-permute-start.9
  71.5 0.0 collective-permute-done.11.refs_5_
  71.6 0.5 collective-permute-start.12
  72.1 0.0 collective-permute-done.1.refs_2_
  72.1 0.0 collective-permute-start.2
  72.1 1.3 %collective-permute-done.5.refs_3_ = f32[2,4,64,128]{3,2,1,0:T(8,128)S(1)} collective-permute-done((f32[2,4,64,128]{3,2,1,0:T(8,128)S(1)}, f32[2,4,64,128]{3,2,1,0:T(8,128)S(1)}, u32[]{:S(2)}, u32[]{:S(2)}) %collective-permute-start.5) | collective-permute-done | bytes 262176 | tf_op jit(solution)/shard_map/ppermute | solution.py:29
  73.4 1.4 %collective-permute-start.6 = (f32[2,4,64,128]{3,2,1,0:T(8,128)S(1)}, f32[2,4,64,128]{3,2,1,0:T(8,128)S(1)}, u32[]{:S(2)}, u32[]{:S(2)}) collective-permute-start(f32[2,4,64,128]{3,2,1,0:T(8,128)S(1)} %collective-permute-done.5.refs_3_), channel_id=1, source_target_pairs={{0,3},{4,196},{1,0},{5,197},{2,1},{6,198},{3,2},{7,199},{64,67},{6... | collective-permute-start | bytes 786440 | tf_op jit(solution)/shard_map/ppermute | solution.py:29
  74.8 0.0 collective-permute-done.16.refs_7_
  74.8 4.4 %collective-permute-start.7 = (f32[2,4,64,128]{3,2,1,0:T(8,128)S(1)}, f32[2,4,64,128]{3,2,1,0:T(8,128)S(1)}, u32[]{:S(2)}, u32[]{:S(2)}) collective-permute-start(f32[2,4,64,128]{3,2,1,0:T(8,128)S(1)} %collective-permute-done.1.refs_2_), channel_id=1, source_target_pairs={{0,4},{4,0},{1,5},{5,1},{2,6},{6,2},{3,7},{7,3},{8,12},{12,8},{9,1... | collective-permute-start | bytes 786440 | tf_op jit(solution)/shard_map/ppermute | solution.py:33
  79.1 0.0 collective-permute-done.9.refs_4_
  79.1 0.1 collective-permute-start.8
  79.2 0.0 collective-permute-done.12.refs_5_
  79.2 0.4 collective-permute-start.10
  79.6 1.4 %collective-permute-done.2.refs_0_ = f32[2,4,64,128]{3,2,1,0:T(8,128)S(1)} collective-permute-done((f32[2,4,64,128]{3,2,1,0:T(8,128)S(1)}, f32[2,4,64,128]{3,2,1,0:T(8,128)S(1)}, u32[]{:S(2)}, u32[]{:S(2)}) %collective-permute-start.2) | collective-permute-done | bytes 262176 | tf_op jit(solution)/shard_map/ppermute | solution.py:29
  81.1 2.3 %collective-permute-start.13 = (f32[2,4,64,128]{3,2,1,0:T(8,128)S(1)}, f32[2,4,64,128]{3,2,1,0:T(8,128)S(1)}, u32[]{:S(2)}, u32[]{:S(2)}) collective-permute-start(f32[2,4,64,128]{3,2,1,0:T(8,128)S(1)} %collective-permute-done.2.refs_0_), channel_id=1, source_target_pairs={{0,4},{4,0},{1,5},{5,1},{2,6},{6,2},{3,7},{7,3},{8,12},{12,8},{9,1... | collective-permute-start | bytes 786440 | tf_op jit(solution)/shard_map/ppermute | solution.py:33
  83.4 0.0 collective-permute-done.6.refs_1_
  83.4 0.0 collective-permute-start.14
  83.4 1.4 %image_early.1.refs_8_ = f32[4,512,512]{2,1,0:T(8,128)} custom-call(f32[2,4,64,128]{3,2,1,0:T(8,128)S(1)} %pad_maximum_fusion.refs_0_, f32[2,4,64,128]{3,2,1,0:T(8,128)S(1)} %pad_maximum_fusion.1.refs_1_, f32[2,4,64,128]{3,2,1,0:T(8,128)S(1)} %collective-permute-done.1.refs_2_, f32[2,4,64,128]{3,2,1,0:T(8,128)S(1)} %collective-permute-done.5.refs_3_, ...), custom_call_target="tpu_custom_call" | custom-call | tf_op jit(solution)/shard_map/image_early/pallas_call | solution.py:104
  84.8 0.0 collective-permute-done.7.refs_2_
  84.8 0.0 collective-permute-done.10.refs_4_
  84.8 0.0 collective-permute-done.8.refs_3_
  84.8 0.0 collective-permute-done.13.refs_6_
  84.9 0.0 collective-permute-done.14.refs_7_
  84.9 1.4 %image_late.1 = f32[4,512,512]{2,1,0:T(8,128)} custom-call(f32[2,4,64,128]{3,2,1,0:T(8,128)S(1)} %collective-permute-done.2.refs_0_, f32[2,4,64,128]{3,2,1,0:T(8,128)S(1)} %collective-permute-done.6.refs_1_, f32[2,4,64,128]{3,2,1,0:T(8,128)S(1)} %collective-permute-done.7.refs_2_, ...), custom_call_target="tpu_custom_call", output_to_operand_aliasing={{}: (8, {})} | custom-call | tf_op jit(solution)/shard_map/image_late/pallas_call | solution.py:104
  (3 shorter events, 0.0 us)
Async XLA Ops:
  0.0 42.6 %copy-start.2 = (s32[64]{0:T(128)S(1)}, s32[64]{0:T(128)}, u32[]{:S(2)}) copy-start(s32[64]{0:T(128)} %order_ref.1) | copy-start | bytes 772
  0.0 1.2 %copy-start = (f32[1,4,128,512]{3,2,1,0:T(8,128)S(1)}, f32[1,4,128,512]{3,2,1,0:T(8,128)}, u32[]{:S(2)}) copy-start(f32[1,4,128,512]{3,2,1,0:T(8,128)} %param.3) | copy-start | bytes 3145732
  1.2 41.4 %copy-start.1 = (s32[64,4]{0,1:T(4,128)S(1)}, s32[64,4]{0,1:T(4,128)}, u32[]{:S(2)}) copy-start(s32[64,4]{0,1:T(4,128)} %param.5) | copy-start | bytes 3076
  55.1 5.2 %collective-permute-start = (f32[4,64,128]{2,1,0:T(8,128)S(1)}, f32[4,64,128]{2,1,0:T(8,128)S(1)}, u32[]{:S(2)}, u32[]{:S(2)}) collective-permute-start(f32[4,64,128]{2,1,0:T(8,128)S(1)} %z_block.1), channel_id=1, source_target_pairs={{0,64},{4,5},{1,65},{5,6},{2,66},{6,7},{3,67},{7,4},{64,128},{68,6... | collective-permute-start | bytes 393224 | tf_op jit(solution)/shard_map/ppermute | solution.py:29
  56.5 10.1 %collective-permute-start.4 = (f32[4,64,128]{2,1,0:T(8,128)S(1)}, f32[4,64,128]{2,1,0:T(8,128)S(1)}, u32[]{:S(2)}, u32[]{:S(2)}) collective-permute-start(f32[4,64,128]{2,1,0:T(8,128)S(1)} %z_block.1), channel_id=1, source_target_pairs={{0,128},{4,6},{1,129},{5,7},{2,130},{6,4},{3,131},{7,5},{64,192},{... | collective-permute-start | bytes 393224 | tf_op jit(solution)/shard_map/ppermute | solution.py:29
  59.1 7.5 %collective-permute-start.3 = (f32[4,64,128]{2,1,0:T(8,128)S(1)}, f32[4,64,128]{2,1,0:T(8,128)S(1)}, u32[]{:S(2)}, u32[]{:S(2)}) collective-permute-start(f32[4,64,128]{2,1,0:T(8,128)S(1)} %z_block.1), channel_id=1, source_target_pairs={{0,192},{4,7},{1,193},{5,4},{2,194},{6,5},{3,195},{7,6},{64,0},{68... | collective-permute-start | bytes 393224 | tf_op jit(solution)/shard_map/ppermute | solution.py:29
  60.3 11.3 %collective-permute-start.15 = (f32[2,4,64,128]{3,2,1,0:T(8,128)S(1)}, f32[2,4,64,128]{3,2,1,0:T(8,128)S(1)}, u32[]{:S(2)}, u32[]{:S(2)}) collective-permute-start(f32[2,4,64,128]{3,2,1,0:T(8,128)S(1)} %pad_maximum_fusion.refs_0_), channel_id=1, source_target_pairs={{0,4},{4,0},{1,5},{5,1},{2,6},{6,2},{3,7},{7,3},{8,12},{12,8},{9,1... | collective-permute-start | bytes 786440 | tf_op jit(solution)/shard_map/ppermute | solution.py:33
  65.1 6.5 %collective-permute-start.11 = (f32[2,4,64,128]{3,2,1,0:T(8,128)S(1)}, f32[2,4,64,128]{3,2,1,0:T(8,128)S(1)}, u32[]{:S(2)}, u32[]{:S(2)}) collective-permute-start(f32[2,4,64,128]{3,2,1,0:T(8,128)S(1)} %pad_maximum_fusion.refs_0_), channel_id=1, source_target_pairs={{0,3},{4,196},{1,0},{5,197},{2,1},{6,198},{3,2},{7,199},{64,67},{6... | collective-permute-start | bytes 786440 | tf_op jit(solution)/shard_map/ppermute | solution.py:29
  65.1 7.0 %collective-permute-start.1 = (f32[2,4,64,128]{3,2,1,0:T(8,128)S(1)}, f32[2,4,64,128]{3,2,1,0:T(8,128)S(1)}, u32[]{:S(2)}, u32[]{:S(2)}) collective-permute-start(f32[2,4,64,128]{3,2,1,0:T(8,128)S(1)} %pad_maximum_fusion.refs_0_), channel_id=1, source_target_pairs={{0,1},{4,68},{1,2},{5,69},{2,3},{6,70},{3,0},{7,71},{64,65},{68,13... | collective-permute-start | bytes 786440 | tf_op jit(solution)/shard_map/ppermute | solution.py:29
  66.6 6.8 %collective-permute-start.5 = (f32[2,4,64,128]{3,2,1,0:T(8,128)S(1)}, f32[2,4,64,128]{3,2,1,0:T(8,128)S(1)}, u32[]{:S(2)}, u32[]{:S(2)}) collective-permute-start(f32[2,4,64,128]{3,2,1,0:T(8,128)S(1)} %pad_maximum_fusion.1.refs_1_), channel_id=1, source_target_pairs={{0,3},{4,196},{1,0},{5,197},{2,1},{6,198},{3,2},{7,199},{64,67},{6... | collective-permute-start | bytes 786440 | tf_op jit(solution)/shard_map/ppermute | solution.py:29
  67.9 6.9 %collective-permute-start.16 = (f32[2,4,64,128]{3,2,1,0:T(8,128)S(1)}, f32[2,4,64,128]{3,2,1,0:T(8,128)S(1)}, u32[]{:S(2)}, u32[]{:S(2)}) collective-permute-start(f32[2,4,64,128]{3,2,1,0:T(8,128)S(1)} %pad_maximum_fusion.1.refs_1_), channel_id=1, source_target_pairs={{0,4},{4,0},{1,5},{5,1},{2,6},{6,2},{3,7},{7,3},{8,12},{12,8},{9,1... | collective-permute-start | bytes 786440 | tf_op jit(solution)/shard_map/ppermute | solution.py:33
  71.5 7.6 %collective-permute-start.9 = (f32[2,4,64,128]{3,2,1,0:T(8,128)S(1)}, f32[2,4,64,128]{3,2,1,0:T(8,128)S(1)}, u32[]{:S(2)}, u32[]{:S(2)}) collective-permute-start(f32[2,4,64,128]{3,2,1,0:T(8,128)S(1)} %pad_maximum_fusion.1.refs_1_), channel_id=1, source_target_pairs={{0,1},{4,68},{1,2},{5,69},{2,3},{6,70},{3,0},{7,71},{64,65},{68,13... | collective-permute-start | bytes 786440 | tf_op jit(solution)/shard_map/ppermute | solution.py:29
  71.6 7.7 %collective-permute-start.12 = (f32[2,4,64,128]{3,2,1,0:T(8,128)S(1)}, f32[2,4,64,128]{3,2,1,0:T(8,128)S(1)}, u32[]{:S(2)}, u32[]{:S(2)}) collective-permute-start(f32[2,4,64,128]{3,2,1,0:T(8,128)S(1)} %collective-permute-done.11.refs_5_), channel_id=1, source_target_pairs={{0,4},{4,0},{1,5},{5,1},{2,6},{6,2},{3,7},{7,3},{8,12},{12,8},{9,1... | collective-permute-start | bytes 786440 | tf_op jit(solution)/shard_map/ppermute | solution.py:33
  72.1 9.0 %collective-permute-start.2 = (f32[2,4,64,128]{3,2,1,0:T(8,128)S(1)}, f32[2,4,64,128]{3,2,1,0:T(8,128)S(1)}, u32[]{:S(2)}, u32[]{:S(2)}) collective-permute-start(f32[2,4,64,128]{3,2,1,0:T(8,128)S(1)} %collective-permute-done.1.refs_2_), channel_id=1, source_target_pairs={{0,1},{4,68},{1,2},{5,69},{2,3},{6,70},{3,0},{7,71},{64,65},{68,13... | collective-permute-start | bytes 786440 | tf_op jit(solution)/shard_map/ppermute | solution.py:29
  73.4 9.9 %collective-permute-start.6 = (f32[2,4,64,128]{3,2,1,0:T(8,128)S(1)}, f32[2,4,64,128]{3,2,1,0:T(8,128)S(1)}, u32[]{:S(2)}, u32[]{:S(2)}) collective-permute-start(f32[2,4,64,128]{3,2,1,0:T(8,128)S(1)} %collective-permute-done.5.refs_3_), channel_id=1, source_target_pairs={{0,3},{4,196},{1,0},{5,197},{2,1},{6,198},{3,2},{7,199},{64,67},{6... | collective-permute-start | bytes 786440 | tf_op jit(solution)/shard_map/ppermute | solution.py:29
  74.8 10.0 %collective-permute-start.7 = (f32[2,4,64,128]{3,2,1,0:T(8,128)S(1)}, f32[2,4,64,128]{3,2,1,0:T(8,128)S(1)}, u32[]{:S(2)}, u32[]{:S(2)}) collective-permute-start(f32[2,4,64,128]{3,2,1,0:T(8,128)S(1)} %collective-permute-done.1.refs_2_), channel_id=1, source_target_pairs={{0,4},{4,0},{1,5},{5,1},{2,6},{6,2},{3,7},{7,3},{8,12},{12,8},{9,1... | collective-permute-start | bytes 786440 | tf_op jit(solution)/shard_map/ppermute | solution.py:33
  79.1 5.7 %collective-permute-start.8 = (f32[2,4,64,128]{3,2,1,0:T(8,128)S(1)}, f32[2,4,64,128]{3,2,1,0:T(8,128)S(1)}, u32[]{:S(2)}, u32[]{:S(2)}) collective-permute-start(f32[2,4,64,128]{3,2,1,0:T(8,128)S(1)} %collective-permute-done.5.refs_3_), channel_id=1, source_target_pairs={{0,4},{4,0},{1,5},{5,1},{2,6},{6,2},{3,7},{7,3},{8,12},{12,8},{9,1... | collective-permute-start | bytes 786440 | tf_op jit(solution)/shard_map/ppermute | solution.py:33
  79.2 5.6 %collective-permute-start.10 = (f32[2,4,64,128]{3,2,1,0:T(8,128)S(1)}, f32[2,4,64,128]{3,2,1,0:T(8,128)S(1)}, u32[]{:S(2)}, u32[]{:S(2)}) collective-permute-start(f32[2,4,64,128]{3,2,1,0:T(8,128)S(1)} %collective-permute-done.9.refs_4_), channel_id=1, source_target_pairs={{0,4},{4,0},{1,5},{5,1},{2,6},{6,2},{3,7},{7,3},{8,12},{12,8},{9,1... | collective-permute-start | bytes 786440 | tf_op jit(solution)/shard_map/ppermute | solution.py:33
  81.1 3.8 %collective-permute-start.13 = (f32[2,4,64,128]{3,2,1,0:T(8,128)S(1)}, f32[2,4,64,128]{3,2,1,0:T(8,128)S(1)}, u32[]{:S(2)}, u32[]{:S(2)}) collective-permute-start(f32[2,4,64,128]{3,2,1,0:T(8,128)S(1)} %collective-permute-done.2.refs_0_), channel_id=1, source_target_pairs={{0,4},{4,0},{1,5},{5,1},{2,6},{6,2},{3,7},{7,3},{8,12},{12,8},{9,1... | collective-permute-start | bytes 786440 | tf_op jit(solution)/shard_map/ppermute | solution.py:33
  83.4 1.5 %collective-permute-start.14 = (f32[2,4,64,128]{3,2,1,0:T(8,128)S(1)}, f32[2,4,64,128]{3,2,1,0:T(8,128)S(1)}, u32[]{:S(2)}, u32[]{:S(2)}) collective-permute-start(f32[2,4,64,128]{3,2,1,0:T(8,128)S(1)} %collective-permute-done.6.refs_1_), channel_id=1, source_target_pairs={{0,4},{4,0},{1,5},{5,1},{2,6},{6,2},{3,7},{7,3},{8,12},{12,8},{9,1... | collective-permute-start | bytes 786440 | tf_op jit(solution)/shard_map/ppermute | solution.py:33

commit v3 on v2

--- a/solution.py
+++ b/solution.py
@@ -91,7 +91,7 @@
         copy.wait()
 
 
-def image_call(parts, image, name):
+def image_call(parts, image):
     layout = [p[1:] for p in parts]
     blocks = sum(len(p[2]) for p in parts)
     anywhere = pl.BlockSpec(memory_space=pl.ANY)
@@ -109,11 +109,10 @@
         scratch_shapes=[pltpu.SemaphoreType.DMA((blocks,))],
         input_output_aliases={} if image is None else {len(parts): 0},
         compiler_params=params(8 * MIB),
-        name=name,
     )(*given)
 
 
-def shards(brick_image, order, active):
+def body(brick_image, order, active):
     own = brick_image[0]
     smem = pl.BlockSpec(memory_space=pltpu.SMEM)
     vmem = pl.BlockSpec(memory_space=pltpu.VMEM)
@@ -145,34 +144,37 @@
         name="z_block",
     )(pieces)
 
-    head = jnp.stack([block, shifted_plane(block, 1, False)])
-    tail = jnp.stack([shifted_plane(block, -1, False), shifted_plane(block, 2, False)])
+    near = shifted_plane(block, 1, False)
+    far = shifted_plane(block, 2, False)
+    back = shifted_plane(block, -1, False)
+    head = jnp.stack([block, near])
+    tail = jnp.stack([back, far])
     head_before = shifted_plane(head, 1, True)
+    head_after = shifted_plane(head, -1, True)
     tail_after = shifted_plane(tail, -1, True)
     tail_before = shifted_plane(tail, 1, True)
-    head_after = shifted_plane(head, -1, True)
     head_across = shifted_plane(head_before, 1, True)
     tail_across = shifted_plane(tail_after, -1, True)
     held = (
-        (head, STEPS[:2], 0),
-        (tail, STEPS[2:], 0),
-        (head_before, STEPS[:2], -1),
-        (tail_after, STEPS[2:], 1),
-        (tail_before, STEPS[2:], -1),
-        (head_after, STEPS[:2], 1),
-        (head_across, STEPS[:2], -2),
-        (tail_across, STEPS[2:], -2),
+        ("head", head, STEPS[:2], 0),
+        ("tail", tail, STEPS[2:], 0),
+        ("head_before", head_before, STEPS[:2], -1),
+        ("tail_after", tail_after, STEPS[2:], 1),
+        ("head_after", head_after, STEPS[:2], 1),
+        ("tail_before", tail_before, STEPS[2:], -1),
+        ("head_across", head_across, STEPS[:2], -2),
+        ("tail_across", tail_across, STEPS[2:], -2),
     )
-    mine = [(part, False, *how) for part, *how in held]
-    others = [(other_core(part), True, *how) for part, *how in held]
-    image = image_call(mine[:6] + others[:2], None, "image_early")
-    return image_call(mine[6:] + others[2:], image, "image_late")
+    mine = [(part, False, *how) for name, part, *how in held]
+    others = [(other_core(part), True, *how) for name, part, *how in held]
+    image = image_call(mine[:6] + others[:2], None)
+    return image_call(mine[6:] + others[2:], image)
 
 
 def solution(mesh):
     split = Mesh(mesh.devices.reshape(4, 8, 2, mesh.shape["tile"]), (X, Z, C, Y))
     return jax.shard_map(
-        shards,
+        body,
         mesh=split,
         in_specs=(P(DEPTH, None, Y, None), P(), P()),
         out_specs=P(),

time: 86.5 us -> 86.5 us (level)
  no operation moved by 1% of the time
where the time goes in v3:
time: 86.5 us; the launch traced here: 86.3 us
  blocking collectives  52.9 us (61%)
  starting transfers between devices  25.3 us (29%)
  Pallas kernels  3.81 us (4%)
  waiting for transfers between devices  2.94 us (3%)
  local copies, waits for them, and re-layouts  1.25 us (1%)
    all_to_all x1, blocking collectives, body(): lax.all_to_all(outgoing, DEPTH, split_axis=0, concat_axis=0, tiled=True)  41.3 us
    ppermute x8, starting transfers between devices, other_core(): return lax.ppermute(value, C, [(0, 1), (1, 0)])  16.2 us
    all_to_all x1, blocking collectives, body(): pieces = lax.all_to_all(piece, Z, split_axis=0, concat_axis=0, tiled=True)  11.6 us
    ppermute x9, starting transfers between devices, shifted_plane(): return lax.ppermute(value, PLANE, pairs)  9.18 us
    ppermute x9, waiting for transfers between devices, shifted_plane(): return lax.ppermute(value, PLANE, pairs)  2.88 us
    pallas_call x2, Pallas kernels, image_call(): pl.pallas_call(kernel, out_shape=jax.ShapeDtypeStruct((4, 512, 512), jnp....  2.87 us
  transfers between devices with their start and end apart: 17, of which 3 were waited for; matrix products, arithmetic and copies ran while one was open for 0% of the time, Pallas kernels for 2%

profile of v3, /device:TPU:1, one launch (start us, length us, event | category | flops | bytes accessed | tf_op | source)
XLA Modules:
  0.0 86.3 jit_solution(9241813651097170478)
XLA Ops:
  0.0 0.0 copy-start.2
  0.0 0.0 copy-start
  0.0 1.2 %copy-done = f32[1,4,128,512]{3,2,1,0:T(8,128)S(1)} copy-done((f32[1,4,128,512]{3,2,1,0:T(8,128)S(1)}, f32[1,4,128,512]{3,2,1,0:T(8,128)}, u32[]{:S(2)}) %copy-start) | copy-done | bytes 1048600
  1.2 0.0 copy-start.1
  1.2 0.1 outgoing.1
  1.3 41.3 %all_to_all.10.layers_ref = f32[64,4,8,128]{3,2,1,0:T(8,128)S(1)} all-to-all(f32[64,4,8,128]{3,2,1,0:T(8,128)S(1)} %outgoing.1), channel_id=1, replica_groups=mesh['depth_0'=4,'depth_1'=8,'depth_2'=2,'tile'=4] {'depth_0','depth_1',..., dimensions={0} | all-to-all | bytes 2097152 | tf_op jit(solution)/shard_map/all_to_all | solution.py:127
  42.6 0.0 copy-done.2
  42.6 0.0 copy-done.1
  42.6 0.9 composite.1
  43.5 11.6 %all_to_all.11.pieces_ref = f32[8,4,8,128]{3,2,1,0:T(8,128)S(1)} all-to-all(f32[8,4,8,128]{3,2,1,0:T(8,128)S(1)} %composite.1), channel_id=1, replica_groups=mesh['depth_0'=4,'depth_1'=8,'depth_2'=2,'tile'=4] {'depth_1'}, dimensions={0} | all-to-all | bytes 262144 | tf_op jit(solution)/shard_map/all_to_all | solution.py:137
  55.1 1.4 %collective-permute-start = (f32[4,64,128]{2,1,0:T(8,128)S(1)}, f32[4,64,128]{2,1,0:T(8,128)S(1)}, u32[]{:S(2)}, u32[]{:S(2)}) collective-permute-start(f32[4,64,128]{2,1,0:T(8,128)S(1)} %z_block.1), channel_id=1, source_target_pairs={{0,64},{4,5},{1,65},{5,6},{2,66},{6,7},{3,67},{7,4},{64,128},{68,6... | collective-permute-start | bytes 393224 | tf_op jit(solution)/shard_map/ppermute | solution.py:29
  56.5 2.6 %collective-permute-start.4 = (f32[4,64,128]{2,1,0:T(8,128)S(1)}, f32[4,64,128]{2,1,0:T(8,128)S(1)}, u32[]{:S(2)}, u32[]{:S(2)}) collective-permute-start(f32[4,64,128]{2,1,0:T(8,128)S(1)} %z_block.1), channel_id=1, source_target_pairs={{0,128},{4,6},{1,129},{5,7},{2,130},{6,4},{3,131},{7,5},{64,192},{... | collective-permute-start | bytes 393224 | tf_op jit(solution)/shard_map/ppermute | solution.py:29
  59.1 1.1 %collective-permute-start.3 = (f32[4,64,128]{2,1,0:T(8,128)S(1)}, f32[4,64,128]{2,1,0:T(8,128)S(1)}, u32[]{:S(2)}, u32[]{:S(2)}) collective-permute-start(f32[4,64,128]{2,1,0:T(8,128)S(1)} %z_block.1), channel_id=1, source_target_pairs={{0,192},{4,7},{1,193},{5,4},{2,194},{6,5},{3,195},{7,6},{64,0},{68... | collective-permute-start | bytes 393224 | tf_op jit(solution)/shard_map/ppermute | solution.py:29
  60.2 0.1 collective-permute-done
  60.3 4.8 %collective-permute-start.15 = (f32[2,4,64,128]{3,2,1,0:T(8,128)S(1)}, f32[2,4,64,128]{3,2,1,0:T(8,128)S(1)}, u32[]{:S(2)}, u32[]{:S(2)}) collective-permute-start(f32[2,4,64,128]{3,2,1,0:T(8,128)S(1)} %pad_maximum_fusion.refs_0_), channel_id=1, source_target_pairs={{0,4},{4,0},{1,5},{5,1},{2,6},{6,2},{3,7},{7,3},{8,12},{12,8},{9,1... | collective-permute-start | bytes 786440 | tf_op jit(solution)/shard_map/ppermute | solution.py:33
  65.1 0.0 collective-permute-start.9
  65.1 1.5 %collective-permute-start.1 = (f32[2,4,64,128]{3,2,1,0:T(8,128)S(1)}, f32[2,4,64,128]{3,2,1,0:T(8,128)S(1)}, u32[]{:S(2)}, u32[]{:S(2)}) collective-permute-start(f32[2,4,64,128]{3,2,1,0:T(8,128)S(1)} %pad_maximum_fusion.refs_0_), channel_id=1, source_target_pairs={{0,1},{4,68},{1,2},{5,69},{2,3},{6,70},{3,0},{7,71},{64,65},{68,13... | collective-permute-start | bytes 786440 | tf_op jit(solution)/shard_map/ppermute | solution.py:29
  66.6 0.0 collective-permute-done.4
  66.6 0.0 collective-permute-done.3
  66.6 1.3 %collective-permute-start.5 = (f32[2,4,64,128]{3,2,1,0:T(8,128)S(1)}, f32[2,4,64,128]{3,2,1,0:T(8,128)S(1)}, u32[]{:S(2)}, u32[]{:S(2)}) collective-permute-start(f32[2,4,64,128]{3,2,1,0:T(8,128)S(1)} %pad_maximum_fusion.1.refs_1_), channel_id=1, source_target_pairs={{0,3},{4,196},{1,0},{5,197},{2,1},{6,198},{3,2},{7,199},{64,67},{6... | collective-permute-start | bytes 786440 | tf_op jit(solution)/shard_map/ppermute | solution.py:29
  67.9 3.7 %collective-permute-start.16 = (f32[2,4,64,128]{3,2,1,0:T(8,128)S(1)}, f32[2,4,64,128]{3,2,1,0:T(8,128)S(1)}, u32[]{:S(2)}, u32[]{:S(2)}) collective-permute-start(f32[2,4,64,128]{3,2,1,0:T(8,128)S(1)} %pad_maximum_fusion.1.refs_1_), channel_id=1, source_target_pairs={{0,4},{4,0},{1,5},{5,1},{2,6},{6,2},{3,7},{7,3},{8,12},{12,8},{9,1... | collective-permute-start | bytes 786440 | tf_op jit(solution)/shard_map/ppermute | solution.py:33
  71.5 0.0 collective-permute-done.15.refs_6_
  71.5 0.0 collective-permute-start.11
  71.5 0.0 collective-permute-done.9.refs_4_
  71.6 0.5 collective-permute-start.10
  72.1 0.0 collective-permute-done.1.refs_2_
  72.1 0.0 collective-permute-start.2
  72.1 1.3 %collective-permute-done.5.refs_3_ = f32[2,4,64,128]{3,2,1,0:T(8,128)S(1)} collective-permute-done((f32[2,4,64,128]{3,2,1,0:T(8,128)S(1)}, f32[2,4,64,128]{3,2,1,0:T(8,128)S(1)}, u32[]{:S(2)}, u32[]{:S(2)}) %collective-permute-start.5) | collective-permute-done | bytes 262176 | tf_op jit(solution)/shard_map/ppermute | solution.py:29
  73.4 1.4 %collective-permute-start.6 = (f32[2,4,64,128]{3,2,1,0:T(8,128)S(1)}, f32[2,4,64,128]{3,2,1,0:T(8,128)S(1)}, u32[]{:S(2)}, u32[]{:S(2)}) collective-permute-start(f32[2,4,64,128]{3,2,1,0:T(8,128)S(1)} %collective-permute-done.5.refs_3_), channel_id=1, source_target_pairs={{0,3},{4,196},{1,0},{5,197},{2,1},{6,198},{3,2},{7,199},{64,67},{6... | collective-permute-start | bytes 786440 | tf_op jit(solution)/shard_map/ppermute | solution.py:29
  74.8 0.0 collective-permute-done.16.refs_7_
  74.8 4.4 %collective-permute-start.7 = (f32[2,4,64,128]{3,2,1,0:T(8,128)S(1)}, f32[2,4,64,128]{3,2,1,0:T(8,128)S(1)}, u32[]{:S(2)}, u32[]{:S(2)}) collective-permute-start(f32[2,4,64,128]{3,2,1,0:T(8,128)S(1)} %collective-permute-done.1.refs_2_), channel_id=1, source_target_pairs={{0,4},{4,0},{1,5},{5,1},{2,6},{6,2},{3,7},{7,3},{8,12},{12,8},{9,1... | collective-permute-start | bytes 786440 | tf_op jit(solution)/shard_map/ppermute | solution.py:33
  79.1 0.0 collective-permute-done.11.refs_5_
  79.1 0.1 collective-permute-start.8
  79.2 0.0 collective-permute-done.10.refs_4_
  79.2 0.4 collective-permute-start.12
  79.6 1.4 %collective-permute-done.2.refs_0_ = f32[2,4,64,128]{3,2,1,0:T(8,128)S(1)} collective-permute-done((f32[2,4,64,128]{3,2,1,0:T(8,128)S(1)}, f32[2,4,64,128]{3,2,1,0:T(8,128)S(1)}, u32[]{:S(2)}, u32[]{:S(2)}) %collective-permute-start.2) | collective-permute-done | bytes 262176 | tf_op jit(solution)/shard_map/ppermute | solution.py:29
  81.1 2.3 %collective-permute-start.13 = (f32[2,4,64,128]{3,2,1,0:T(8,128)S(1)}, f32[2,4,64,128]{3,2,1,0:T(8,128)S(1)}, u32[]{:S(2)}, u32[]{:S(2)}) collective-permute-start(f32[2,4,64,128]{3,2,1,0:T(8,128)S(1)} %collective-permute-done.2.refs_0_), channel_id=1, source_target_pairs={{0,4},{4,0},{1,5},{5,1},{2,6},{6,2},{3,7},{7,3},{8,12},{12,8},{9,1... | collective-permute-start | bytes 786440 | tf_op jit(solution)/shard_map/ppermute | solution.py:33
  83.4 0.0 collective-permute-done.6.refs_1_
  83.4 0.0 collective-permute-start.14
  83.4 1.4 %shard_map.37.refs_8_ = f32[4,512,512]{2,1,0:T(8,128)} custom-call(f32[2,4,64,128]{3,2,1,0:T(8,128)S(1)} %pad_maximum_fusion.refs_0_, f32[2,4,64,128]{3,2,1,0:T(8,128)S(1)} %pad_maximum_fusion.1.refs_1_, f32[2,4,64,128]{3,2,1,0:T(8,128)S(1)} %collective-permute-done.1.refs_2_, f32[2,4,64,128]{3,2,1,0:T(8,128)S(1)} %collective-permute-done.5.refs_3_, ...), custom_call_target="tpu_custom_call" | custom-call | tf_op jit(solution)/shard_map/pallas_call | solution.py:104
  84.8 0.0 collective-permute-done.7.refs_2_
  84.8 0.0 collective-permute-done.12.refs_5_
  84.8 0.0 collective-permute-done.8.refs_3_
  84.8 0.0 collective-permute-done.13.refs_6_
  84.9 0.0 collective-permute-done.14.refs_7_
  84.9 1.4 %shard_map.38 = f32[4,512,512]{2,1,0:T(8,128)} custom-call(f32[2,4,64,128]{3,2,1,0:T(8,128)S(1)} %collective-permute-done.2.refs_0_, f32[2,4,64,128]{3,2,1,0:T(8,128)S(1)} %collective-permute-done.6.refs_1_, f32[2,4,64,128]{3,2,1,0:T(8,128)S(1)} %collective-permute-done.7.refs_2_, ...), custom_call_target="tpu_custom_call", output_to_operand_aliasing={{}: (8, {})} | custom-call | tf_op jit(solution)/shard_map/pallas_call | solution.py:104
  (3 shorter events, 0.0 us)
Async XLA Ops:
  0.0 42.6 %copy-start.2 = (s32[64]{0:T(128)S(1)}, s32[64]{0:T(128)}, u32[]{:S(2)}) copy-start(s32[64]{0:T(128)} %order_ref.1) | copy-start | bytes 772
  0.0 1.2 %copy-start = (f32[1,4,128,512]{3,2,1,0:T(8,128)S(1)}, f32[1,4,128,512]{3,2,1,0:T(8,128)}, u32[]{:S(2)}) copy-start(f32[1,4,128,512]{3,2,1,0:T(8,128)} %param.3) | copy-start | bytes 3145732
  1.2 41.4 %copy-start.1 = (s32[64,4]{0,1:T(4,128)S(1)}, s32[64,4]{0,1:T(4,128)}, u32[]{:S(2)}) copy-start(s32[64,4]{0,1:T(4,128)} %param.5) | copy-start | bytes 3076
  55.1 5.2 %collective-permute-start = (f32[4,64,128]{2,1,0:T(8,128)S(1)}, f32[4,64,128]{2,1,0:T(8,128)S(1)}, u32[]{:S(2)}, u32[]{:S(2)}) collective-permute-start(f32[4,64,128]{2,1,0:T(8,128)S(1)} %z_block.1), channel_id=1, source_target_pairs={{0,64},{4,5},{1,65},{5,6},{2,66},{6,7},{3,67},{7,4},{64,128},{68,6... | collective-permute-start | bytes 393224 | tf_op jit(solution)/shard_map/ppermute | solution.py:29
  56.5 10.1 %collective-permute-start.4 = (f32[4,64,128]{2,1,0:T(8,128)S(1)}, f32[4,64,128]{2,1,0:T(8,128)S(1)}, u32[]{:S(2)}, u32[]{:S(2)}) collective-permute-start(f32[4,64,128]{2,1,0:T(8,128)S(1)} %z_block.1), channel_id=1, source_target_pairs={{0,128},{4,6},{1,129},{5,7},{2,130},{6,4},{3,131},{7,5},{64,192},{... | collective-permute-start | bytes 393224 | tf_op jit(solution)/shard_map/ppermute | solution.py:29
  59.1 7.5 %collective-permute-start.3 = (f32[4,64,128]{2,1,0:T(8,128)S(1)}, f32[4,64,128]{2,1,0:T(8,128)S(1)}, u32[]{:S(2)}, u32[]{:S(2)}) collective-permute-start(f32[4,64,128]{2,1,0:T(8,128)S(1)} %z_block.1), channel_id=1, source_target_pairs={{0,192},{4,7},{1,193},{5,4},{2,194},{6,5},{3,195},{7,6},{64,0},{68... | collective-permute-start | bytes 393224 | tf_op jit(solution)/shard_map/ppermute | solution.py:29
  60.3 11.3 %collective-permute-start.15 = (f32[2,4,64,128]{3,2,1,0:T(8,128)S(1)}, f32[2,4,64,128]{3,2,1,0:T(8,128)S(1)}, u32[]{:S(2)}, u32[]{:S(2)}) collective-permute-start(f32[2,4,64,128]{3,2,1,0:T(8,128)S(1)} %pad_maximum_fusion.refs_0_), channel_id=1, source_target_pairs={{0,4},{4,0},{1,5},{5,1},{2,6},{6,2},{3,7},{7,3},{8,12},{12,8},{9,1... | collective-permute-start | bytes 786440 | tf_op jit(solution)/shard_map/ppermute | solution.py:33
  65.1 6.5 %collective-permute-start.9 = (f32[2,4,64,128]{3,2,1,0:T(8,128)S(1)}, f32[2,4,64,128]{3,2,1,0:T(8,128)S(1)}, u32[]{:S(2)}, u32[]{:S(2)}) collective-permute-start(f32[2,4,64,128]{3,2,1,0:T(8,128)S(1)} %pad_maximum_fusion.refs_0_), channel_id=1, source_target_pairs={{0,3},{4,196},{1,0},{5,197},{2,1},{6,198},{3,2},{7,199},{64,67},{6... | collective-permute-start | bytes 786440 | tf_op jit(solution)/shard_map/ppermute | solution.py:29
  65.1 7.0 %collective-permute-start.1 = (f32[2,4,64,128]{3,2,1,0:T(8,128)S(1)}, f32[2,4,64,128]{3,2,1,0:T(8,128)S(1)}, u32[]{:S(2)}, u32[]{:S(2)}) collective-permute-start(f32[2,4,64,128]{3,2,1,0:T(8,128)S(1)} %pad_maximum_fusion.refs_0_), channel_id=1, source_target_pairs={{0,1},{4,68},{1,2},{5,69},{2,3},{6,70},{3,0},{7,71},{64,65},{68,13... | collective-permute-start | bytes 786440 | tf_op jit(solution)/shard_map/ppermute | solution.py:29
  66.6 6.8 %collective-permute-start.5 = (f32[2,4,64,128]{3,2,1,0:T(8,128)S(1)}, f32[2,4,64,128]{3,2,1,0:T(8,128)S(1)}, u32[]{:S(2)}, u32[]{:S(2)}) collective-permute-start(f32[2,4,64,128]{3,2,1,0:T(8,128)S(1)} %pad_maximum_fusion.1.refs_1_), channel_id=1, source_target_pairs={{0,3},{4,196},{1,0},{5,197},{2,1},{6,198},{3,2},{7,199},{64,67},{6... | collective-permute-start | bytes 786440 | tf_op jit(solution)/shard_map/ppermute | solution.py:29
  67.9 6.9 %collective-permute-start.16 = (f32[2,4,64,128]{3,2,1,0:T(8,128)S(1)}, f32[2,4,64,128]{3,2,1,0:T(8,128)S(1)}, u32[]{:S(2)}, u32[]{:S(2)}) collective-permute-start(f32[2,4,64,128]{3,2,1,0:T(8,128)S(1)} %pad_maximum_fusion.1.refs_1_), channel_id=1, source_target_pairs={{0,4},{4,0},{1,5},{5,1},{2,6},{6,2},{3,7},{7,3},{8,12},{12,8},{9,1... | collective-permute-start | bytes 786440 | tf_op jit(solution)/shard_map/ppermute | solution.py:33
  71.5 7.6 %collective-permute-start.11 = (f32[2,4,64,128]{3,2,1,0:T(8,128)S(1)}, f32[2,4,64,128]{3,2,1,0:T(8,128)S(1)}, u32[]{:S(2)}, u32[]{:S(2)}) collective-permute-start(f32[2,4,64,128]{3,2,1,0:T(8,128)S(1)} %pad_maximum_fusion.1.refs_1_), channel_id=1, source_target_pairs={{0,1},{4,68},{1,2},{5,69},{2,3},{6,70},{3,0},{7,71},{64,65},{68,13... | collective-permute-start | bytes 786440 | tf_op jit(solution)/shard_map/ppermute | solution.py:29
  71.6 7.7 %collective-permute-start.10 = (f32[2,4,64,128]{3,2,1,0:T(8,128)S(1)}, f32[2,4,64,128]{3,2,1,0:T(8,128)S(1)}, u32[]{:S(2)}, u32[]{:S(2)}) collective-permute-start(f32[2,4,64,128]{3,2,1,0:T(8,128)S(1)} %collective-permute-done.9.refs_4_), channel_id=1, source_target_pairs={{0,4},{4,0},{1,5},{5,1},{2,6},{6,2},{3,7},{7,3},{8,12},{12,8},{9,1... | collective-permute-start | bytes 786440 | tf_op jit(solution)/shard_map/ppermute | solution.py:33
  72.1 9.0 %collective-permute-start.2 = (f32[2,4,64,128]{3,2,1,0:T(8,128)S(1)}, f32[2,4,64,128]{3,2,1,0:T(8,128)S(1)}, u32[]{:S(2)}, u32[]{:S(2)}) collective-permute-start(f32[2,4,64,128]{3,2,1,0:T(8,128)S(1)} %collective-permute-done.1.refs_2_), channel_id=1, source_target_pairs={{0,1},{4,68},{1,2},{5,69},{2,3},{6,70},{3,0},{7,71},{64,65},{68,13... | collective-permute-start | bytes 786440 | tf_op jit(solution)/shard_map/ppermute | solution.py:29
  73.4 9.9 %collective-permute-start.6 = (f32[2,4,64,128]{3,2,1,0:T(8,128)S(1)}, f32[2,4,64,128]{3,2,1,0:T(8,128)S(1)}, u32[]{:S(2)}, u32[]{:S(2)}) collective-permute-start(f32[2,4,64,128]{3,2,1,0:T(8,128)S(1)} %collective-permute-done.5.refs_3_), channel_id=1, source_target_pairs={{0,3},{4,196},{1,0},{5,197},{2,1},{6,198},{3,2},{7,199},{64,67},{6... | collective-permute-start | bytes 786440 | tf_op jit(solution)/shard_map/ppermute | solution.py:29
  74.8 10.0 %collective-permute-start.7 = (f32[2,4,64,128]{3,2,1,0:T(8,128)S(1)}, f32[2,4,64,128]{3,2,1,0:T(8,128)S(1)}, u32[]{:S(2)}, u32[]{:S(2)}) collective-permute-start(f32[2,4,64,128]{3,2,1,0:T(8,128)S(1)} %collective-permute-done.1.refs_2_), channel_id=1, source_target_pairs={{0,4},{4,0},{1,5},{5,1},{2,6},{6,2},{3,7},{7,3},{8,12},{12,8},{9,1... | collective-permute-start | bytes 786440 | tf_op jit(solution)/shard_map/ppermute | solution.py:33
  79.1 5.7 %collective-permute-start.8 = (f32[2,4,64,128]{3,2,1,0:T(8,128)S(1)}, f32[2,4,64,128]{3,2,1,0:T(8,128)S(1)}, u32[]{:S(2)}, u32[]{:S(2)}) collective-permute-start(f32[2,4,64,128]{3,2,1,0:T(8,128)S(1)} %collective-permute-done.5.refs_3_), channel_id=1, source_target_pairs={{0,4},{4,0},{1,5},{5,1},{2,6},{6,2},{3,7},{7,3},{8,12},{12,8},{9,1... | collective-permute-start | bytes 786440 | tf_op jit(solution)/shard_map/ppermute | solution.py:33
  79.2 5.6 %collective-permute-start.12 = (f32[2,4,64,128]{3,2,1,0:T(8,128)S(1)}, f32[2,4,64,128]{3,2,1,0:T(8,128)S(1)}, u32[]{:S(2)}, u32[]{:S(2)}) collective-permute-start(f32[2,4,64,128]{3,2,1,0:T(8,128)S(1)} %collective-permute-done.11.refs_5_), channel_id=1, source_target_pairs={{0,4},{4,0},{1,5},{5,1},{2,6},{6,2},{3,7},{7,3},{8,12},{12,8},{9,1... | collective-permute-start | bytes 786440 | tf_op jit(solution)/shard_map/ppermute | solution.py:33
  81.1 3.8 %collective-permute-start.13 = (f32[2,4,64,128]{3,2,1,0:T(8,128)S(1)}, f32[2,4,64,128]{3,2,1,0:T(8,128)S(1)}, u32[]{:S(2)}, u32[]{:S(2)}) collective-permute-start(f32[2,4,64,128]{3,2,1,0:T(8,128)S(1)} %collective-permute-done.2.refs_0_), channel_id=1, source_target_pairs={{0,4},{4,0},{1,5},{5,1},{2,6},{6,2},{3,7},{7,3},{8,12},{12,8},{9,1... | collective-permute-start | bytes 786440 | tf_op jit(solution)/shard_map/ppermute | solution.py:33
  83.4 1.5 %collective-permute-start.14 = (f32[2,4,64,128]{3,2,1,0:T(8,128)S(1)}, f32[2,4,64,128]{3,2,1,0:T(8,128)S(1)}, u32[]{:S(2)}, u32[]{:S(2)}) collective-permute-start(f32[2,4,64,128]{3,2,1,0:T(8,128)S(1)} %collective-permute-done.6.refs_1_), channel_id=1, source_target_pairs={{0,4},{4,0},{1,5},{5,1},{2,6},{6,2},{3,7},{7,3},{8,12},{12,8},{9,1... | collective-permute-start | bytes 786440 | tf_op jit(solution)/shard_map/ppermute | solution.py:33

commit v4 on v3

--- a/solution.py
+++ b/solution.py
@@ -71,7 +71,7 @@
 def place_blocks(parts, out_ref, sem):
     x, c, y = (lax.axis_index(a) for a in PLANE)
     copies = []
-    for ref, other, firsts, second in parts:
+    for ref, start, other, firsts, second in parts:
         core = 1 - c if other else c
         for slot, first in enumerate(firsts):
             bx = lax.rem(x + jnp.where(core == 0, first, second) + 4, 4)
@@ -80,7 +80,7 @@
             col = pl.multiple_of(bx * 128, 128)
             copies.append(
                 pltpu.make_async_copy(
-                    ref.at[slot],
+                    ref.at[start + slot],
                     out_ref.at[:, pl.ds(row, 64), pl.ds(col, 128)],
                     sem.at[len(copies)],
                 )
@@ -92,22 +92,26 @@
 
 
 def image_call(parts, image):
-    layout = [p[1:] for p in parts]
-    blocks = sum(len(p[2]) for p in parts)
+    arrays = []
+    for array, *_ in parts:
+        if not any(array is known for known in arrays):
+            arrays.append(array)
+    where = [[array is known for known in arrays].index(True) for array, *_ in parts]
+    blocks = sum(len(part[3]) for part in parts)
     anywhere = pl.BlockSpec(memory_space=pl.ANY)
 
     def kernel(*refs):
         out_ref, sem = refs[-2:]
-        place_blocks([(ref, *how) for ref, how in zip(refs, layout)], out_ref, sem)
+        place_blocks([(refs[k], *part[1:]) for k, part in zip(where, parts)], out_ref, sem)
 
-    given = [p[0] for p in parts] + ([] if image is None else [image])
+    given = arrays + ([] if image is None else [image])
     return pl.pallas_call(
         kernel,
         out_shape=jax.ShapeDtypeStruct((4, 512, 512), jnp.float32),
         in_specs=[anywhere] * len(given),
         out_specs=anywhere,
         scratch_shapes=[pltpu.SemaphoreType.DMA((blocks,))],
-        input_output_aliases={} if image is None else {len(parts): 0},
+        input_output_aliases={} if image is None else {len(arrays): 0},
         compiler_params=params(8 * MIB),
     )(*given)
 
@@ -156,19 +160,26 @@
     head_across = shifted_plane(head_before, 1, True)
     tail_across = shifted_plane(tail_after, -1, True)
     held = (
-        ("head", head, STEPS[:2], 0),
-        ("tail", tail, STEPS[2:], 0),
-        ("head_before", head_before, STEPS[:2], -1),
-        ("tail_after", tail_after, STEPS[2:], 1),
-        ("head_after", head_after, STEPS[:2], 1),
-        ("tail_before", tail_before, STEPS[2:], -1),
-        ("head_across", head_across, STEPS[:2], -2),
-        ("tail_across", tail_across, STEPS[2:], -2),
+        (head, STEPS[:2], 0),
+        (tail, STEPS[2:], 0),
+        (head_before, STEPS[:2], -1),
+        (tail_after, STEPS[2:], 1),
+        (head_after, STEPS[:2], 1),
+        (tail_before, STEPS[2:], -1),
     )
-    mine = [(part, False, *how) for name, part, *how in held]
-    others = [(other_core(part), True, *how) for name, part, *how in held]
-    image = image_call(mine[:6] + others[:2], None)
-    return image_call(mine[6:] + others[2:], image)
+    last = ((head_across, STEPS[:2], -2), (tail_across, STEPS[2:], -2))
+    swapped = other_core(jnp.concatenate([part[0] for part in held]))
+    swapped_last = other_core(jnp.concatenate([part[0] for part in last]))
+
+    def blocks(parts):
+        return [(part, 0, False, *how) for part, *how in parts]
+
+    def from_other(joined, parts):
+        return [(joined, 2 * k, True, *how) for k, (part, *how) in enumerate(parts)]
+
+    image = image_call(blocks(held), None)
+    image = image_call(blocks(last) + from_other(swapped, held), image)
+    return image_call(from_other(swapped_last, last), image)
 
 
 def solution(mesh):

time: 86.5 us -> 91.4 us (1.057)
  waiting for transfers between devices: 2.94 us -> 17 us
  starting transfers between devices: 25.3 us -> 15.2 us
    ppermute x9, waiting for transfers between devices: 2.88 us -> 17 us  [shifted_plane(): return lax.ppermute(value, PLANE, pairs)]
    ppermute x8 -> x2, starting transfers between devices: 16.2 us -> 3.92 us  [other_core(): return lax.ppermute(value, C, [(0, 1), (1, 0)])]
    ppermute x9, starting transfers between devices: 9.18 us -> 11.3 us  [shifted_plane(): return lax.ppermute(value, PLANE, pairs)]
    pallas_call x2 -> x3, Pallas kernels: 2.87 us -> 3.54 us  [image_call(): pl.pallas_call(kernel, out_shape=jax.ShapeDtypeStruct((4, 512, 512), jnp....]
  transfers between devices with their start and end apart: 17 -> 11, of which waited for: 3 -> 5; matrix products, arithmetic and copies ran while one was open for 0% -> 0% of each run, Pallas kernels for 2% -> 3%
where the time goes in v4:
time: 91.4 us; the launch traced here: 91.2 us
  blocking collectives  52.9 us (58%)
  waiting for transfers between devices  17 us (19%)
  starting transfers between devices  15.2 us (17%)
  Pallas kernels  4.48 us (5%)
  local copies, waits for them, and re-layouts  1.36 us (1%)
    all_to_all x1, blocking collectives, body(): lax.all_to_all(outgoing, DEPTH, split_axis=0, concat_axis=0, tiled=True)  41.3 us
    ppermute x9, waiting for transfers between devices, shifted_plane(): return lax.ppermute(value, PLANE, pairs)  17 us
    all_to_all x1, blocking collectives, body(): pieces = lax.all_to_all(piece, Z, split_axis=0, concat_axis=0, tiled=True)  11.6 us
    ppermute x9, starting transfers between devices, shifted_plane(): return lax.ppermute(value, PLANE, pairs)  11.3 us
    ppermute x2, starting transfers between devices, other_core(): return lax.ppermute(value, C, [(0, 1), (1, 0)])  3.92 us
    pallas_call x3, Pallas kernels, image_call(): pl.pallas_call(kernel, out_shape=jax.ShapeDtypeStruct((4, 512, 512), jnp....  3.54 us
  transfers between devices with their start and end apart: 11, of which 5 were waited for; matrix products, arithmetic and copies ran while one was open for 0% of the time, Pallas kernels for 3%

profile of v4, /device:TPU:1, one launch (start us, length us, event | category | flops | bytes accessed | tf_op | source)
XLA Modules:
  0.0 91.2 jit_solution(15261079735387778723)
XLA Ops:
  0.0 0.0 copy-start
  0.0 1.2 %copy-done = f32[1,4,128,512]{3,2,1,0:T(8,128)S(1)} copy-done((f32[1,4,128,512]{3,2,1,0:T(8,128)S(1)}, f32[1,4,128,512]{3,2,1,0:T(8,128)}, u32[]{:S(2)}) %copy-start) | copy-done | bytes 1048600
  1.2 0.1 outgoing.1
  1.3 0.0 copy-start.1
  1.3 0.0 copy-start.2
  1.3 41.3 %all_to_all.10.layers_ref = f32[64,4,8,128]{3,2,1,0:T(8,128)S(1)} all-to-all(f32[64,4,8,128]{3,2,1,0:T(8,128)S(1)} %outgoing.1), channel_id=1, replica_groups=mesh['depth_0'=4,'depth_1'=8,'depth_2'=2,'tile'=4] {'depth_0','depth_1',..., dimensions={0} | all-to-all | bytes 2097152 | tf_op jit(solution)/shard_map/all_to_all | solution.py:131
  42.6 0.0 copy-done.1
  42.6 0.0 copy-done.2
  42.6 0.9 composite.1
  43.5 11.6 %all_to_all.11.pieces_ref = f32[8,4,8,128]{3,2,1,0:T(8,128)S(1)} all-to-all(f32[8,4,8,128]{3,2,1,0:T(8,128)S(1)} %composite.1), channel_id=1, replica_groups=mesh['depth_0'=4,'depth_1'=8,'depth_2'=2,'tile'=4] {'depth_1'}, dimensions={0} | all-to-all | bytes 262144 | tf_op jit(solution)/shard_map/all_to_all | solution.py:141
  55.1 2.8 %collective-permute-start.3 = (f32[4,64,128]{2,1,0:T(8,128)S(1)}, f32[4,64,128]{2,1,0:T(8,128)S(1)}, u32[]{:S(2)}, u32[]{:S(2)}) collective-permute-start(f32[4,64,128]{2,1,0:T(8,128)S(1)} %z_block.1), channel_id=1, source_target_pairs={{0,192},{4,7},{1,193},{5,4},{2,194},{6,5},{3,195},{7,6},{64,0},{68... | collective-permute-start | bytes 393224 | tf_op jit(solution)/shard_map/ppermute | solution.py:29
  57.9 0.3 collective-permute-start.4
  58.3 0.7 collective-permute-start
  59.0 2.3 %collective-permute-done.3 = f32[4,64,128]{2,1,0:T(8,128)S(1)} collective-permute-done((f32[4,64,128]{2,1,0:T(8,128)S(1)}, f32[4,64,128]{2,1,0:T(8,128)S(1)}, u32[]{:S(2)}, u32[]{:S(2)}) %collective-permute-start.3) | collective-permute-done | bytes 131104 | tf_op jit(solution)/shard_map/ppermute | solution.py:29
  61.2 2.1 %collective-permute-done.4 = f32[4,64,128]{2,1,0:T(8,128)S(1)} collective-permute-done((f32[4,64,128]{2,1,0:T(8,128)S(1)}, f32[4,64,128]{2,1,0:T(8,128)S(1)}, u32[]{:S(2)}, u32[]{:S(2)}) %collective-permute-start.4) | collective-permute-done | bytes 131104 | tf_op jit(solution)/shard_map/ppermute | solution.py:29
  63.4 3.1 %collective-permute-start.5 = (f32[2,4,64,128]{3,2,1,0:T(8,128)S(1)}, f32[2,4,64,128]{3,2,1,0:T(8,128)S(1)}, u32[]{:S(2)}, u32[]{:S(2)}) collective-permute-start(f32[2,4,64,128]{3,2,1,0:T(8,128)S(1)} %pad_maximum_fusion.2.refs_1_), channel_id=1, source_target_pairs={{0,3},{4,196},{1,0},{5,197},{2,1},{6,198},{3,2},{7,199},{64,67},{6... | collective-permute-start | bytes 786440 | tf_op jit(solution)/shard_map/ppermute | solution.py:29
  66.5 0.0 collective-permute-start.9
  66.5 0.0 collective-permute-done
  66.5 0.1 collective-permute-start.1
  66.6 2.8 %collective-permute-start.8 = (f32[2,4,64,128]{3,2,1,0:T(8,128)S(1)}, f32[2,4,64,128]{3,2,1,0:T(8,128)S(1)}, u32[]{:S(2)}, u32[]{:S(2)}) collective-permute-start(f32[2,4,64,128]{3,2,1,0:T(8,128)S(1)} %pad_maximum_fusion.1.refs_0_), channel_id=1, source_target_pairs={{0,3},{4,196},{1,0},{5,197},{2,1},{6,198},{3,2},{7,199},{64,67},{6... | collective-permute-start | bytes 786440 | tf_op jit(solution)/shard_map/ppermute | solution.py:29
  69.4 6.6 %collective-permute-done.1.refs_2_ = f32[2,4,64,128]{3,2,1,0:T(8,128)S(1)} collective-permute-done((f32[2,4,64,128]{3,2,1,0:T(8,128)S(1)}, f32[2,4,64,128]{3,2,1,0:T(8,128)S(1)}, u32[]{:S(2)}, u32[]{:S(2)}) %collective-permute-start.1) | collective-permute-done | bytes 262176 | tf_op jit(solution)/shard_map/ppermute | solution.py:29
  76.0 0.0 collective-permute-done.5.refs_3_
  76.1 0.0 collective-permute-done.8.refs_4_
  76.1 0.0 collective-permute-done.9.refs_5_
  76.2 3.1 %collective-permute-start.10 = (f32[12,4,64,128]{3,2,1,0:T(8,128)S(1)}, f32[12,4,64,128]{3,2,1,0:T(8,128)S(1)}, u32[]{:S(2)}, u32[]{:S(2)}) collective-permute-start(f32[12,4,64,128]{3,2,1,0:T(8,128)S(1)} %constant_dynamic-update-slice_fusion), channel_id=1, source_target_pairs={{0,4},{4,0},{1,5},{5,1},{2,6},{6,2},{3,7},{7,3},{8,12},{12,8},{9,1... | collective-permute-start | bytes 4718600 | tf_op jit(solution)/shard_map/ppermute | solution.py:33
  79.2 0.7 collective-permute-start.6
  80.0 0.7 collective-permute-start.2
  80.7 4.1 %collective-permute-done.6.refs_1_ = f32[2,4,64,128]{3,2,1,0:T(8,128)S(1)} collective-permute-done((f32[2,4,64,128]{3,2,1,0:T(8,128)S(1)}, f32[2,4,64,128]{3,2,1,0:T(8,128)S(1)}, u32[]{:S(2)}, u32[]{:S(2)}) %collective-permute-start.6) | collective-permute-done | bytes 262176 | tf_op jit(solution)/shard_map/ppermute | solution.py:29
  84.8 1.9 %collective-permute-done.2.refs_0_ = f32[2,4,64,128]{3,2,1,0:T(8,128)S(1)} collective-permute-done((f32[2,4,64,128]{3,2,1,0:T(8,128)S(1)}, f32[2,4,64,128]{3,2,1,0:T(8,128)S(1)}, u32[]{:S(2)}, u32[]{:S(2)}) %collective-permute-start.2) | collective-permute-done | bytes 262176 | tf_op jit(solution)/shard_map/ppermute | solution.py:29
  86.7 0.8 collective-permute-start.7
  87.6 1.2 %shard_map.37.refs_3_ = f32[4,512,512]{2,1,0:T(8,128)} custom-call(f32[2,4,64,128]{3,2,1,0:T(8,128)S(1)} %pad_maximum_fusion.1.refs_0_, f32[2,4,64,128]{3,2,1,0:T(8,128)S(1)} %pad_maximum_fusion.2.refs_1_, f32[2,4,64,128]{3,2,1,0:T(8,128)S(1)} %collective-permute-done.1.refs_2_, f32[2,4,64,128]{3,2,1,0:T(8,128)S(1)} %collective-permute-done.5.refs_3_, ...), custom_call_target="tpu_custom_call" | custom-call | tf_op jit(solution)/shard_map/pallas_call | solution.py:108
  88.8 0.0 collective-permute-done.10.refs_2_
  88.8 1.5 %shard_map.38.refs_1_ = f32[4,512,512]{2,1,0:T(8,128)} custom-call(f32[2,4,64,128]{3,2,1,0:T(8,128)S(1)} %collective-permute-done.2.refs_0_, f32[2,4,64,128]{3,2,1,0:T(8,128)S(1)} %collective-permute-done.6.refs_1_, f32[12,4,64,128]{3,2,1,0:T(8,128)S(1)} %collective-permute-done.10.refs_2_, ...), custom_call_target="tpu_custom_call", output_to_operand_aliasing={{}: (3, {})} | custom-call | tf_op jit(solution)/shard_map/pallas_call | solution.py:108
  90.3 0.0 collective-permute-done.7.refs_0_
  90.3 0.8 shard_map.39
  (12 shorter events, 0.2 us)
Async XLA Ops:
  0.0 1.2 %copy-start = (f32[1,4,128,512]{3,2,1,0:T(8,128)S(1)}, f32[1,4,128,512]{3,2,1,0:T(8,128)}, u32[]{:S(2)}) copy-start(f32[1,4,128,512]{3,2,1,0:T(8,128)} %param.3) | copy-start | bytes 3145732
  1.3 41.3 %copy-start.1 = (s32[64,4]{0,1:T(4,128)S(1)}, s32[64,4]{0,1:T(4,128)}, u32[]{:S(2)}) copy-start(s32[64,4]{0,1:T(4,128)} %param.5) | copy-start | bytes 3076
  1.3 41.3 %copy-start.2 = (s32[64]{0:T(128)S(1)}, s32[64]{0:T(128)}, u32[]{:S(2)}) copy-start(s32[64]{0:T(128)} %order_ref.1) | copy-start | bytes 772
  55.1 6.1 %collective-permute-start.3 = (f32[4,64,128]{2,1,0:T(8,128)S(1)}, f32[4,64,128]{2,1,0:T(8,128)S(1)}, u32[]{:S(2)}, u32[]{:S(2)}) collective-permute-start(f32[4,64,128]{2,1,0:T(8,128)S(1)} %z_block.1), channel_id=1, source_target_pairs={{0,192},{4,7},{1,193},{5,4},{2,194},{6,5},{3,195},{7,6},{64,0},{68... | collective-permute-start | bytes 393224 | tf_op jit(solution)/shard_map/ppermute | solution.py:29
  57.9 5.4 %collective-permute-start.4 = (f32[4,64,128]{2,1,0:T(8,128)S(1)}, f32[4,64,128]{2,1,0:T(8,128)S(1)}, u32[]{:S(2)}, u32[]{:S(2)}) collective-permute-start(f32[4,64,128]{2,1,0:T(8,128)S(1)} %z_block.1), channel_id=1, source_target_pairs={{0,128},{4,6},{1,129},{5,7},{2,130},{6,4},{3,131},{7,5},{64,192},{... | collective-permute-start | bytes 393224 | tf_op jit(solution)/shard_map/ppermute | solution.py:29
  58.3 8.2 %collective-permute-start = (f32[4,64,128]{2,1,0:T(8,128)S(1)}, f32[4,64,128]{2,1,0:T(8,128)S(1)}, u32[]{:S(2)}, u32[]{:S(2)}) collective-permute-start(f32[4,64,128]{2,1,0:T(8,128)S(1)} %z_block.1), channel_id=1, source_target_pairs={{0,64},{4,5},{1,65},{5,6},{2,66},{6,7},{3,67},{7,4},{64,128},{68,6... | collective-permute-start | bytes 393224 | tf_op jit(solution)/shard_map/ppermute | solution.py:29
  63.4 12.7 %collective-permute-start.5 = (f32[2,4,64,128]{3,2,1,0:T(8,128)S(1)}, f32[2,4,64,128]{3,2,1,0:T(8,128)S(1)}, u32[]{:S(2)}, u32[]{:S(2)}) collective-permute-start(f32[2,4,64,128]{3,2,1,0:T(8,128)S(1)} %pad_maximum_fusion.2.refs_1_), channel_id=1, source_target_pairs={{0,3},{4,196},{1,0},{5,197},{2,1},{6,198},{3,2},{7,199},{64,67},{6... | collective-permute-start | bytes 786440 | tf_op jit(solution)/shard_map/ppermute | solution.py:29
  66.5 9.6 %collective-permute-start.9 = (f32[2,4,64,128]{3,2,1,0:T(8,128)S(1)}, f32[2,4,64,128]{3,2,1,0:T(8,128)S(1)}, u32[]{:S(2)}, u32[]{:S(2)}) collective-permute-start(f32[2,4,64,128]{3,2,1,0:T(8,128)S(1)} %pad_maximum_fusion.2.refs_1_), channel_id=1, source_target_pairs={{0,1},{4,68},{1,2},{5,69},{2,3},{6,70},{3,0},{7,71},{64,65},{68,13... | collective-permute-start | bytes 786440 | tf_op jit(solution)/shard_map/ppermute | solution.py:29
  66.5 9.5 %collective-permute-start.1 = (f32[2,4,64,128]{3,2,1,0:T(8,128)S(1)}, f32[2,4,64,128]{3,2,1,0:T(8,128)S(1)}, u32[]{:S(2)}, u32[]{:S(2)}) collective-permute-start(f32[2,4,64,128]{3,2,1,0:T(8,128)S(1)} %pad_maximum_fusion.1.refs_0_), channel_id=1, source_target_pairs={{0,1},{4,68},{1,2},{5,69},{2,3},{6,70},{3,0},{7,71},{64,65},{68,13... | collective-permute-start | bytes 786440 | tf_op jit(solution)/shard_map/ppermute | solution.py:29
  66.6 9.5 %collective-permute-start.8 = (f32[2,4,64,128]{3,2,1,0:T(8,128)S(1)}, f32[2,4,64,128]{3,2,1,0:T(8,128)S(1)}, u32[]{:S(2)}, u32[]{:S(2)}) collective-permute-start(f32[2,4,64,128]{3,2,1,0:T(8,128)S(1)} %pad_maximum_fusion.1.refs_0_), channel_id=1, source_target_pairs={{0,3},{4,196},{1,0},{5,197},{2,1},{6,198},{3,2},{7,199},{64,67},{6... | collective-permute-start | bytes 786440 | tf_op jit(solution)/shard_map/ppermute | solution.py:29
  76.2 12.7 %collective-permute-start.10 = (f32[12,4,64,128]{3,2,1,0:T(8,128)S(1)}, f32[12,4,64,128]{3,2,1,0:T(8,128)S(1)}, u32[]{:S(2)}, u32[]{:S(2)}) collective-permute-start(f32[12,4,64,128]{3,2,1,0:T(8,128)S(1)} %constant_dynamic-update-slice_fusion), channel_id=1, source_target_pairs={{0,4},{4,0},{1,5},{5,1},{2,6},{6,2},{3,7},{7,3},{8,12},{12,8},{9,1... | collective-permute-start | bytes 4718600 | tf_op jit(solution)/shard_map/ppermute | solution.py:33
  79.2 5.5 %collective-permute-start.6 = (f32[2,4,64,128]{3,2,1,0:T(8,128)S(1)}, f32[2,4,64,128]{3,2,1,0:T(8,128)S(1)}, u32[]{:S(2)}, u32[]{:S(2)}) collective-permute-start(f32[2,4,64,128]{3,2,1,0:T(8,128)S(1)} %collective-permute-done.5.refs_3_), channel_id=1, source_target_pairs={{0,3},{4,196},{1,0},{5,197},{2,1},{6,198},{3,2},{7,199},{64,67},{6... | collective-permute-start | bytes 786440 | tf_op jit(solution)/shard_map/ppermute | solution.py:29
  80.0 6.7 %collective-permute-start.2 = (f32[2,4,64,128]{3,2,1,0:T(8,128)S(1)}, f32[2,4,64,128]{3,2,1,0:T(8,128)S(1)}, u32[]{:S(2)}, u32[]{:S(2)}) collective-permute-start(f32[2,4,64,128]{3,2,1,0:T(8,128)S(1)} %collective-permute-done.1.refs_2_), channel_id=1, source_target_pairs={{0,1},{4,68},{1,2},{5,69},{2,3},{6,70},{3,0},{7,71},{64,65},{68,13... | collective-permute-start | bytes 786440 | tf_op jit(solution)/shard_map/ppermute | solution.py:29
  86.7 3.6 %collective-permute-start.7 = (f32[4,4,64,128]{3,2,1,0:T(8,128)S(1)}, f32[4,4,64,128]{3,2,1,0:T(8,128)S(1)}, u32[]{:S(2)}, u32[]{:S(2)}) collective-permute-start(f32[4,4,64,128]{3,2,1,0:T(8,128)S(1)} %pad_maximum_fusion), channel_id=1, source_target_pairs={{0,4},{4,0},{1,5},{5,1},{2,6},{6,2},{3,7},{7,3},{8,12},{12,8},{9,1... | collective-permute-start | bytes 1572872 | tf_op jit(solution)/shard_map/ppermute | solution.py:33

commit v5 on v4

--- a/solution.py
+++ b/solution.py
@@ -9,7 +9,7 @@
 X, Z, C, Y = "depth_0", "depth_1", "depth_2", "tile"
 DEPTH = (X, Z, C)
 PLANE = (X, C, Y)
-STEPS = (0, -1, 1, -2)
+STEPS = (0, 1, -1, -2)
 MIB = 1 << 20
 
 
@@ -151,8 +151,8 @@
     near = shifted_plane(block, 1, False)
     far = shifted_plane(block, 2, False)
     back = shifted_plane(block, -1, False)
-    head = jnp.stack([block, near])
-    tail = jnp.stack([back, far])
+    head = jnp.stack([block, back])
+    tail = jnp.stack([near, far])
     head_before = shifted_plane(head, 1, True)
     head_after = shifted_plane(head, -1, True)
     tail_after = shifted_plane(tail, -1, True)

time: 91.4 us -> 91.6 us (level)
  starting transfers between devices: 15.2 us -> 16.4 us
  waiting for transfers between devices: 17 us -> 16 us
    ppermute x9, starting transfers between devices: 11.3 us -> 13.5 us  [shifted_plane(): return lax.ppermute(value, PLANE, pairs)]
    ppermute x2, starting transfers between devices: 3.92 us -> 2.84 us  [other_core(): return lax.ppermute(value, C, [(0, 1), (1, 0)])]
    ppermute x9, waiting for transfers between devices: 17 us -> 16 us  [shifted_plane(): return lax.ppermute(value, PLANE, pairs)]
where the time goes in v5:
time: 91.6 us; the launch traced here: 91.4 us
  blocking collectives  52.9 us (58%)
  starting transfers between devices  16.4 us (18%)
  waiting for transfers between devices  16 us (17%)
  Pallas kernels  4.5 us (5%)
  local copies, waits for them, and re-layouts  1.36 us (1%)
    all_to_all x1, blocking collectives, body(): lax.all_to_all(outgoing, DEPTH, split_axis=0, concat_axis=0, tiled=True)  41.3 us
    ppermute x9, waiting for transfers between devices, shifted_plane(): return lax.ppermute(value, PLANE, pairs)  16 us
    ppermute x9, starting transfers between devices, shifted_plane(): return lax.ppermute(value, PLANE, pairs)  13.5 us
    all_to_all x1, blocking collectives, body(): pieces = lax.all_to_all(piece, Z, split_axis=0, concat_axis=0, tiled=True)  11.6 us
    pallas_call x3, Pallas kernels, image_call(): pl.pallas_call(kernel, out_shape=jax.ShapeDtypeStruct((4, 512, 512), jnp....  3.56 us
    ppermute x2, starting transfers between devices, other_core(): return lax.ppermute(value, C, [(0, 1), (1, 0)])  2.84 us
  transfers between devices with their start and end apart: 11, of which 5 were waited for; matrix products, arithmetic and copies ran while one was open for 0% of the time, Pallas kernels for 3%

profile of v5, /device:TPU:1, one launch (start us, length us, event | category | flops | bytes accessed | tf_op | source)
XLA Modules:
  0.0 91.4 jit_solution(434907456633494944)
XLA Ops:
  0.0 0.0 copy-start
  0.0 1.2 %copy-done = f32[1,4,128,512]{3,2,1,0:T(8,128)S(1)} copy-done((f32[1,4,128,512]{3,2,1,0:T(8,128)S(1)}, f32[1,4,128,512]{3,2,1,0:T(8,128)}, u32[]{:S(2)}) %copy-start) | copy-done | bytes 1048600
  1.2 0.1 outgoing.1
  1.3 0.0 copy-start.1
  1.3 0.0 copy-start.2
  1.3 41.3 %all_to_all.10.layers_ref = f32[64,4,8,128]{3,2,1,0:T(8,128)S(1)} all-to-all(f32[64,4,8,128]{3,2,1,0:T(8,128)S(1)} %outgoing.1), channel_id=1, replica_groups=mesh['depth_0'=4,'depth_1'=8,'depth_2'=2,'tile'=4] {'depth_0','depth_1',..., dimensions={0} | all-to-all | bytes 2097152 | tf_op jit(solution)/shard_map/all_to_all | solution.py:131
  42.6 0.0 copy-done.1
  42.6 0.0 copy-done.2
  42.6 0.9 composite.1
  43.5 11.6 %all_to_all.11.pieces_ref = f32[8,4,8,128]{3,2,1,0:T(8,128)S(1)} all-to-all(f32[8,4,8,128]{3,2,1,0:T(8,128)S(1)} %composite.1), channel_id=1, replica_groups=mesh['depth_0'=4,'depth_1'=8,'depth_2'=2,'tile'=4] {'depth_1'}, dimensions={0} | all-to-all | bytes 262144 | tf_op jit(solution)/shard_map/all_to_all | solution.py:141
  55.1 1.4 %collective-permute-start.3 = (f32[4,64,128]{2,1,0:T(8,128)S(1)}, f32[4,64,128]{2,1,0:T(8,128)S(1)}, u32[]{:S(2)}, u32[]{:S(2)}) collective-permute-start(f32[4,64,128]{2,1,0:T(8,128)S(1)} %z_block.1), channel_id=1, source_target_pairs={{0,64},{4,5},{1,65},{5,6},{2,66},{6,7},{3,67},{7,4},{64,128},{68,6... | collective-permute-start | bytes 393224 | tf_op jit(solution)/shard_map/ppermute | solution.py:29
  56.5 2.6 %collective-permute-start.4 = (f32[4,64,128]{2,1,0:T(8,128)S(1)}, f32[4,64,128]{2,1,0:T(8,128)S(1)}, u32[]{:S(2)}, u32[]{:S(2)}) collective-permute-start(f32[4,64,128]{2,1,0:T(8,128)S(1)} %z_block.1), channel_id=1, source_target_pairs={{0,128},{4,6},{1,129},{5,7},{2,130},{6,4},{3,131},{7,5},{64,192},{... | collective-permute-start | bytes 393224 | tf_op jit(solution)/shard_map/ppermute | solution.py:29
  59.1 1.1 %collective-permute-start = (f32[4,64,128]{2,1,0:T(8,128)S(1)}, f32[4,64,128]{2,1,0:T(8,128)S(1)}, u32[]{:S(2)}, u32[]{:S(2)}) collective-permute-start(f32[4,64,128]{2,1,0:T(8,128)S(1)} %z_block.1), channel_id=1, source_target_pairs={{0,192},{4,7},{1,193},{5,4},{2,194},{6,5},{3,195},{7,6},{64,0},{68... | collective-permute-start | bytes 393224 | tf_op jit(solution)/shard_map/ppermute | solution.py:29
  60.2 0.1 collective-permute-done.3
  60.3 2.9 %collective-permute-done.4 = f32[4,64,128]{2,1,0:T(8,128)S(1)} collective-permute-done((f32[4,64,128]{2,1,0:T(8,128)S(1)}, f32[4,64,128]{2,1,0:T(8,128)S(1)}, u32[]{:S(2)}, u32[]{:S(2)}) %collective-permute-start.4) | collective-permute-done | bytes 131104 | tf_op jit(solution)/shard_map/ppermute | solution.py:29
  63.2 3.1 %collective-permute-start.5 = (f32[2,4,64,128]{3,2,1,0:T(8,128)S(1)}, f32[2,4,64,128]{3,2,1,0:T(8,128)S(1)}, u32[]{:S(2)}, u32[]{:S(2)}) collective-permute-start(f32[2,4,64,128]{3,2,1,0:T(8,128)S(1)} %pad_maximum_fusion.2.refs_1_), channel_id=1, source_target_pairs={{0,3},{4,196},{1,0},{5,197},{2,1},{6,198},{3,2},{7,199},{64,67},{6... | collective-permute-start | bytes 786440 | tf_op jit(solution)/shard_map/ppermute | solution.py:29
  66.3 0.0 collective-permute-start.9
  66.3 0.0 collective-permute-done
  66.3 0.1 collective-permute-start.1
  66.4 2.8 %collective-permute-start.8 = (f32[2,4,64,128]{3,2,1,0:T(8,128)S(1)}, f32[2,4,64,128]{3,2,1,0:T(8,128)S(1)}, u32[]{:S(2)}, u32[]{:S(2)}) collective-permute-start(f32[2,4,64,128]{3,2,1,0:T(8,128)S(1)} %pad_maximum_fusion.1.refs_0_), channel_id=1, source_target_pairs={{0,3},{4,196},{1,0},{5,197},{2,1},{6,198},{3,2},{7,199},{64,67},{6... | collective-permute-start | bytes 786440 | tf_op jit(solution)/shard_map/ppermute | solution.py:29
  69.2 6.6 %collective-permute-done.1.refs_2_ = f32[2,4,64,128]{3,2,1,0:T(8,128)S(1)} collective-permute-done((f32[2,4,64,128]{3,2,1,0:T(8,128)S(1)}, f32[2,4,64,128]{3,2,1,0:T(8,128)S(1)}, u32[]{:S(2)}, u32[]{:S(2)}) %collective-permute-start.1) | collective-permute-done | bytes 262176 | tf_op jit(solution)/shard_map/ppermute | solution.py:29
  75.9 0.0 collective-permute-done.5.refs_3_
  75.9 0.0 collective-permute-done.8.refs_4_
  75.9 0.0 collective-permute-done.9.refs_5_
  76.0 2.8 %collective-permute-start.10 = (f32[12,4,64,128]{3,2,1,0:T(8,128)S(1)}, f32[12,4,64,128]{3,2,1,0:T(8,128)S(1)}, u32[]{:S(2)}, u32[]{:S(2)}) collective-permute-start(f32[12,4,64,128]{3,2,1,0:T(8,128)S(1)} %constant_dynamic-update-slice_fusion), channel_id=1, source_target_pairs={{0,4},{4,0},{1,5},{5,1},{2,6},{6,2},{3,7},{7,3},{8,12},{12,8},{9,1... | collective-permute-start | bytes 4718600 | tf_op jit(solution)/shard_map/ppermute | solution.py:33
  78.7 2.5 %collective-permute-start.6 = (f32[2,4,64,128]{3,2,1,0:T(8,128)S(1)}, f32[2,4,64,128]{3,2,1,0:T(8,128)S(1)}, u32[]{:S(2)}, u32[]{:S(2)}) collective-permute-start(f32[2,4,64,128]{3,2,1,0:T(8,128)S(1)} %collective-permute-done.5.refs_3_), channel_id=1, source_target_pairs={{0,3},{4,196},{1,0},{5,197},{2,1},{6,198},{3,2},{7,199},{64,67},{6... | collective-permute-start | bytes 786440 | tf_op jit(solution)/shard_map/ppermute | solution.py:29
  81.2 0.0 collective-permute-start.2
  81.2 3.3 %collective-permute-done.6.refs_1_ = f32[2,4,64,128]{3,2,1,0:T(8,128)S(1)} collective-permute-done((f32[2,4,64,128]{3,2,1,0:T(8,128)S(1)}, f32[2,4,64,128]{3,2,1,0:T(8,128)S(1)}, u32[]{:S(2)}, u32[]{:S(2)}) %collective-permute-start.6) | collective-permute-done | bytes 262176 | tf_op jit(solution)/shard_map/ppermute | solution.py:29
  84.5 3.1 %collective-permute-done.2.refs_0_ = f32[2,4,64,128]{3,2,1,0:T(8,128)S(1)} collective-permute-done((f32[2,4,64,128]{3,2,1,0:T(8,128)S(1)}, f32[2,4,64,128]{3,2,1,0:T(8,128)S(1)}, u32[]{:S(2)}, u32[]{:S(2)}) %collective-permute-start.2) | collective-permute-done | bytes 262176 | tf_op jit(solution)/shard_map/ppermute | solution.py:29
  87.7 0.1 collective-permute-start.7
  87.8 1.3 %shard_map.37.refs_3_ = f32[4,512,512]{2,1,0:T(8,128)} custom-call(f32[2,4,64,128]{3,2,1,0:T(8,128)S(1)} %pad_maximum_fusion.1.refs_0_, f32[2,4,64,128]{3,2,1,0:T(8,128)S(1)} %pad_maximum_fusion.2.refs_1_, f32[2,4,64,128]{3,2,1,0:T(8,128)S(1)} %collective-permute-done.1.refs_2_, f32[2,4,64,128]{3,2,1,0:T(8,128)S(1)} %collective-permute-done.5.refs_3_, ...), custom_call_target="tpu_custom_call" | custom-call | tf_op jit(solution)/shard_map/pallas_call | solution.py:108
  89.0 0.0 collective-permute-done.10.refs_2_
  89.1 1.5 %shard_map.38.refs_1_ = f32[4,512,512]{2,1,0:T(8,128)} custom-call(f32[2,4,64,128]{3,2,1,0:T(8,128)S(1)} %collective-permute-done.2.refs_0_, f32[2,4,64,128]{3,2,1,0:T(8,128)S(1)} %collective-permute-done.6.refs_1_, f32[12,4,64,128]{3,2,1,0:T(8,128)S(1)} %collective-permute-done.10.refs_2_, ...), custom_call_target="tpu_custom_call", output_to_operand_aliasing={{}: (3, {})} | custom-call | tf_op jit(solution)/shard_map/pallas_call | solution.py:108
  90.5 0.0 collective-permute-done.7.refs_0_
  90.5 0.8 shard_map.39
  (12 shorter events, 0.2 us)
Async XLA Ops:
  0.0 1.2 %copy-start = (f32[1,4,128,512]{3,2,1,0:T(8,128)S(1)}, f32[1,4,128,512]{3,2,1,0:T(8,128)}, u32[]{:S(2)}) copy-start(f32[1,4,128,512]{3,2,1,0:T(8,128)} %param.3) | copy-start | bytes 3145732
  1.3 41.3 %copy-start.1 = (s32[64,4]{0,1:T(4,128)S(1)}, s32[64,4]{0,1:T(4,128)}, u32[]{:S(2)}) copy-start(s32[64,4]{0,1:T(4,128)} %param.5) | copy-start | bytes 3076
  1.3 41.3 %copy-start.2 = (s32[64]{0:T(128)S(1)}, s32[64]{0:T(128)}, u32[]{:S(2)}) copy-start(s32[64]{0:T(128)} %order_ref.1) | copy-start | bytes 772
  55.1 5.2 %collective-permute-start.3 = (f32[4,64,128]{2,1,0:T(8,128)S(1)}, f32[4,64,128]{2,1,0:T(8,128)S(1)}, u32[]{:S(2)}, u32[]{:S(2)}) collective-permute-start(f32[4,64,128]{2,1,0:T(8,128)S(1)} %z_block.1), channel_id=1, source_target_pairs={{0,64},{4,5},{1,65},{5,6},{2,66},{6,7},{3,67},{7,4},{64,128},{68,6... | collective-permute-start | bytes 393224 | tf_op jit(solution)/shard_map/ppermute | solution.py:29
  56.5 6.7 %collective-permute-start.4 = (f32[4,64,128]{2,1,0:T(8,128)S(1)}, f32[4,64,128]{2,1,0:T(8,128)S(1)}, u32[]{:S(2)}, u32[]{:S(2)}) collective-permute-start(f32[4,64,128]{2,1,0:T(8,128)S(1)} %z_block.1), channel_id=1, source_target_pairs={{0,128},{4,6},{1,129},{5,7},{2,130},{6,4},{3,131},{7,5},{64,192},{... | collective-permute-start | bytes 393224 | tf_op jit(solution)/shard_map/ppermute | solution.py:29
  59.1 7.2 %collective-permute-start = (f32[4,64,128]{2,1,0:T(8,128)S(1)}, f32[4,64,128]{2,1,0:T(8,128)S(1)}, u32[]{:S(2)}, u32[]{:S(2)}) collective-permute-start(f32[4,64,128]{2,1,0:T(8,128)S(1)} %z_block.1), channel_id=1, source_target_pairs={{0,192},{4,7},{1,193},{5,4},{2,194},{6,5},{3,195},{7,6},{64,0},{68... | collective-permute-start | bytes 393224 | tf_op jit(solution)/shard_map/ppermute | solution.py:29
  63.2 12.7 %collective-permute-start.5 = (f32[2,4,64,128]{3,2,1,0:T(8,128)S(1)}, f32[2,4,64,128]{3,2,1,0:T(8,128)S(1)}, u32[]{:S(2)}, u32[]{:S(2)}) collective-permute-start(f32[2,4,64,128]{3,2,1,0:T(8,128)S(1)} %pad_maximum_fusion.2.refs_1_), channel_id=1, source_target_pairs={{0,3},{4,196},{1,0},{5,197},{2,1},{6,198},{3,2},{7,199},{64,67},{6... | collective-permute-start | bytes 786440 | tf_op jit(solution)/shard_map/ppermute | solution.py:29
  66.3 9.6 %collective-permute-start.9 = (f32[2,4,64,128]{3,2,1,0:T(8,128)S(1)}, f32[2,4,64,128]{3,2,1,0:T(8,128)S(1)}, u32[]{:S(2)}, u32[]{:S(2)}) collective-permute-start(f32[2,4,64,128]{3,2,1,0:T(8,128)S(1)} %pad_maximum_fusion.2.refs_1_), channel_id=1, source_target_pairs={{0,1},{4,68},{1,2},{5,69},{2,3},{6,70},{3,0},{7,71},{64,65},{68,13... | collective-permute-start | bytes 786440 | tf_op jit(solution)/shard_map/ppermute | solution.py:29
  66.3 9.5 %collective-permute-start.1 = (f32[2,4,64,128]{3,2,1,0:T(8,128)S(1)}, f32[2,4,64,128]{3,2,1,0:T(8,128)S(1)}, u32[]{:S(2)}, u32[]{:S(2)}) collective-permute-start(f32[2,4,64,128]{3,2,1,0:T(8,128)S(1)} %pad_maximum_fusion.1.refs_0_), channel_id=1, source_target_pairs={{0,1},{4,68},{1,2},{5,69},{2,3},{6,70},{3,0},{7,71},{64,65},{68,13... | collective-permute-start | bytes 786440 | tf_op jit(solution)/shard_map/ppermute | solution.py:29
  66.4 9.5 %collective-permute-start.8 = (f32[2,4,64,128]{3,2,1,0:T(8,128)S(1)}, f32[2,4,64,128]{3,2,1,0:T(8,128)S(1)}, u32[]{:S(2)}, u32[]{:S(2)}) collective-permute-start(f32[2,4,64,128]{3,2,1,0:T(8,128)S(1)} %pad_maximum_fusion.1.refs_0_), channel_id=1, source_target_pairs={{0,3},{4,196},{1,0},{5,197},{2,1},{6,198},{3,2},{7,199},{64,67},{6... | collective-permute-start | bytes 786440 | tf_op jit(solution)/shard_map/ppermute | solution.py:29
  76.0 13.1 %collective-permute-start.10 = (f32[12,4,64,128]{3,2,1,0:T(8,128)S(1)}, f32[12,4,64,128]{3,2,1,0:T(8,128)S(1)}, u32[]{:S(2)}, u32[]{:S(2)}) collective-permute-start(f32[12,4,64,128]{3,2,1,0:T(8,128)S(1)} %constant_dynamic-update-slice_fusion), channel_id=1, source_target_pairs={{0,4},{4,0},{1,5},{5,1},{2,6},{6,2},{3,7},{7,3},{8,12},{12,8},{9,1... | collective-permute-start | bytes 4718600 | tf_op jit(solution)/shard_map/ppermute | solution.py:33
  78.7 5.8 %collective-permute-start.6 = (f32[2,4,64,128]{3,2,1,0:T(8,128)S(1)}, f32[2,4,64,128]{3,2,1,0:T(8,128)S(1)}, u32[]{:S(2)}, u32[]{:S(2)}) collective-permute-start(f32[2,4,64,128]{3,2,1,0:T(8,128)S(1)} %collective-permute-done.5.refs_3_), channel_id=1, source_target_pairs={{0,3},{4,196},{1,0},{5,197},{2,1},{6,198},{3,2},{7,199},{64,67},{6... | collective-permute-start | bytes 786440 | tf_op jit(solution)/shard_map/ppermute | solution.py:29
  81.2 6.4 %collective-permute-start.2 = (f32[2,4,64,128]{3,2,1,0:T(8,128)S(1)}, f32[2,4,64,128]{3,2,1,0:T(8,128)S(1)}, u32[]{:S(2)}, u32[]{:S(2)}) collective-permute-start(f32[2,4,64,128]{3,2,1,0:T(8,128)S(1)} %collective-permute-done.1.refs_2_), channel_id=1, source_target_pairs={{0,1},{4,68},{1,2},{5,69},{2,3},{6,70},{3,0},{7,71},{64,65},{68,13... | collective-permute-start | bytes 786440 | tf_op jit(solution)/shard_map/ppermute | solution.py:29
  87.7 2.8 %collective-permute-start.7 = (f32[4,4,64,128]{3,2,1,0:T(8,128)S(1)}, f32[4,4,64,128]{3,2,1,0:T(8,128)S(1)}, u32[]{:S(2)}, u32[]{:S(2)}) collective-permute-start(f32[4,4,64,128]{3,2,1,0:T(8,128)S(1)} %pad_maximum_fusion), channel_id=1, source_target_pairs={{0,4},{4,0},{1,5},{5,1},{2,6},{6,2},{3,7},{7,3},{8,12},{12,8},{9,1... | collective-permute-start | bytes 1572872 | tf_op jit(solution)/shard_map/ppermute | solution.py:33

commit v6 on v5

--- a/solution.py
+++ b/solution.py
@@ -17,7 +17,7 @@
     return pltpu.CompilerParams(vmem_limit_bytes=limit)
 
 
-def shifted_plane(value, by, second):
+def shifted_plane(value, by, second, crossed=False):
     nx, nc, ny = (lax.axis_size(a) for a in PLANE)
     pairs = []
     for x in range(nx):
@@ -25,7 +25,7 @@
             for c in range(nc):
                 along_x = (c == 0) != second
                 tx, ty = ((x + by) % nx, y) if along_x else (x, (y + by) % ny)
-                pairs.append(((x * nc + c) * ny + y, (tx * nc + c) * ny + ty))
+                pairs.append(((x * nc + c) * ny + y, (tx * nc + (1 - c if crossed else c)) * ny + ty))
     return lax.ppermute(value, PLANE, pairs)
 
 
@@ -37,16 +37,26 @@
     count = layers_ref.shape[0]
     tile = lax.axis_index(Y)
 
+    parts = 4
+    run = count // parts
+
     def step(k, accumulated):
-        brick = order_ref[k]
-        flag = active_ref[tile, brick].astype(jnp.float32)
-        return tuple(
-            a + (1.0 - accumulated[3]) * (layers_ref[brick, ch] * flag)
-            for ch, a in enumerate(accumulated)
-        )
+        new = []
+        for part, near in enumerate(accumulated):
+            brick = order_ref[part * run + k]
+            flag = active_ref[tile, brick].astype(jnp.float32)
+            through = 1.0 - near[3]
+            new.append(
+                tuple(a + through * (layers_ref[brick, ch] * flag) for ch, a in enumerate(near))
+            )
+        return tuple(new)
 
     zero = jnp.zeros(layers_ref.shape[2:], jnp.float32)
-    done = lax.fori_loop(0, count, step, (zero,) * 4, unroll=8)
+    runs = lax.fori_loop(0, run, step, ((zero,) * 4,) * parts, unroll=4)
+    done = runs[0]
+    for far in runs[1:]:
+        through = 1.0 - done[3]
+        done = tuple(a + through * b for a, b in zip(done, far))
     for copy in range(out_ref.shape[0]):
         for ch in range(4):
             out_ref[copy, ch] = done[ch]
@@ -148,6 +158,9 @@
         name="z_block",
     )(pieces)
 
+    def go_crossed(value, by):
+        return shifted_plane(value, by, True, True)
+
     near = shifted_plane(block, 1, False)
     far = shifted_plane(block, 2, False)
     back = shifted_plane(block, -1, False)
@@ -169,7 +182,8 @@
     )
     last = ((head_across, STEPS[:2], -2), (tail_across, STEPS[2:], -2))
     swapped = other_core(jnp.concatenate([part[0] for part in held]))
-    swapped_last = other_core(jnp.concatenate([part[0] for part in last]))
+    head_crossed = go_crossed(head_after, -1)
+    tail_crossed = go_crossed(tail_before, 1)
 
     def blocks(parts):
         return [(part, 0, False, *how) for part, *how in parts]
@@ -179,7 +193,7 @@
 
     image = image_call(blocks(held), None)
     image = image_call(blocks(last) + from_other(swapped, held), image)
-    return image_call(from_other(swapped_last, last), image)
+    return image_call(from_other(head_crossed, last[:1]) + from_other(tail_crossed, last[1:]), image)
 
 
 def solution(mesh):

time: 91.6 us -> 90.3 us (0.986)
  waiting for transfers between devices: 16 us -> 14.6 us
    ppermute x9 -> x11, waiting for transfers between devices: 16 us -> 14.6 us  [shifted_plane(): return lax.ppermute(value, PLANE, pairs)]
    ppermute x9 -> x11, starting transfers between devices: 13.5 us -> 13.9 us  [shifted_plane(): return lax.ppermute(value, PLANE, pairs)]
    ppermute x2 -> x1, starting transfers between devices: 2.84 us -> 2.78 us  [other_core(): return lax.ppermute(value, C, [(0, 1), (1, 0)])]
  transfers between devices with their start and end apart: 11 -> 12, of which waited for: 5 -> 5; matrix products, arithmetic and copies ran while one was open for 0% -> 0% of each run, Pallas kernels for 3% -> 3%
where the time goes in v6:
time: 90.3 us; the launch traced here: 90.1 us
  blocking collectives  52.9 us (59%)
  starting transfers between devices  16.7 us (18%)
  waiting for transfers between devices  14.6 us (16%)
  Pallas kernels  4.37 us (5%)
  local copies, waits for them, and re-layouts  1.36 us (2%)
    all_to_all x1, blocking collectives, body(): lax.all_to_all(outgoing, DEPTH, split_axis=0, concat_axis=0, tiled=True)  41.3 us
    ppermute x11, waiting for transfers between devices, shifted_plane(): return lax.ppermute(value, PLANE, pairs)  14.6 us
    ppermute x11, starting transfers between devices, shifted_plane(): return lax.ppermute(value, PLANE, pairs)  13.9 us
    all_to_all x1, blocking collectives, body(): pieces = lax.all_to_all(piece, Z, split_axis=0, concat_axis=0, tiled=True)  11.6 us
    pallas_call x3, Pallas kernels, image_call(): pl.pallas_call(kernel, out_shape=jax.ShapeDtypeStruct((4, 512, 512), jnp....  3.49 us
    ppermute x1, starting transfers between devices, other_core(): return lax.ppermute(value, C, [(0, 1), (1, 0)])  2.78 us
  transfers between devices with their start and end apart: 12, of which 5 were waited for; matrix products, arithmetic and copies ran while one was open for 0% of the time, Pallas kernels for 3%

profile of v6, /device:TPU:1, one launch (start us, length us, event | category | flops | bytes accessed | tf_op | source)
XLA Modules:
  0.0 90.1 jit_solution(11817387841274939116)
XLA Ops:
  0.0 0.0 copy-start
  0.0 1.2 %copy-done = f32[1,4,128,512]{3,2,1,0:T(8,128)S(1)} copy-done((f32[1,4,128,512]{3,2,1,0:T(8,128)S(1)}, f32[1,4,128,512]{3,2,1,0:T(8,128)}, u32[]{:S(2)}) %copy-start) | copy-done | bytes 1048600
  1.2 0.1 outgoing.1
  1.3 0.0 copy-start.1
  1.3 0.0 copy-start.2
  1.3 41.3 %all_to_all.10.layers_ref = f32[64,4,8,128]{3,2,1,0:T(8,128)S(1)} all-to-all(f32[64,4,8,128]{3,2,1,0:T(8,128)S(1)} %outgoing.1), channel_id=1, replica_groups=mesh['depth_0'=4,'depth_1'=8,'depth_2'=2,'tile'=4] {'depth_0','depth_1',..., dimensions={0} | all-to-all | bytes 2097152 | tf_op jit(solution)/shard_map/all_to_all | solution.py:141
  42.6 0.0 copy-done.1
  42.6 0.0 copy-done.2
  42.6 0.8 composite.1
  43.4 11.6 %all_to_all.11.pieces_ref = f32[8,4,8,128]{3,2,1,0:T(8,128)S(1)} all-to-all(f32[8,4,8,128]{3,2,1,0:T(8,128)S(1)} %composite.1), channel_id=1, replica_groups=mesh['depth_0'=4,'depth_1'=8,'depth_2'=2,'tile'=4] {'depth_1'}, dimensions={0} | all-to-all | bytes 262144 | tf_op jit(solution)/shard_map/all_to_all | solution.py:151
  55.0 3.0 %collective-permute-start.4 = (f32[4,64,128]{2,1,0:T(8,128)S(1)}, f32[4,64,128]{2,1,0:T(8,128)S(1)}, u32[]{:S(2)}, u32[]{:S(2)}) collective-permute-start(f32[4,64,128]{2,1,0:T(8,128)S(1)} %z_block.1), channel_id=1, source_target_pairs={{0,128},{4,6},{1,129},{5,7},{2,130},{6,4},{3,131},{7,5},{64,192},{... | collective-permute-start | bytes 393224 | tf_op jit(solution)/shard_map/ppermute | solution.py:29
  58.0 0.4 collective-permute-start.3
  58.4 2.3 %collective-permute-start = (f32[4,64,128]{2,1,0:T(8,128)S(1)}, f32[4,64,128]{2,1,0:T(8,128)S(1)}, u32[]{:S(2)}, u32[]{:S(2)}) collective-permute-start(f32[4,64,128]{2,1,0:T(8,128)S(1)} %z_block.1), channel_id=1, source_target_pairs={{0,192},{4,7},{1,193},{5,4},{2,194},{6,5},{3,195},{7,6},{64,0},{68... | collective-permute-start | bytes 393224 | tf_op jit(solution)/shard_map/ppermute | solution.py:29
  60.7 0.0 collective-permute-done.4
  60.7 2.6 %collective-permute-done.3 = f32[4,64,128]{2,1,0:T(8,128)S(1)} collective-permute-done((f32[4,64,128]{2,1,0:T(8,128)S(1)}, f32[4,64,128]{2,1,0:T(8,128)S(1)}, u32[]{:S(2)}, u32[]{:S(2)}) %collective-permute-start.3) | collective-permute-done | bytes 131104 | tf_op jit(solution)/shard_map/ppermute | solution.py:29
  63.4 3.1 %collective-permute-start.9 = (f32[2,4,64,128]{3,2,1,0:T(8,128)S(1)}, f32[2,4,64,128]{3,2,1,0:T(8,128)S(1)}, u32[]{:S(2)}, u32[]{:S(2)}) collective-permute-start(f32[2,4,64,128]{3,2,1,0:T(8,128)S(1)} %pad_maximum_fusion.1.refs_1_), channel_id=1, source_target_pairs={{0,3},{4,196},{1,0},{5,197},{2,1},{6,198},{3,2},{7,199},{64,67},{6... | collective-permute-start | bytes 786440 | tf_op jit(solution)/shard_map/ppermute | solution.py:29
  66.5 0.0 collective-permute-start.5
  66.5 0.0 collective-permute-done
  66.6 0.1 collective-permute-start.7
  66.6 2.8 %collective-permute-start.1 = (f32[2,4,64,128]{3,2,1,0:T(8,128)S(1)}, f32[2,4,64,128]{3,2,1,0:T(8,128)S(1)}, u32[]{:S(2)}, u32[]{:S(2)}) collective-permute-start(f32[2,4,64,128]{3,2,1,0:T(8,128)S(1)} %pad_maximum_fusion.refs_0_), channel_id=1, source_target_pairs={{0,3},{4,196},{1,0},{5,197},{2,1},{6,198},{3,2},{7,199},{64,67},{6... | collective-permute-start | bytes 786440 | tf_op jit(solution)/shard_map/ppermute | solution.py:29
  69.4 6.6 %collective-permute-done.7.refs_2_ = f32[2,4,64,128]{3,2,1,0:T(8,128)S(1)} collective-permute-done((f32[2,4,64,128]{3,2,1,0:T(8,128)S(1)}, f32[2,4,64,128]{3,2,1,0:T(8,128)S(1)}, u32[]{:S(2)}, u32[]{:S(2)}) %collective-permute-start.7) | collective-permute-done | bytes 262176 | tf_op jit(solution)/shard_map/ppermute | solution.py:29
  76.1 0.0 collective-permute-done.9.refs_3_
  76.1 0.0 collective-permute-done.1.refs_4_
  76.2 0.0 collective-permute-done.5.refs_5_
  76.2 2.8 %collective-permute-start.11 = (f32[12,4,64,128]{3,2,1,0:T(8,128)S(1)}, f32[12,4,64,128]{3,2,1,0:T(8,128)S(1)}, u32[]{:S(2)}, u32[]{:S(2)}) collective-permute-start(f32[12,4,64,128]{3,2,1,0:T(8,128)S(1)} %constant_dynamic-update-slice_fusion), channel_id=1, source_target_pairs={{0,4},{4,0},{1,5},{5,1},{2,6},{6,2},{3,7},{7,3},{8,12},{12,8},{9,1... | collective-permute-start | bytes 4718600 | tf_op jit(solution)/shard_map/ppermute | solution.py:33
  79.0 0.3 collective-permute-start.10
  79.3 1.2 %collective-permute-start.8 = (f32[2,4,64,128]{3,2,1,0:T(8,128)S(1)}, f32[2,4,64,128]{3,2,1,0:T(8,128)S(1)}, u32[]{:S(2)}, u32[]{:S(2)}) collective-permute-start(f32[2,4,64,128]{3,2,1,0:T(8,128)S(1)} %collective-permute-done.7.refs_2_), channel_id=1, source_target_pairs={{0,1},{4,68},{1,2},{5,69},{2,3},{6,70},{3,0},{7,71},{64,65},{68,13... | collective-permute-start | bytes 786440 | tf_op jit(solution)/shard_map/ppermute | solution.py:29
  80.4 0.5 collective-permute-start.6
  81.0 0.3 collective-permute-start.2
  81.3 1.2 %shard_map.37.refs_3_ = f32[4,512,512]{2,1,0:T(8,128)} custom-call(f32[2,4,64,128]{3,2,1,0:T(8,128)S(1)} %pad_maximum_fusion.refs_0_, f32[2,4,64,128]{3,2,1,0:T(8,128)S(1)} %pad_maximum_fusion.1.refs_1_, f32[2,4,64,128]{3,2,1,0:T(8,128)S(1)} %collective-permute-done.7.refs_2_, f32[2,4,64,128]{3,2,1,0:T(8,128)S(1)} %collective-permute-done.9.refs_3_, ...), custom_call_target="tpu_custom_call" | custom-call | tf_op jit(solution)/shard_map/pallas_call | solution.py:118
  82.5 2.0 %collective-permute-done.10.refs_1_ = f32[2,4,64,128]{3,2,1,0:T(8,128)S(1)} collective-permute-done((f32[2,4,64,128]{3,2,1,0:T(8,128)S(1)}, f32[2,4,64,128]{3,2,1,0:T(8,128)S(1)}, u32[]{:S(2)}, u32[]{:S(2)}) %collective-permute-start.10) | collective-permute-done | bytes 262176 | tf_op jit(solution)/shard_map/ppermute | solution.py:29
  84.5 1.5 %collective-permute-done.8.refs_0_ = f32[2,4,64,128]{3,2,1,0:T(8,128)S(1)} collective-permute-done((f32[2,4,64,128]{3,2,1,0:T(8,128)S(1)}, f32[2,4,64,128]{3,2,1,0:T(8,128)S(1)}, u32[]{:S(2)}, u32[]{:S(2)}) %collective-permute-start.8) | collective-permute-done | bytes 262176 | tf_op jit(solution)/shard_map/ppermute | solution.py:29
  86.0 0.0 collective-permute-done.11.refs_2_
  86.0 1.4 %shard_map.38.refs_2_ = f32[4,512,512]{2,1,0:T(8,128)} custom-call(f32[2,4,64,128]{3,2,1,0:T(8,128)S(1)} %collective-permute-done.8.refs_0_, f32[2,4,64,128]{3,2,1,0:T(8,128)S(1)} %collective-permute-done.10.refs_1_, f32[12,4,64,128]{3,2,1,0:T(8,128)S(1)} %collective-permute-done.11.refs_2_, ...), custom_call_target="tpu_custom_call", output_to_operand_aliasing={{}: (3, {})} | custom-call | tf_op jit(solution)/shard_map/pallas_call | solution.py:118
  87.4 1.9 %collective-permute-done.6.refs_1_ = f32[2,4,64,128]{3,2,1,0:T(8,128)S(1)} collective-permute-done((f32[2,4,64,128]{3,2,1,0:T(8,128)S(1)}, f32[2,4,64,128]{3,2,1,0:T(8,128)S(1)}, u32[]{:S(2)}, u32[]{:S(2)}) %collective-permute-start.6) | collective-permute-done | bytes 262176 | tf_op jit(solution)/shard_map/ppermute | solution.py:29
  89.3 0.0 collective-permute-done.2.refs_0_
  89.3 0.8 shard_map.39
  (11 shorter events, 0.2 us)
Async XLA Ops:
  0.0 1.2 %copy-start = (f32[1,4,128,512]{3,2,1,0:T(8,128)S(1)}, f32[1,4,128,512]{3,2,1,0:T(8,128)}, u32[]{:S(2)}) copy-start(f32[1,4,128,512]{3,2,1,0:T(8,128)} %param.3) | copy-start | bytes 3145732
  1.3 41.3 %copy-start.1 = (s32[64,4]{0,1:T(4,128)S(1)}, s32[64,4]{0,1:T(4,128)}, u32[]{:S(2)}) copy-start(s32[64,4]{0,1:T(4,128)} %param.5) | copy-start | bytes 3076
  1.3 41.3 %copy-start.2 = (s32[64]{0:T(128)S(1)}, s32[64]{0:T(128)}, u32[]{:S(2)}) copy-start(s32[64]{0:T(128)} %order_ref.1) | copy-start | bytes 772
  55.0 5.7 %collective-permute-start.4 = (f32[4,64,128]{2,1,0:T(8,128)S(1)}, f32[4,64,128]{2,1,0:T(8,128)S(1)}, u32[]{:S(2)}, u32[]{:S(2)}) collective-permute-start(f32[4,64,128]{2,1,0:T(8,128)S(1)} %z_block.1), channel_id=1, source_target_pairs={{0,128},{4,6},{1,129},{5,7},{2,130},{6,4},{3,131},{7,5},{64,192},{... | collective-permute-start | bytes 393224 | tf_op jit(solution)/shard_map/ppermute | solution.py:29
  58.0 5.3 %collective-permute-start.3 = (f32[4,64,128]{2,1,0:T(8,128)S(1)}, f32[4,64,128]{2,1,0:T(8,128)S(1)}, u32[]{:S(2)}, u32[]{:S(2)}) collective-permute-start(f32[4,64,128]{2,1,0:T(8,128)S(1)} %z_block.1), channel_id=1, source_target_pairs={{0,64},{4,5},{1,65},{5,6},{2,66},{6,7},{3,67},{7,4},{64,128},{68,6... | collective-permute-start | bytes 393224 | tf_op jit(solution)/shard_map/ppermute | solution.py:29
  58.4 8.1 %collective-permute-start = (f32[4,64,128]{2,1,0:T(8,128)S(1)}, f32[4,64,128]{2,1,0:T(8,128)S(1)}, u32[]{:S(2)}, u32[]{:S(2)}) collective-permute-start(f32[4,64,128]{2,1,0:T(8,128)S(1)} %z_block.1), channel_id=1, source_target_pairs={{0,192},{4,7},{1,193},{5,4},{2,194},{6,5},{3,195},{7,6},{64,0},{68... | collective-permute-start | bytes 393224 | tf_op jit(solution)/shard_map/ppermute | solution.py:29
  63.4 12.7 %collective-permute-start.9 = (f32[2,4,64,128]{3,2,1,0:T(8,128)S(1)}, f32[2,4,64,128]{3,2,1,0:T(8,128)S(1)}, u32[]{:S(2)}, u32[]{:S(2)}) collective-permute-start(f32[2,4,64,128]{3,2,1,0:T(8,128)S(1)} %pad_maximum_fusion.1.refs_1_), channel_id=1, source_target_pairs={{0,3},{4,196},{1,0},{5,197},{2,1},{6,198},{3,2},{7,199},{64,67},{6... | collective-permute-start | bytes 786440 | tf_op jit(solution)/shard_map/ppermute | solution.py:29
  66.5 9.6 %collective-permute-start.5 = (f32[2,4,64,128]{3,2,1,0:T(8,128)S(1)}, f32[2,4,64,128]{3,2,1,0:T(8,128)S(1)}, u32[]{:S(2)}, u32[]{:S(2)}) collective-permute-start(f32[2,4,64,128]{3,2,1,0:T(8,128)S(1)} %pad_maximum_fusion.1.refs_1_), channel_id=1, source_target_pairs={{0,1},{4,68},{1,2},{5,69},{2,3},{6,70},{3,0},{7,71},{64,65},{68,13... | collective-permute-start | bytes 786440 | tf_op jit(solution)/shard_map/ppermute | solution.py:29
  66.6 9.5 %collective-permute-start.7 = (f32[2,4,64,128]{3,2,1,0:T(8,128)S(1)}, f32[2,4,64,128]{3,2,1,0:T(8,128)S(1)}, u32[]{:S(2)}, u32[]{:S(2)}) collective-permute-start(f32[2,4,64,128]{3,2,1,0:T(8,128)S(1)} %pad_maximum_fusion.refs_0_), channel_id=1, source_target_pairs={{0,1},{4,68},{1,2},{5,69},{2,3},{6,70},{3,0},{7,71},{64,65},{68,13... | collective-permute-start | bytes 786440 | tf_op jit(solution)/shard_map/ppermute | solution.py:29
  66.6 9.5 %collective-permute-start.1 = (f32[2,4,64,128]{3,2,1,0:T(8,128)S(1)}, f32[2,4,64,128]{3,2,1,0:T(8,128)S(1)}, u32[]{:S(2)}, u32[]{:S(2)}) collective-permute-start(f32[2,4,64,128]{3,2,1,0:T(8,128)S(1)} %pad_maximum_fusion.refs_0_), channel_id=1, source_target_pairs={{0,3},{4,196},{1,0},{5,197},{2,1},{6,198},{3,2},{7,199},{64,67},{6... | collective-permute-start | bytes 786440 | tf_op jit(solution)/shard_map/ppermute | solution.py:29
  76.2 9.8 %collective-permute-start.11 = (f32[12,4,64,128]{3,2,1,0:T(8,128)S(1)}, f32[12,4,64,128]{3,2,1,0:T(8,128)S(1)}, u32[]{:S(2)}, u32[]{:S(2)}) collective-permute-start(f32[12,4,64,128]{3,2,1,0:T(8,128)S(1)} %constant_dynamic-update-slice_fusion), channel_id=1, source_target_pairs={{0,4},{4,0},{1,5},{5,1},{2,6},{6,2},{3,7},{7,3},{8,12},{12,8},{9,1... | collective-permute-start | bytes 4718600 | tf_op jit(solution)/shard_map/ppermute | solution.py:33
  79.0 5.5 %collective-permute-start.10 = (f32[2,4,64,128]{3,2,1,0:T(8,128)S(1)}, f32[2,4,64,128]{3,2,1,0:T(8,128)S(1)}, u32[]{:S(2)}, u32[]{:S(2)}) collective-permute-start(f32[2,4,64,128]{3,2,1,0:T(8,128)S(1)} %collective-permute-done.9.refs_3_), channel_id=1, source_target_pairs={{0,3},{4,196},{1,0},{5,197},{2,1},{6,198},{3,2},{7,199},{64,67},{6... | collective-permute-start | bytes 786440 | tf_op jit(solution)/shard_map/ppermute | solution.py:29
  79.3 6.7 %collective-permute-start.8 = (f32[2,4,64,128]{3,2,1,0:T(8,128)S(1)}, f32[2,4,64,128]{3,2,1,0:T(8,128)S(1)}, u32[]{:S(2)}, u32[]{:S(2)}) collective-permute-start(f32[2,4,64,128]{3,2,1,0:T(8,128)S(1)} %collective-permute-done.7.refs_2_), channel_id=1, source_target_pairs={{0,1},{4,68},{1,2},{5,69},{2,3},{6,70},{3,0},{7,71},{64,65},{68,13... | collective-permute-start | bytes 786440 | tf_op jit(solution)/shard_map/ppermute | solution.py:29
  80.4 8.9 %collective-permute-start.6 = (f32[2,4,64,128]{3,2,1,0:T(8,128)S(1)}, f32[2,4,64,128]{3,2,1,0:T(8,128)S(1)}, u32[]{:S(2)}, u32[]{:S(2)}) collective-permute-start(f32[2,4,64,128]{3,2,1,0:T(8,128)S(1)} %collective-permute-done.5.refs_5_), channel_id=1, source_target_pairs={{0,5},{4,64},{1,6},{5,65},{2,7},{6,66},{3,4},{7,67},{64,69},{68,12... | collective-permute-start | bytes 786440 | tf_op jit(solution)/shard_map/ppermute | solution.py:29
  81.0 8.3 %collective-permute-start.2 = (f32[2,4,64,128]{3,2,1,0:T(8,128)S(1)}, f32[2,4,64,128]{3,2,1,0:T(8,128)S(1)}, u32[]{:S(2)}, u32[]{:S(2)}) collective-permute-start(f32[2,4,64,128]{3,2,1,0:T(8,128)S(1)} %collective-permute-done.1.refs_4_), channel_id=1, source_target_pairs={{0,7},{4,192},{1,4},{5,193},{2,5},{6,194},{3,6},{7,195},{64,71},{6... | collective-permute-start | bytes 786440 | tf_op jit(solution)/shard_map/ppermute | solution.py:29

commit v7 on v6

--- a/solution.py
+++ b/solution.py
@@ -158,9 +158,6 @@
         name="z_block",
     )(pieces)
 
-    def go_crossed(value, by):
-        return shifted_plane(value, by, True, True)
-
     near = shifted_plane(block, 1, False)
     far = shifted_plane(block, 2, False)
     back = shifted_plane(block, -1, False)
@@ -170,20 +167,22 @@
     head_after = shifted_plane(head, -1, True)
     tail_after = shifted_plane(tail, -1, True)
     tail_before = shifted_plane(tail, 1, True)
-    head_across = shifted_plane(head_before, 1, True)
-    tail_across = shifted_plane(tail_after, -1, True)
-    held = (
+    head_far = shifted_plane(head, 2, True)
+    tail_far = shifted_plane(tail, 2, True)
+    first = (
         (head, STEPS[:2], 0),
         (tail, STEPS[2:], 0),
         (head_before, STEPS[:2], -1),
+        (head_after, STEPS[:2], 1),
+        (head_far, STEPS[:2], -2),
+        (tail_far, STEPS[2:], -2),
+    )
+    last = (
         (tail_after, STEPS[2:], 1),
-        (head_after, STEPS[:2], 1),
         (tail_before, STEPS[2:], -1),
     )
-    last = ((head_across, STEPS[:2], -2), (tail_across, STEPS[2:], -2))
-    swapped = other_core(jnp.concatenate([part[0] for part in held]))
-    head_crossed = go_crossed(head_after, -1)
-    tail_crossed = go_crossed(tail_before, 1)
+    swapped = other_core(jnp.concatenate([part[0] for part in first]))
+    swapped_last = other_core(jnp.concatenate([part[0] for part in last]))
 
     def blocks(parts):
         return [(part, 0, False, *how) for part, *how in parts]
@@ -191,9 +190,9 @@
     def from_other(joined, parts):
         return [(joined, 2 * k, True, *how) for k, (part, *how) in enumerate(parts)]
 
-    image = image_call(blocks(held), None)
-    image = image_call(blocks(last) + from_other(swapped, held), image)
-    return image_call(from_other(head_crossed, last[:1]) + from_other(tail_crossed, last[1:]), image)
+    image = image_call(blocks(first), None)
+    image = image_call(blocks(last) + from_other(swapped, first), image)
+    return image_call(from_other(swapped_last, last), image)
 
 
 def solution(mesh):

time: 90.3 us -> 94.1 us (1.042)
  waiting for transfers between devices: 14.6 us -> 17.3 us
  starting transfers between devices: 16.7 us -> 17.7 us
    ppermute x11 -> x9, waiting for transfers between devices: 14.6 us -> 17.3 us  [shifted_plane(): return lax.ppermute(value, PLANE, pairs)]
    ppermute x1 -> x2, starting transfers between devices: 2.78 us -> 3.97 us  [other_core(): return lax.ppermute(value, C, [(0, 1), (1, 0)])]
    ppermute x11 -> x9, starting transfers between devices: 13.9 us -> 13.7 us  [shifted_plane(): return lax.ppermute(value, PLANE, pairs)]
  transfers between devices with their start and end apart: 12 -> 11, of which waited for: 5 -> 6; matrix products, arithmetic and copies ran while one was open for 0% -> 0% of each run, Pallas kernels for 3% -> 3%
where the time goes in v7:
time: 94.1 us; the launch traced here: 93.9 us
  blocking collectives  52.9 us (56%)
  starting transfers between devices  17.7 us (19%)
  waiting for transfers between devices  17.3 us (18%)
  Pallas kernels  4.42 us (5%)
  local copies, waits for them, and re-layouts  1.35 us (1%)
    all_to_all x1, blocking collectives, body(): lax.all_to_all(outgoing, DEPTH, split_axis=0, concat_axis=0, tiled=True)  41.3 us
    ppermute x9, waiting for transfers between devices, shifted_plane(): return lax.ppermute(value, PLANE, pairs)  17.3 us
    ppermute x9, starting transfers between devices, shifted_plane(): return lax.ppermute(value, PLANE, pairs)  13.7 us
    all_to_all x1, blocking collectives, body(): pieces = lax.all_to_all(piece, Z, split_axis=0, concat_axis=0, tiled=True)  11.6 us
    ppermute x2, starting transfers between devices, other_core(): return lax.ppermute(value, C, [(0, 1), (1, 0)])  3.97 us
    pallas_call x3, Pallas kernels, image_call(): pl.pallas_call(kernel, out_shape=jax.ShapeDtypeStruct((4, 512, 512), jnp....  3.53 us
  transfers between devices with their start and end apart: 11, of which 6 were waited for; matrix products, arithmetic and copies ran while one was open for 0% of the time, Pallas kernels for 3%

profile of v7, /device:TPU:1, one launch (start us, length us, event | category | flops | bytes accessed | tf_op | source)
XLA Modules:
  0.0 93.9 jit_solution(3219856640369370079)
XLA Ops:
  0.0 0.0 copy-start
  0.0 1.2 %copy-done = f32[1,4,128,512]{3,2,1,0:T(8,128)S(1)} copy-done((f32[1,4,128,512]{3,2,1,0:T(8,128)S(1)}, f32[1,4,128,512]{3,2,1,0:T(8,128)}, u32[]{:S(2)}) %copy-start) | copy-done | bytes 1048600
  1.2 0.1 outgoing.1
  1.3 0.0 copy-start.1
  1.3 0.0 copy-start.2
  1.3 41.3 %all_to_all.10.layers_ref = f32[64,4,8,128]{3,2,1,0:T(8,128)S(1)} all-to-all(f32[64,4,8,128]{3,2,1,0:T(8,128)S(1)} %outgoing.1), channel_id=1, replica_groups=mesh['depth_0'=4,'depth_1'=8,'depth_2'=2,'tile'=4] {'depth_0','depth_1',..., dimensions={0} | all-to-all | bytes 2097152 | tf_op jit(solution)/shard_map/all_to_all | solution.py:141
  42.6 0.0 copy-done.1
  42.6 0.0 copy-done.2
  42.6 0.8 composite.1
  43.4 11.6 %all_to_all.11.pieces_ref = f32[8,4,8,128]{3,2,1,0:T(8,128)S(1)} all-to-all(f32[8,4,8,128]{3,2,1,0:T(8,128)S(1)} %composite.1), channel_id=1, replica_groups=mesh['depth_0'=4,'depth_1'=8,'depth_2'=2,'tile'=4] {'depth_1'}, dimensions={0} | all-to-all | bytes 262144 | tf_op jit(solution)/shard_map/all_to_all | solution.py:151
  55.0 1.4 %collective-permute-start = (f32[4,64,128]{2,1,0:T(8,128)S(1)}, f32[4,64,128]{2,1,0:T(8,128)S(1)}, u32[]{:S(2)}, u32[]{:S(2)}) collective-permute-start(f32[4,64,128]{2,1,0:T(8,128)S(1)} %z_block.1), channel_id=1, source_target_pairs={{0,64},{4,5},{1,65},{5,6},{2,66},{6,7},{3,67},{7,4},{64,128},{68,6... | collective-permute-start | bytes 393224 | tf_op jit(solution)/shard_map/ppermute | solution.py:29
  56.4 2.6 %collective-permute-start.1 = (f32[4,64,128]{2,1,0:T(8,128)S(1)}, f32[4,64,128]{2,1,0:T(8,128)S(1)}, u32[]{:S(2)}, u32[]{:S(2)}) collective-permute-start(f32[4,64,128]{2,1,0:T(8,128)S(1)} %z_block.1), channel_id=1, source_target_pairs={{0,128},{4,6},{1,129},{5,7},{2,130},{6,4},{3,131},{7,5},{64,192},{... | collective-permute-start | bytes 393224 | tf_op jit(solution)/shard_map/ppermute | solution.py:29
  59.0 1.1 %collective-permute-start.5 = (f32[4,64,128]{2,1,0:T(8,128)S(1)}, f32[4,64,128]{2,1,0:T(8,128)S(1)}, u32[]{:S(2)}, u32[]{:S(2)}) collective-permute-start(f32[4,64,128]{2,1,0:T(8,128)S(1)} %z_block.1), channel_id=1, source_target_pairs={{0,192},{4,7},{1,193},{5,4},{2,194},{6,5},{3,195},{7,6},{64,0},{68... | collective-permute-start | bytes 393224 | tf_op jit(solution)/shard_map/ppermute | solution.py:29
  60.1 3.0 %collective-permute-done.5 = f32[4,64,128]{2,1,0:T(8,128)S(1)} collective-permute-done((f32[4,64,128]{2,1,0:T(8,128)S(1)}, f32[4,64,128]{2,1,0:T(8,128)S(1)}, u32[]{:S(2)}, u32[]{:S(2)}) %collective-permute-start.5) | collective-permute-done | bytes 131104 | tf_op jit(solution)/shard_map/ppermute | solution.py:29
  63.2 0.1 collective-permute-start.6
  63.3 3.1 %collective-permute-start.7 = (f32[2,4,64,128]{3,2,1,0:T(8,128)S(1)}, f32[2,4,64,128]{3,2,1,0:T(8,128)S(1)}, u32[]{:S(2)}, u32[]{:S(2)}) collective-permute-start(f32[2,4,64,128]{3,2,1,0:T(8,128)S(1)} %pad_maximum_fusion.2.refs_0_), channel_id=1, source_target_pairs={{0,3},{4,196},{1,0},{5,197},{2,1},{6,198},{3,2},{7,199},{64,67},{6... | collective-permute-start | bytes 786440 | tf_op jit(solution)/shard_map/ppermute | solution.py:29
  66.4 1.1 %collective-permute-start.8 = (f32[2,4,64,128]{3,2,1,0:T(8,128)S(1)}, f32[2,4,64,128]{3,2,1,0:T(8,128)S(1)}, u32[]{:S(2)}, u32[]{:S(2)}) collective-permute-start(f32[2,4,64,128]{3,2,1,0:T(8,128)S(1)} %pad_maximum_fusion.2.refs_0_), channel_id=1, source_target_pairs={{0,2},{4,132},{1,3},{5,133},{2,0},{6,134},{3,1},{7,135},{64,66},{6... | collective-permute-start | bytes 786440 | tf_op jit(solution)/shard_map/ppermute | solution.py:29
  67.5 0.0 collective-permute-done
  67.5 0.0 collective-permute-done.1
  67.5 2.0 %collective-permute-start.9 = (f32[2,4,64,128]{3,2,1,0:T(8,128)S(1)}, f32[2,4,64,128]{3,2,1,0:T(8,128)S(1)}, u32[]{:S(2)}, u32[]{:S(2)}) collective-permute-start(f32[2,4,64,128]{3,2,1,0:T(8,128)S(1)} %pad_maximum_fusion.1.refs_1_), channel_id=1, source_target_pairs={{0,2},{4,132},{1,3},{5,133},{2,0},{6,134},{3,1},{7,135},{64,66},{6... | collective-permute-start | bytes 786440 | tf_op jit(solution)/shard_map/ppermute | solution.py:29
  69.5 0.8 collective-permute-done.6.refs_2_
  70.4 4.9 %collective-permute-done.7.refs_3_ = f32[2,4,64,128]{3,2,1,0:T(8,128)S(1)} collective-permute-done((f32[2,4,64,128]{3,2,1,0:T(8,128)S(1)}, f32[2,4,64,128]{3,2,1,0:T(8,128)S(1)}, u32[]{:S(2)}, u32[]{:S(2)}) %collective-permute-start.7) | collective-permute-done | bytes 262176 | tf_op jit(solution)/shard_map/ppermute | solution.py:29
  75.4 0.0 collective-permute-done.8.refs_4_
  75.4 1.8 %collective-permute-done.9.refs_5_ = f32[2,4,64,128]{3,2,1,0:T(8,128)S(1)} collective-permute-done((f32[2,4,64,128]{3,2,1,0:T(8,128)S(1)}, f32[2,4,64,128]{3,2,1,0:T(8,128)S(1)}, u32[]{:S(2)}, u32[]{:S(2)}) %collective-permute-start.9) | collective-permute-done | bytes 262176 | tf_op jit(solution)/shard_map/ppermute | solution.py:29
  77.2 3.3 %collective-permute-start.10 = (f32[12,4,64,128]{3,2,1,0:T(8,128)S(1)}, f32[12,4,64,128]{3,2,1,0:T(8,128)S(1)}, u32[]{:S(2)}, u32[]{:S(2)}) collective-permute-start(f32[12,4,64,128]{3,2,1,0:T(8,128)S(1)} %constant_dynamic-update-slice_fusion), channel_id=1, source_target_pairs={{0,4},{4,0},{1,5},{5,1},{2,6},{6,2},{3,7},{7,3},{8,12},{12,8},{9,1... | collective-permute-start | bytes 4718600 | tf_op jit(solution)/shard_map/ppermute | solution.py:33
  80.4 2.4 %collective-permute-start.2 = (f32[2,4,64,128]{3,2,1,0:T(8,128)S(1)}, f32[2,4,64,128]{3,2,1,0:T(8,128)S(1)}, u32[]{:S(2)}, u32[]{:S(2)}) collective-permute-start(f32[2,4,64,128]{3,2,1,0:T(8,128)S(1)} %pad_maximum_fusion.1.refs_1_), channel_id=1, source_target_pairs={{0,3},{4,196},{1,0},{5,197},{2,1},{6,198},{3,2},{7,199},{64,67},{6... | collective-permute-start | bytes 786440 | tf_op jit(solution)/shard_map/ppermute | solution.py:29
  82.8 0.0 collective-permute-start.3
  82.8 3.3 %collective-permute-done.2.refs_0_ = f32[2,4,64,128]{3,2,1,0:T(8,128)S(1)} collective-permute-done((f32[2,4,64,128]{3,2,1,0:T(8,128)S(1)}, f32[2,4,64,128]{3,2,1,0:T(8,128)S(1)}, u32[]{:S(2)}, u32[]{:S(2)}) %collective-permute-start.2) | collective-permute-done | bytes 262176 | tf_op jit(solution)/shard_map/ppermute | solution.py:29
  86.2 3.4 %collective-permute-done.3.refs_1_ = f32[2,4,64,128]{3,2,1,0:T(8,128)S(1)} collective-permute-done((f32[2,4,64,128]{3,2,1,0:T(8,128)S(1)}, f32[2,4,64,128]{3,2,1,0:T(8,128)S(1)}, u32[]{:S(2)}, u32[]{:S(2)}) %collective-permute-start.3) | collective-permute-done | bytes 262176 | tf_op jit(solution)/shard_map/ppermute | solution.py:29
  89.6 0.7 collective-permute-start.4
  90.3 1.2 %shard_map.37.refs_3_ = f32[4,512,512]{2,1,0:T(8,128)} custom-call(f32[2,4,64,128]{3,2,1,0:T(8,128)S(1)} %pad_maximum_fusion.2.refs_0_, f32[2,4,64,128]{3,2,1,0:T(8,128)S(1)} %pad_maximum_fusion.1.refs_1_, f32[2,4,64,128]{3,2,1,0:T(8,128)S(1)} %collective-permute-done.6.refs_2_, f32[2,4,64,128]{3,2,1,0:T(8,128)S(1)} %collective-permute-done.7.refs_3_, ...), custom_call_target="tpu_custom_call" | custom-call | tf_op jit(solution)/shard_map/pallas_call | solution.py:118
  91.6 0.0 collective-permute-done.10.refs_2_
  91.6 1.5 %shard_map.38.refs_1_ = f32[4,512,512]{2,1,0:T(8,128)} custom-call(f32[2,4,64,128]{3,2,1,0:T(8,128)S(1)} %collective-permute-done.2.refs_0_, f32[2,4,64,128]{3,2,1,0:T(8,128)S(1)} %collective-permute-done.3.refs_1_, f32[12,4,64,128]{3,2,1,0:T(8,128)S(1)} %collective-permute-done.10.refs_2_, ...), custom_call_target="tpu_custom_call", output_to_operand_aliasing={{}: (3, {})} | custom-call | tf_op jit(solution)/shard_map/pallas_call | solution.py:118
  93.0 0.0 collective-permute-done.4.refs_0_
  93.1 0.8 shard_map.39
  (12 shorter events, 0.2 us)
Async XLA Ops:
  0.0 1.2 %copy-start = (f32[1,4,128,512]{3,2,1,0:T(8,128)S(1)}, f32[1,4,128,512]{3,2,1,0:T(8,128)}, u32[]{:S(2)}) copy-start(f32[1,4,128,512]{3,2,1,0:T(8,128)} %param.3) | copy-start | bytes 3145732
  1.3 41.3 %copy-start.1 = (s32[64,4]{0,1:T(4,128)S(1)}, s32[64,4]{0,1:T(4,128)}, u32[]{:S(2)}) copy-start(s32[64,4]{0,1:T(4,128)} %param.5) | copy-start | bytes 3076
  1.3 41.3 %copy-start.2 = (s32[64]{0:T(128)S(1)}, s32[64]{0:T(128)}, u32[]{:S(2)}) copy-start(s32[64]{0:T(128)} %order_ref.1) | copy-start | bytes 772
  55.0 12.5 %collective-permute-start = (f32[4,64,128]{2,1,0:T(8,128)S(1)}, f32[4,64,128]{2,1,0:T(8,128)S(1)}, u32[]{:S(2)}, u32[]{:S(2)}) collective-permute-start(f32[4,64,128]{2,1,0:T(8,128)S(1)} %z_block.1), channel_id=1, source_target_pairs={{0,64},{4,5},{1,65},{5,6},{2,66},{6,7},{3,67},{7,4},{64,128},{68,6... | collective-permute-start | bytes 393224 | tf_op jit(solution)/shard_map/ppermute | solution.py:29
  56.4 11.1 %collective-permute-start.1 = (f32[4,64,128]{2,1,0:T(8,128)S(1)}, f32[4,64,128]{2,1,0:T(8,128)S(1)}, u32[]{:S(2)}, u32[]{:S(2)}) collective-permute-start(f32[4,64,128]{2,1,0:T(8,128)S(1)} %z_block.1), channel_id=1, source_target_pairs={{0,128},{4,6},{1,129},{5,7},{2,130},{6,4},{3,131},{7,5},{64,192},{... | collective-permute-start | bytes 393224 | tf_op jit(solution)/shard_map/ppermute | solution.py:29
  59.0 4.1 %collective-permute-start.5 = (f32[4,64,128]{2,1,0:T(8,128)S(1)}, f32[4,64,128]{2,1,0:T(8,128)S(1)}, u32[]{:S(2)}, u32[]{:S(2)}) collective-permute-start(f32[4,64,128]{2,1,0:T(8,128)S(1)} %z_block.1), channel_id=1, source_target_pairs={{0,192},{4,7},{1,193},{5,4},{2,194},{6,5},{3,195},{7,6},{64,0},{68... | collective-permute-start | bytes 393224 | tf_op jit(solution)/shard_map/ppermute | solution.py:29
  63.2 7.2 %collective-permute-start.6 = (f32[2,4,64,128]{3,2,1,0:T(8,128)S(1)}, f32[2,4,64,128]{3,2,1,0:T(8,128)S(1)}, u32[]{:S(2)}, u32[]{:S(2)}) collective-permute-start(f32[2,4,64,128]{3,2,1,0:T(8,128)S(1)} %pad_maximum_fusion.2.refs_0_), channel_id=1, source_target_pairs={{0,1},{4,68},{1,2},{5,69},{2,3},{6,70},{3,0},{7,71},{64,65},{68,13... | collective-permute-start | bytes 786440 | tf_op jit(solution)/shard_map/ppermute | solution.py:29
  63.3 12.1 %collective-permute-start.7 = (f32[2,4,64,128]{3,2,1,0:T(8,128)S(1)}, f32[2,4,64,128]{3,2,1,0:T(8,128)S(1)}, u32[]{:S(2)}, u32[]{:S(2)}) collective-permute-start(f32[2,4,64,128]{3,2,1,0:T(8,128)S(1)} %pad_maximum_fusion.2.refs_0_), channel_id=1, source_target_pairs={{0,3},{4,196},{1,0},{5,197},{2,1},{6,198},{3,2},{7,199},{64,67},{6... | collective-permute-start | bytes 786440 | tf_op jit(solution)/shard_map/ppermute | solution.py:29
  66.4 9.0 %collective-permute-start.8 = (f32[2,4,64,128]{3,2,1,0:T(8,128)S(1)}, f32[2,4,64,128]{3,2,1,0:T(8,128)S(1)}, u32[]{:S(2)}, u32[]{:S(2)}) collective-permute-start(f32[2,4,64,128]{3,2,1,0:T(8,128)S(1)} %pad_maximum_fusion.2.refs_0_), channel_id=1, source_target_pairs={{0,2},{4,132},{1,3},{5,133},{2,0},{6,134},{3,1},{7,135},{64,66},{6... | collective-permute-start | bytes 786440 | tf_op jit(solution)/shard_map/ppermute | solution.py:29
  67.5 9.6 %collective-permute-start.9 = (f32[2,4,64,128]{3,2,1,0:T(8,128)S(1)}, f32[2,4,64,128]{3,2,1,0:T(8,128)S(1)}, u32[]{:S(2)}, u32[]{:S(2)}) collective-permute-start(f32[2,4,64,128]{3,2,1,0:T(8,128)S(1)} %pad_maximum_fusion.1.refs_1_), channel_id=1, source_target_pairs={{0,2},{4,132},{1,3},{5,133},{2,0},{6,134},{3,1},{7,135},{64,66},{6... | collective-permute-start | bytes 786440 | tf_op jit(solution)/shard_map/ppermute | solution.py:29
  77.2 14.4 %collective-permute-start.10 = (f32[12,4,64,128]{3,2,1,0:T(8,128)S(1)}, f32[12,4,64,128]{3,2,1,0:T(8,128)S(1)}, u32[]{:S(2)}, u32[]{:S(2)}) collective-permute-start(f32[12,4,64,128]{3,2,1,0:T(8,128)S(1)} %constant_dynamic-update-slice_fusion), channel_id=1, source_target_pairs={{0,4},{4,0},{1,5},{5,1},{2,6},{6,2},{3,7},{7,3},{8,12},{12,8},{9,1... | collective-permute-start | bytes 4718600 | tf_op jit(solution)/shard_map/ppermute | solution.py:33
  80.4 5.7 %collective-permute-start.2 = (f32[2,4,64,128]{3,2,1,0:T(8,128)S(1)}, f32[2,4,64,128]{3,2,1,0:T(8,128)S(1)}, u32[]{:S(2)}, u32[]{:S(2)}) collective-permute-start(f32[2,4,64,128]{3,2,1,0:T(8,128)S(1)} %pad_maximum_fusion.1.refs_1_), channel_id=1, source_target_pairs={{0,3},{4,196},{1,0},{5,197},{2,1},{6,198},{3,2},{7,199},{64,67},{6... | collective-permute-start | bytes 786440 | tf_op jit(solution)/shard_map/ppermute | solution.py:29
  82.8 6.7 %collective-permute-start.3 = (f32[2,4,64,128]{3,2,1,0:T(8,128)S(1)}, f32[2,4,64,128]{3,2,1,0:T(8,128)S(1)}, u32[]{:S(2)}, u32[]{:S(2)}) collective-permute-start(f32[2,4,64,128]{3,2,1,0:T(8,128)S(1)} %pad_maximum_fusion.1.refs_1_), channel_id=1, source_target_pairs={{0,1},{4,68},{1,2},{5,69},{2,3},{6,70},{3,0},{7,71},{64,65},{68,13... | collective-permute-start | bytes 786440 | tf_op jit(solution)/shard_map/ppermute | solution.py:29
  89.6 3.4 %collective-permute-start.4 = (f32[4,4,64,128]{3,2,1,0:T(8,128)S(1)}, f32[4,4,64,128]{3,2,1,0:T(8,128)S(1)}, u32[]{:S(2)}, u32[]{:S(2)}) collective-permute-start(f32[4,4,64,128]{3,2,1,0:T(8,128)S(1)} %pad_maximum_fusion), channel_id=1, source_target_pairs={{0,4},{4,0},{1,5},{5,1},{2,6},{6,2},{3,7},{7,3},{8,12},{12,8},{9,1... | collective-permute-start | bytes 1572872 | tf_op jit(solution)/shard_map/ppermute | solution.py:33

commit v8 on v7

--- a/solution.py
+++ b/solution.py
@@ -37,7 +37,7 @@
     count = layers_ref.shape[0]
     tile = lax.axis_index(Y)
 
-    parts = 4
+    parts = 8
     run = count // parts
 
     def step(k, accumulated):
@@ -52,7 +52,7 @@
         return tuple(new)
 
     zero = jnp.zeros(layers_ref.shape[2:], jnp.float32)
-    runs = lax.fori_loop(0, run, step, ((zero,) * 4,) * parts, unroll=4)
+    runs = lax.fori_loop(0, run, step, ((zero,) * 4,) * parts, unroll=8)
     done = runs[0]
     for far in runs[1:]:
         through = 1.0 - done[3]
@@ -173,6 +173,8 @@
         (head, STEPS[:2], 0),
         (tail, STEPS[2:], 0),
         (head_before, STEPS[:2], -1),
+    )
+    middle = (
         (head_after, STEPS[:2], 1),
         (head_far, STEPS[:2], -2),
         (tail_far, STEPS[2:], -2),
@@ -182,6 +184,7 @@
         (tail_before, STEPS[2:], -1),
     )
     swapped = other_core(jnp.concatenate([part[0] for part in first]))
+    swapped_middle = other_core(jnp.concatenate([part[0] for part in middle]))
     swapped_last = other_core(jnp.concatenate([part[0] for part in last]))
 
     def blocks(parts):
@@ -190,8 +193,10 @@
     def from_other(joined, parts):
         return [(joined, 2 * k, True, *how) for k, (part, *how) in enumerate(parts)]
 
-    image = image_call(blocks(first), None)
-    image = image_call(blocks(last) + from_other(swapped, first), image)
+    image = image_call(blocks(first) + blocks(middle), None)
+    image = image_call(
+        blocks(last) + from_other(swapped, first) + from_other(swapped_middle, middle), image
+    )
     return image_call(from_other(swapped_last, last), image)
 
 

time: 94.1 us -> 91.8 us (0.976)
  waiting for transfers between devices: 17.3 us -> 10.7 us
  starting transfers between devices: 17.7 us -> 22 us
    ppermute x9, waiting for transfers between devices: 17.3 us -> 10.7 us  [shifted_plane(): return lax.ppermute(value, PLANE, pairs)]
    ppermute x2 -> x3, starting transfers between devices: 3.97 us -> 8.4 us  [other_core(): return lax.ppermute(value, C, [(0, 1), (1, 0)])]
  transfers between devices with their start and end apart: 11 -> 12, of which waited for: 6 -> 3; matrix products, arithmetic and copies ran while one was open for 0% -> 0% of each run, Pallas kernels for 3% -> 3%
where the time goes in v8:
time: 91.8 us; the launch traced here: 91.6 us
  blocking collectives  52.9 us (58%)
  starting transfers between devices  22 us (24%)
  waiting for transfers between devices  10.7 us (12%)
  Pallas kernels  4.44 us (5%)
  local copies, waits for them, and re-layouts  1.31 us (1%)
    all_to_all x1, blocking collectives, body(): lax.all_to_all(outgoing, DEPTH, split_axis=0, concat_axis=0, tiled=True)  41.3 us
    ppermute x9, starting transfers between devices, shifted_plane(): return lax.ppermute(value, PLANE, pairs)  13.6 us
    all_to_all x1, blocking collectives, body(): pieces = lax.all_to_all(piece, Z, split_axis=0, concat_axis=0, tiled=True)  11.6 us
    ppermute x9, waiting for transfers between devices, shifted_plane(): return lax.ppermute(value, PLANE, pairs)  10.7 us
    ppermute x3, starting transfers between devices, other_core(): return lax.ppermute(value, C, [(0, 1), (1, 0)])  8.4 us
    pallas_call x3, Pallas kernels, image_call(): pl.pallas_call(kernel, out_shape=jax.ShapeDtypeStruct((4, 512, 512), jnp....  3.53 us
  transfers between devices with their start and end apart: 12, of which 3 were waited for; matrix products, arithmetic and copies ran while one was open for 0% of the time, Pallas kernels for 3%

profile of v8, /device:TPU:1, one launch (start us, length us, event | category | flops | bytes accessed | tf_op | source)
XLA Modules:
  0.0 91.6 jit_solution(10957843563438122972)
XLA Ops:
  0.0 0.0 copy-start.2
  0.0 0.0 copy-start
  0.0 1.2 %copy-done = f32[1,4,128,512]{3,2,1,0:T(8,128)S(1)} copy-done((f32[1,4,128,512]{3,2,1,0:T(8,128)S(1)}, f32[1,4,128,512]{3,2,1,0:T(8,128)}, u32[]{:S(2)}) %copy-start) | copy-done | bytes 1048600
  1.2 0.0 copy-start.1
  1.2 0.1 outgoing.1
  1.3 41.3 %all_to_all.10.layers_ref = f32[64,4,8,128]{3,2,1,0:T(8,128)S(1)} all-to-all(f32[64,4,8,128]{3,2,1,0:T(8,128)S(1)} %outgoing.1), channel_id=1, replica_groups=mesh['depth_0'=4,'depth_1'=8,'depth_2'=2,'tile'=4] {'depth_0','depth_1',..., dimensions={0} | all-to-all | bytes 2097152 | tf_op jit(solution)/shard_map/all_to_all | solution.py:141
  42.6 0.0 copy-done.2
  42.6 0.0 copy-done.1
  42.6 0.8 composite.1
  43.5 11.6 %all_to_all.11.pieces_ref = f32[8,4,8,128]{3,2,1,0:T(8,128)S(1)} all-to-all(f32[8,4,8,128]{3,2,1,0:T(8,128)S(1)} %composite.1), channel_id=1, replica_groups=mesh['depth_0'=4,'depth_1'=8,'depth_2'=2,'tile'=4] {'depth_1'}, dimensions={0} | all-to-all | bytes 262144 | tf_op jit(solution)/shard_map/all_to_all | solution.py:151
  55.1 1.4 %collective-permute-start = (f32[4,64,128]{2,1,0:T(8,128)S(1)}, f32[4,64,128]{2,1,0:T(8,128)S(1)}, u32[]{:S(2)}, u32[]{:S(2)}) collective-permute-start(f32[4,64,128]{2,1,0:T(8,128)S(1)} %z_block.1), channel_id=1, source_target_pairs={{0,64},{4,5},{1,65},{5,6},{2,66},{6,7},{3,67},{7,4},{64,128},{68,6... | collective-permute-start | bytes 393224 | tf_op jit(solution)/shard_map/ppermute | solution.py:29
  56.4 2.6 %collective-permute-start.1 = (f32[4,64,128]{2,1,0:T(8,128)S(1)}, f32[4,64,128]{2,1,0:T(8,128)S(1)}, u32[]{:S(2)}, u32[]{:S(2)}) collective-permute-start(f32[4,64,128]{2,1,0:T(8,128)S(1)} %z_block.1), channel_id=1, source_target_pairs={{0,128},{4,6},{1,129},{5,7},{2,130},{6,4},{3,131},{7,5},{64,192},{... | collective-permute-start | bytes 393224 | tf_op jit(solution)/shard_map/ppermute | solution.py:29
  59.0 1.1 %collective-permute-start.5 = (f32[4,64,128]{2,1,0:T(8,128)S(1)}, f32[4,64,128]{2,1,0:T(8,128)S(1)}, u32[]{:S(2)}, u32[]{:S(2)}) collective-permute-start(f32[4,64,128]{2,1,0:T(8,128)S(1)} %z_block.1), channel_id=1, source_target_pairs={{0,192},{4,7},{1,193},{5,4},{2,194},{6,5},{3,195},{7,6},{64,0},{68... | collective-permute-start | bytes 393224 | tf_op jit(solution)/shard_map/ppermute | solution.py:29
  60.1 3.0 %collective-permute-done.5 = f32[4,64,128]{2,1,0:T(8,128)S(1)} collective-permute-done((f32[4,64,128]{2,1,0:T(8,128)S(1)}, f32[4,64,128]{2,1,0:T(8,128)S(1)}, u32[]{:S(2)}, u32[]{:S(2)}) %collective-permute-start.5) | collective-permute-done | bytes 131104 | tf_op jit(solution)/shard_map/ppermute | solution.py:29
  63.2 0.1 collective-permute-start.6
  63.3 3.1 %collective-permute-start.8 = (f32[2,4,64,128]{3,2,1,0:T(8,128)S(1)}, f32[2,4,64,128]{3,2,1,0:T(8,128)S(1)}, u32[]{:S(2)}, u32[]{:S(2)}) collective-permute-start(f32[2,4,64,128]{3,2,1,0:T(8,128)S(1)} %pad_maximum_fusion.3.refs_0_), channel_id=1, source_target_pairs={{0,3},{4,196},{1,0},{5,197},{2,1},{6,198},{3,2},{7,199},{64,67},{6... | collective-permute-start | bytes 786440 | tf_op jit(solution)/shard_map/ppermute | solution.py:29
  66.4 1.1 %collective-permute-start.9 = (f32[2,4,64,128]{3,2,1,0:T(8,128)S(1)}, f32[2,4,64,128]{3,2,1,0:T(8,128)S(1)}, u32[]{:S(2)}, u32[]{:S(2)}) collective-permute-start(f32[2,4,64,128]{3,2,1,0:T(8,128)S(1)} %pad_maximum_fusion.3.refs_0_), channel_id=1, source_target_pairs={{0,2},{4,132},{1,3},{5,133},{2,0},{6,134},{3,1},{7,135},{64,66},{6... | collective-permute-start | bytes 786440 | tf_op jit(solution)/shard_map/ppermute | solution.py:29
  67.5 0.0 collective-permute-done
  67.5 0.0 collective-permute-done.1
  67.5 2.0 %collective-permute-start.10 = (f32[2,4,64,128]{3,2,1,0:T(8,128)S(1)}, f32[2,4,64,128]{3,2,1,0:T(8,128)S(1)}, u32[]{:S(2)}, u32[]{:S(2)}) collective-permute-start(f32[2,4,64,128]{3,2,1,0:T(8,128)S(1)} %pad_maximum_fusion.2.refs_1_), channel_id=1, source_target_pairs={{0,2},{4,132},{1,3},{5,133},{2,0},{6,134},{3,1},{7,135},{64,66},{6... | collective-permute-start | bytes 786440 | tf_op jit(solution)/shard_map/ppermute | solution.py:29
  69.5 1.4 %collective-permute-start.2 = (f32[2,4,64,128]{3,2,1,0:T(8,128)S(1)}, f32[2,4,64,128]{3,2,1,0:T(8,128)S(1)}, u32[]{:S(2)}, u32[]{:S(2)}) collective-permute-start(f32[2,4,64,128]{3,2,1,0:T(8,128)S(1)} %pad_maximum_fusion.2.refs_1_), channel_id=1, source_target_pairs={{0,3},{4,196},{1,0},{5,197},{2,1},{6,198},{3,2},{7,199},{64,67},{6... | collective-permute-start | bytes 786440 | tf_op jit(solution)/shard_map/ppermute | solution.py:29
  70.9 6.2 %collective-permute-done.10.refs_5_ = f32[2,4,64,128]{3,2,1,0:T(8,128)S(1)} collective-permute-done((f32[2,4,64,128]{3,2,1,0:T(8,128)S(1)}, f32[2,4,64,128]{3,2,1,0:T(8,128)S(1)}, u32[]{:S(2)}, u32[]{:S(2)}) %collective-permute-start.10) | collective-permute-done | bytes 262176 | tf_op jit(solution)/shard_map/ppermute | solution.py:29
  77.2 0.9 collective-permute-start.3
  78.1 0.0 collective-permute-done.8.refs_3_
  78.1 0.0 collective-permute-done.9.refs_4_
  78.1 0.1 pad_maximum_fusion
  78.2 3.9 %collective-permute-start.11 = (f32[6,4,64,128]{3,2,1,0:T(8,128)S(1)}, f32[6,4,64,128]{3,2,1,0:T(8,128)S(1)}, u32[]{:S(2)}, u32[]{:S(2)}) collective-permute-start(f32[6,4,64,128]{3,2,1,0:T(8,128)S(1)} %pad_maximum_fusion), channel_id=1, source_target_pairs={{0,4},{4,0},{1,5},{5,1},{2,6},{6,2},{3,7},{7,3},{8,12},{12,8},{9,1... | collective-permute-start | bytes 2359304 | tf_op jit(solution)/shard_map/ppermute | solution.py:33
  82.0 0.0 collective-permute-done.6.refs_2_
  82.1 0.1 collective-permute-start.7
  82.2 0.0 collective-permute-done.2.refs_0_
  82.2 1.4 %collective-permute-done.3.refs_1_ = f32[2,4,64,128]{3,2,1,0:T(8,128)S(1)} collective-permute-done((f32[2,4,64,128]{3,2,1,0:T(8,128)S(1)}, f32[2,4,64,128]{3,2,1,0:T(8,128)S(1)}, u32[]{:S(2)}, u32[]{:S(2)}) %collective-permute-start.3) | collective-permute-done | bytes 262176 | tf_op jit(solution)/shard_map/ppermute | solution.py:29
  83.7 4.4 %collective-permute-start.4 = (f32[4,4,64,128]{3,2,1,0:T(8,128)S(1)}, f32[4,4,64,128]{3,2,1,0:T(8,128)S(1)}, u32[]{:S(2)}, u32[]{:S(2)}) collective-permute-start(f32[4,4,64,128]{3,2,1,0:T(8,128)S(1)} %pad_maximum_fusion.1), channel_id=1, source_target_pairs={{0,4},{4,0},{1,5},{5,1},{2,6},{6,2},{3,7},{7,3},{8,12},{12,8},{9,1... | collective-permute-start | bytes 1572872 | tf_op jit(solution)/shard_map/ppermute | solution.py:33
  88.1 1.2 %shard_map.37.refs_4_ = f32[4,512,512]{2,1,0:T(8,128)} custom-call(f32[2,4,64,128]{3,2,1,0:T(8,128)S(1)} %pad_maximum_fusion.3.refs_0_, f32[2,4,64,128]{3,2,1,0:T(8,128)S(1)} %pad_maximum_fusion.2.refs_1_, f32[2,4,64,128]{3,2,1,0:T(8,128)S(1)} %collective-permute-done.6.refs_2_, f32[2,4,64,128]{3,2,1,0:T(8,128)S(1)} %collective-permute-done.8.refs_3_, ...), custom_call_target="tpu_custom_call" | custom-call | tf_op jit(solution)/shard_map/pallas_call | solution.py:118
  89.3 0.0 collective-permute-done.11.refs_3_
  89.3 0.0 collective-permute-done.7.refs_2_
  89.3 1.5 %shard_map.38.refs_1_ = f32[4,512,512]{2,1,0:T(8,128)} custom-call(f32[2,4,64,128]{3,2,1,0:T(8,128)S(1)} %collective-permute-done.2.refs_0_, f32[2,4,64,128]{3,2,1,0:T(8,128)S(1)} %collective-permute-done.3.refs_1_, f32[6,4,64,128]{3,2,1,0:T(8,128)S(1)} %collective-permute-done.7.refs_2_, ...), custom_call_target="tpu_custom_call", output_to_operand_aliasing={{}: (4, {})} | custom-call | tf_op jit(solution)/shard_map/pallas_call | solution.py:118
  90.8 0.0 collective-permute-done.4.refs_0_
  90.8 0.8 shard_map.39
  (9 shorter events, 0.1 us)
Async XLA Ops:
  0.0 42.6 %copy-start.2 = (s32[64]{0:T(128)S(1)}, s32[64]{0:T(128)}, u32[]{:S(2)}) copy-start(s32[64]{0:T(128)} %order_ref.1) | copy-start | bytes 772
  0.0 1.2 %copy-start = (f32[1,4,128,512]{3,2,1,0:T(8,128)S(1)}, f32[1,4,128,512]{3,2,1,0:T(8,128)}, u32[]{:S(2)}) copy-start(f32[1,4,128,512]{3,2,1,0:T(8,128)} %param.3) | copy-start | bytes 3145732
  1.2 41.4 %copy-start.1 = (s32[64,4]{0,1:T(4,128)S(1)}, s32[64,4]{0,1:T(4,128)}, u32[]{:S(2)}) copy-start(s32[64,4]{0,1:T(4,128)} %param.5) | copy-start | bytes 3076
  55.1 12.5 %collective-permute-start = (f32[4,64,128]{2,1,0:T(8,128)S(1)}, f32[4,64,128]{2,1,0:T(8,128)S(1)}, u32[]{:S(2)}, u32[]{:S(2)}) collective-permute-start(f32[4,64,128]{2,1,0:T(8,128)S(1)} %z_block.1), channel_id=1, source_target_pairs={{0,64},{4,5},{1,65},{5,6},{2,66},{6,7},{3,67},{7,4},{64,128},{68,6... | collective-permute-start | bytes 393224 | tf_op jit(solution)/shard_map/ppermute | solution.py:29
  56.4 11.1 %collective-permute-start.1 = (f32[4,64,128]{2,1,0:T(8,128)S(1)}, f32[4,64,128]{2,1,0:T(8,128)S(1)}, u32[]{:S(2)}, u32[]{:S(2)}) collective-permute-start(f32[4,64,128]{2,1,0:T(8,128)S(1)} %z_block.1), channel_id=1, source_target_pairs={{0,128},{4,6},{1,129},{5,7},{2,130},{6,4},{3,131},{7,5},{64,192},{... | collective-permute-start | bytes 393224 | tf_op jit(solution)/shard_map/ppermute | solution.py:29
  59.0 4.1 %collective-permute-start.5 = (f32[4,64,128]{2,1,0:T(8,128)S(1)}, f32[4,64,128]{2,1,0:T(8,128)S(1)}, u32[]{:S(2)}, u32[]{:S(2)}) collective-permute-start(f32[4,64,128]{2,1,0:T(8,128)S(1)} %z_block.1), channel_id=1, source_target_pairs={{0,192},{4,7},{1,193},{5,4},{2,194},{6,5},{3,195},{7,6},{64,0},{68... | collective-permute-start | bytes 393224 | tf_op jit(solution)/shard_map/ppermute | solution.py:29
  63.2 18.9 %collective-permute-start.6 = (f32[2,4,64,128]{3,2,1,0:T(8,128)S(1)}, f32[2,4,64,128]{3,2,1,0:T(8,128)S(1)}, u32[]{:S(2)}, u32[]{:S(2)}) collective-permute-start(f32[2,4,64,128]{3,2,1,0:T(8,128)S(1)} %pad_maximum_fusion.3.refs_0_), channel_id=1, source_target_pairs={{0,1},{4,68},{1,2},{5,69},{2,3},{6,70},{3,0},{7,71},{64,65},{68,13... | collective-permute-start | bytes 786440 | tf_op jit(solution)/shard_map/ppermute | solution.py:29
  63.3 14.8 %collective-permute-start.8 = (f32[2,4,64,128]{3,2,1,0:T(8,128)S(1)}, f32[2,4,64,128]{3,2,1,0:T(8,128)S(1)}, u32[]{:S(2)}, u32[]{:S(2)}) collective-permute-start(f32[2,4,64,128]{3,2,1,0:T(8,128)S(1)} %pad_maximum_fusion.3.refs_0_), channel_id=1, source_target_pairs={{0,3},{4,196},{1,0},{5,197},{2,1},{6,198},{3,2},{7,199},{64,67},{6... | collective-permute-start | bytes 786440 | tf_op jit(solution)/shard_map/ppermute | solution.py:29
  66.4 11.7 %collective-permute-start.9 = (f32[2,4,64,128]{3,2,1,0:T(8,128)S(1)}, f32[2,4,64,128]{3,2,1,0:T(8,128)S(1)}, u32[]{:S(2)}, u32[]{:S(2)}) collective-permute-start(f32[2,4,64,128]{3,2,1,0:T(8,128)S(1)} %pad_maximum_fusion.3.refs_0_), channel_id=1, source_target_pairs={{0,2},{4,132},{1,3},{5,133},{2,0},{6,134},{3,1},{7,135},{64,66},{6... | collective-permute-start | bytes 786440 | tf_op jit(solution)/shard_map/ppermute | solution.py:29
  67.5 9.6 %collective-permute-start.10 = (f32[2,4,64,128]{3,2,1,0:T(8,128)S(1)}, f32[2,4,64,128]{3,2,1,0:T(8,128)S(1)}, u32[]{:S(2)}, u32[]{:S(2)}) collective-permute-start(f32[2,4,64,128]{3,2,1,0:T(8,128)S(1)} %pad_maximum_fusion.2.refs_1_), channel_id=1, source_target_pairs={{0,2},{4,132},{1,3},{5,133},{2,0},{6,134},{3,1},{7,135},{64,66},{6... | collective-permute-start | bytes 786440 | tf_op jit(solution)/shard_map/ppermute | solution.py:29
  69.5 12.7 %collective-permute-start.2 = (f32[2,4,64,128]{3,2,1,0:T(8,128)S(1)}, f32[2,4,64,128]{3,2,1,0:T(8,128)S(1)}, u32[]{:S(2)}, u32[]{:S(2)}) collective-permute-start(f32[2,4,64,128]{3,2,1,0:T(8,128)S(1)} %pad_maximum_fusion.2.refs_1_), channel_id=1, source_target_pairs={{0,3},{4,196},{1,0},{5,197},{2,1},{6,198},{3,2},{7,199},{64,67},{6... | collective-permute-start | bytes 786440 | tf_op jit(solution)/shard_map/ppermute | solution.py:29
  77.2 6.4 %collective-permute-start.3 = (f32[2,4,64,128]{3,2,1,0:T(8,128)S(1)}, f32[2,4,64,128]{3,2,1,0:T(8,128)S(1)}, u32[]{:S(2)}, u32[]{:S(2)}) collective-permute-start(f32[2,4,64,128]{3,2,1,0:T(8,128)S(1)} %pad_maximum_fusion.2.refs_1_), channel_id=1, source_target_pairs={{0,1},{4,68},{1,2},{5,69},{2,3},{6,70},{3,0},{7,71},{64,65},{68,13... | collective-permute-start | bytes 786440 | tf_op jit(solution)/shard_map/ppermute | solution.py:29
  78.2 11.1 %collective-permute-start.11 = (f32[6,4,64,128]{3,2,1,0:T(8,128)S(1)}, f32[6,4,64,128]{3,2,1,0:T(8,128)S(1)}, u32[]{:S(2)}, u32[]{:S(2)}) collective-permute-start(f32[6,4,64,128]{3,2,1,0:T(8,128)S(1)} %pad_maximum_fusion), channel_id=1, source_target_pairs={{0,4},{4,0},{1,5},{5,1},{2,6},{6,2},{3,7},{7,3},{8,12},{12,8},{9,1... | collective-permute-start | bytes 2359304 | tf_op jit(solution)/shard_map/ppermute | solution.py:33
  82.1 7.3 %collective-permute-start.7 = (f32[6,4,64,128]{3,2,1,0:T(8,128)S(1)}, f32[6,4,64,128]{3,2,1,0:T(8,128)S(1)}, u32[]{:S(2)}, u32[]{:S(2)}) collective-permute-start(f32[6,4,64,128]{3,2,1,0:T(8,128)S(1)} %constant_dynamic-update-slice_fusion), channel_id=1, source_target_pairs={{0,4},{4,0},{1,5},{5,1},{2,6},{6,2},{3,7},{7,3},{8,12},{12,8},{9,1... | collective-permute-start | bytes 2359304 | tf_op jit(solution)/shard_map/ppermute | solution.py:33
  83.7 7.1 %collective-permute-start.4 = (f32[4,4,64,128]{3,2,1,0:T(8,128)S(1)}, f32[4,4,64,128]{3,2,1,0:T(8,128)S(1)}, u32[]{:S(2)}, u32[]{:S(2)}) collective-permute-start(f32[4,4,64,128]{3,2,1,0:T(8,128)S(1)} %pad_maximum_fusion.1), channel_id=1, source_target_pairs={{0,4},{4,0},{1,5},{5,1},{2,6},{6,2},{3,7},{7,3},{8,12},{12,8},{9,1... | collective-permute-start | bytes 1572872 | tf_op jit(solution)/shard_map/ppermute | solution.py:33

commit v9 on v8

--- a/solution.py
+++ b/solution.py
@@ -37,7 +37,7 @@
     count = layers_ref.shape[0]
     tile = lax.axis_index(Y)
 
-    parts = 8
+    parts = 4
     run = count // parts
 
     def step(k, accumulated):
@@ -52,7 +52,7 @@
         return tuple(new)
 
     zero = jnp.zeros(layers_ref.shape[2:], jnp.float32)
-    runs = lax.fori_loop(0, run, step, ((zero,) * 4,) * parts, unroll=8)
+    runs = lax.fori_loop(0, run, step, ((zero,) * 4,) * parts, unroll=4)
     done = runs[0]
     for far in runs[1:]:
         through = 1.0 - done[3]
@@ -185,7 +185,8 @@
     )
     swapped = other_core(jnp.concatenate([part[0] for part in first]))
     swapped_middle = other_core(jnp.concatenate([part[0] for part in middle]))
-    swapped_last = other_core(jnp.concatenate([part[0] for part in last]))
+    swapped_before = other_core(tail_before)
+    swapped_after = other_core(tail_after)
 
     def blocks(parts):
         return [(part, 0, False, *how) for part, *how in parts]
@@ -197,7 +198,8 @@
     image = image_call(
         blocks(last) + from_other(swapped, first) + from_other(swapped_middle, middle), image
     )
-    return image_call(from_other(swapped_last, last), image)
+    parts = from_other(swapped_after, last[:1]) + from_other(swapped_before, last[1:])
+    return image_call(parts, image)
 
 
 def solution(mesh):

time: 91.8 us -> 94.9 us (1.034)
  waiting for transfers between devices: 10.7 us -> 15.5 us
  starting transfers between devices: 22 us -> 20.4 us
    ppermute x9, waiting for transfers between devices: 10.7 us -> 15.4 us  [shifted_plane(): return lax.ppermute(value, PLANE, pairs)]
    ppermute x3 -> x4, starting transfers between devices: 8.4 us -> 7.27 us  [other_core(): return lax.ppermute(value, C, [(0, 1), (1, 0)])]
  transfers between devices with their start and end apart: 12 -> 13, of which waited for: 3 -> 4; matrix products, arithmetic and copies ran while one was open for 0% -> 0% of each run, Pallas kernels for 3% -> 3%
where the time goes in v9:
time: 94.9 us; the launch traced here: 94.7 us
  blocking collectives  52.9 us (56%)
  starting transfers between devices  20.4 us (21%)
  waiting for transfers between devices  15.5 us (16%)
  Pallas kernels  4.42 us (5%)
  local copies, waits for them, and re-layouts  1.31 us (1%)
    all_to_all x1, blocking collectives, body(): lax.all_to_all(outgoing, DEPTH, split_axis=0, concat_axis=0, tiled=True)  41.3 us
    ppermute x9, waiting for transfers between devices, shifted_plane(): return lax.ppermute(value, PLANE, pairs)  15.4 us
    ppermute x9, starting transfers between devices, shifted_plane(): return lax.ppermute(value, PLANE, pairs)  13.1 us
    all_to_all x1, blocking collectives, body(): pieces = lax.all_to_all(piece, Z, split_axis=0, concat_axis=0, tiled=True)  11.6 us
    ppermute x4, starting transfers between devices, other_core(): return lax.ppermute(value, C, [(0, 1), (1, 0)])  7.27 us
    pallas_call x3, Pallas kernels, image_call(): pl.pallas_call(kernel, out_shape=jax.ShapeDtypeStruct((4, 512, 512), jnp....  3.53 us
  transfers between devices with their start and end apart: 13, of which 4 were waited for; matrix products, arithmetic and copies ran while one was open for 0% of the time, Pallas kernels for 3%

profile of v9, /device:TPU:1, one launch (start us, length us, event | category | flops | bytes accessed | tf_op | source)
XLA Modules:
  0.0 94.7 jit_solution(4107406110774047693)
XLA Ops:
  0.0 0.0 copy-start.2
  0.0 0.0 copy-start
  0.0 1.2 %copy-done = f32[1,4,128,512]{3,2,1,0:T(8,128)S(1)} copy-done((f32[1,4,128,512]{3,2,1,0:T(8,128)S(1)}, f32[1,4,128,512]{3,2,1,0:T(8,128)}, u32[]{:S(2)}) %copy-start) | copy-done | bytes 1048600
  1.2 0.0 copy-start.1
  1.2 0.1 outgoing.1
  1.3 41.3 %all_to_all.10.layers_ref = f32[64,4,8,128]{3,2,1,0:T(8,128)S(1)} all-to-all(f32[64,4,8,128]{3,2,1,0:T(8,128)S(1)} %outgoing.1), channel_id=1, replica_groups=mesh['depth_0'=4,'depth_1'=8,'depth_2'=2,'tile'=4] {'depth_0','depth_1',..., dimensions={0} | all-to-all | bytes 2097152 | tf_op jit(solution)/shard_map/all_to_all | solution.py:141
  42.6 0.0 copy-done.2
  42.6 0.0 copy-done.1
  42.6 0.8 composite.1
  43.4 11.6 %all_to_all.11.pieces_ref = f32[8,4,8,128]{3,2,1,0:T(8,128)S(1)} all-to-all(f32[8,4,8,128]{3,2,1,0:T(8,128)S(1)} %composite.1), channel_id=1, replica_groups=mesh['depth_0'=4,'depth_1'=8,'depth_2'=2,'tile'=4] {'depth_1'}, dimensions={0} | all-to-all | bytes 262144 | tf_op jit(solution)/shard_map/all_to_all | solution.py:151
  55.0 1.4 %collective-permute-start = (f32[4,64,128]{2,1,0:T(8,128)S(1)}, f32[4,64,128]{2,1,0:T(8,128)S(1)}, u32[]{:S(2)}, u32[]{:S(2)}) collective-permute-start(f32[4,64,128]{2,1,0:T(8,128)S(1)} %z_block.1), channel_id=1, source_target_pairs={{0,64},{4,5},{1,65},{5,6},{2,66},{6,7},{3,67},{7,4},{64,128},{68,6... | collective-permute-start | bytes 393224 | tf_op jit(solution)/shard_map/ppermute | solution.py:29
  56.4 2.6 %collective-permute-start.1 = (f32[4,64,128]{2,1,0:T(8,128)S(1)}, f32[4,64,128]{2,1,0:T(8,128)S(1)}, u32[]{:S(2)}, u32[]{:S(2)}) collective-permute-start(f32[4,64,128]{2,1,0:T(8,128)S(1)} %z_block.1), channel_id=1, source_target_pairs={{0,128},{4,6},{1,129},{5,7},{2,130},{6,4},{3,131},{7,5},{64,192},{... | collective-permute-start | bytes 393224 | tf_op jit(solution)/shard_map/ppermute | solution.py:29
  59.0 1.1 %collective-permute-start.6 = (f32[4,64,128]{2,1,0:T(8,128)S(1)}, f32[4,64,128]{2,1,0:T(8,128)S(1)}, u32[]{:S(2)}, u32[]{:S(2)}) collective-permute-start(f32[4,64,128]{2,1,0:T(8,128)S(1)} %z_block.1), channel_id=1, source_target_pairs={{0,192},{4,7},{1,193},{5,4},{2,194},{6,5},{3,195},{7,6},{64,0},{68... | collective-permute-start | bytes 393224 | tf_op jit(solution)/shard_map/ppermute | solution.py:29
  60.1 3.0 %collective-permute-done.6 = f32[4,64,128]{2,1,0:T(8,128)S(1)} collective-permute-done((f32[4,64,128]{2,1,0:T(8,128)S(1)}, f32[4,64,128]{2,1,0:T(8,128)S(1)}, u32[]{:S(2)}, u32[]{:S(2)}) %collective-permute-start.6) | collective-permute-done | bytes 131104 | tf_op jit(solution)/shard_map/ppermute | solution.py:29
  63.2 1.9 %collective-permute-start.10 = (f32[2,4,64,128]{3,2,1,0:T(8,128)S(1)}, f32[2,4,64,128]{3,2,1,0:T(8,128)S(1)}, u32[]{:S(2)}, u32[]{:S(2)}) collective-permute-start(f32[2,4,64,128]{3,2,1,0:T(8,128)S(1)} %pad_maximum_fusion.2.refs_0_), channel_id=1, source_target_pairs={{0,2},{4,132},{1,3},{5,133},{2,0},{6,134},{3,1},{7,135},{64,66},{6... | collective-permute-start | bytes 786440 | tf_op jit(solution)/shard_map/ppermute | solution.py:29
  65.1 1.8 %collective-permute-start.7 = (f32[2,4,64,128]{3,2,1,0:T(8,128)S(1)}, f32[2,4,64,128]{3,2,1,0:T(8,128)S(1)}, u32[]{:S(2)}, u32[]{:S(2)}) collective-permute-start(f32[2,4,64,128]{3,2,1,0:T(8,128)S(1)} %pad_maximum_fusion.2.refs_0_), channel_id=1, source_target_pairs={{0,1},{4,68},{1,2},{5,69},{2,3},{6,70},{3,0},{7,71},{64,65},{68,13... | collective-permute-start | bytes 786440 | tf_op jit(solution)/shard_map/ppermute | solution.py:29
  66.9 0.9 collective-permute-start.9
  67.7 0.0 collective-permute-done
  67.7 0.0 collective-permute-done.1
  67.8 1.0 %collective-permute-start.11 = (f32[2,4,64,128]{3,2,1,0:T(8,128)S(1)}, f32[2,4,64,128]{3,2,1,0:T(8,128)S(1)}, u32[]{:S(2)}, u32[]{:S(2)}) collective-permute-start(f32[2,4,64,128]{3,2,1,0:T(8,128)S(1)} %pad_maximum_fusion.1.refs_1_), channel_id=1, source_target_pairs={{0,2},{4,132},{1,3},{5,133},{2,0},{6,134},{3,1},{7,135},{64,66},{6... | collective-permute-start | bytes 786440 | tf_op jit(solution)/shard_map/ppermute | solution.py:29
  68.8 6.8 %collective-permute-done.11.refs_5_ = f32[2,4,64,128]{3,2,1,0:T(8,128)S(1)} collective-permute-done((f32[2,4,64,128]{3,2,1,0:T(8,128)S(1)}, f32[2,4,64,128]{3,2,1,0:T(8,128)S(1)}, u32[]{:S(2)}, u32[]{:S(2)}) %collective-permute-start.11) | collective-permute-done | bytes 262176 | tf_op jit(solution)/shard_map/ppermute | solution.py:29
  75.6 0.0 collective-permute-done.10.refs_4_
  75.6 0.0 collective-permute-done.9.refs_3_
  75.6 0.1 pad_maximum_fusion
  75.7 4.8 %collective-permute-start.12 = (f32[6,4,64,128]{3,2,1,0:T(8,128)S(1)}, f32[6,4,64,128]{3,2,1,0:T(8,128)S(1)}, u32[]{:S(2)}, u32[]{:S(2)}) collective-permute-start(f32[6,4,64,128]{3,2,1,0:T(8,128)S(1)} %pad_maximum_fusion), channel_id=1, source_target_pairs={{0,4},{4,0},{1,5},{5,1},{2,6},{6,2},{3,7},{7,3},{8,12},{12,8},{9,1... | collective-permute-start | bytes 2359304 | tf_op jit(solution)/shard_map/ppermute | solution.py:33
  80.5 0.0 collective-permute-done.7.refs_2_
  80.5 0.1 collective-permute-start.8
  80.6 2.5 %collective-permute-start.2 = (f32[2,4,64,128]{3,2,1,0:T(8,128)S(1)}, f32[2,4,64,128]{3,2,1,0:T(8,128)S(1)}, u32[]{:S(2)}, u32[]{:S(2)}) collective-permute-start(f32[2,4,64,128]{3,2,1,0:T(8,128)S(1)} %pad_maximum_fusion.1.refs_1_), channel_id=1, source_target_pairs={{0,3},{4,196},{1,0},{5,197},{2,1},{6,198},{3,2},{7,199},{64,67},{6... | collective-permute-start | bytes 786440 | tf_op jit(solution)/shard_map/ppermute | solution.py:29
  83.1 0.0 collective-permute-start.4
  83.1 3.3 %collective-permute-done.2.refs_0_ = f32[2,4,64,128]{3,2,1,0:T(8,128)S(1)} collective-permute-done((f32[2,4,64,128]{3,2,1,0:T(8,128)S(1)}, f32[2,4,64,128]{3,2,1,0:T(8,128)S(1)}, u32[]{:S(2)}, u32[]{:S(2)}) %collective-permute-start.2) | collective-permute-done | bytes 262176 | tf_op jit(solution)/shard_map/ppermute | solution.py:29
  86.4 1.1 %collective-permute-start.3 = (f32[2,4,64,128]{3,2,1,0:T(8,128)S(1)}, f32[2,4,64,128]{3,2,1,0:T(8,128)S(1)}, u32[]{:S(2)}, u32[]{:S(2)}) collective-permute-start(f32[2,4,64,128]{3,2,1,0:T(8,128)S(1)} %collective-permute-done.2.refs_0_), channel_id=1, source_target_pairs={{0,4},{4,0},{1,5},{5,1},{2,6},{6,2},{3,7},{7,3},{8,12},{12,8},{9,1... | collective-permute-start | bytes 786440 | tf_op jit(solution)/shard_map/ppermute | solution.py:33
  87.5 2.3 %collective-permute-done.4.refs_1_ = f32[2,4,64,128]{3,2,1,0:T(8,128)S(1)} collective-permute-done((f32[2,4,64,128]{3,2,1,0:T(8,128)S(1)}, f32[2,4,64,128]{3,2,1,0:T(8,128)S(1)}, u32[]{:S(2)}, u32[]{:S(2)}) %collective-permute-start.4) | collective-permute-done | bytes 262176 | tf_op jit(solution)/shard_map/ppermute | solution.py:29
  89.8 1.3 %collective-permute-start.5 = (f32[2,4,64,128]{3,2,1,0:T(8,128)S(1)}, f32[2,4,64,128]{3,2,1,0:T(8,128)S(1)}, u32[]{:S(2)}, u32[]{:S(2)}) collective-permute-start(f32[2,4,64,128]{3,2,1,0:T(8,128)S(1)} %collective-permute-done.4.refs_1_), channel_id=1, source_target_pairs={{0,4},{4,0},{1,5},{5,1},{2,6},{6,2},{3,7},{7,3},{8,12},{12,8},{9,1... | collective-permute-start | bytes 786440 | tf_op jit(solution)/shard_map/ppermute | solution.py:33
  91.1 1.2 %shard_map.37.refs_4_ = f32[4,512,512]{2,1,0:T(8,128)} custom-call(f32[2,4,64,128]{3,2,1,0:T(8,128)S(1)} %pad_maximum_fusion.2.refs_0_, f32[2,4,64,128]{3,2,1,0:T(8,128)S(1)} %pad_maximum_fusion.1.refs_1_, f32[2,4,64,128]{3,2,1,0:T(8,128)S(1)} %collective-permute-done.7.refs_2_, f32[2,4,64,128]{3,2,1,0:T(8,128)S(1)} %collective-permute-done.9.refs_3_, ...), custom_call_target="tpu_custom_call" | custom-call | tf_op jit(solution)/shard_map/pallas_call | solution.py:118
  92.3 0.0 collective-permute-done.12.refs_3_
  92.3 0.0 collective-permute-done.8.refs_2_
  92.3 1.5 %shard_map.38.refs_2_ = f32[4,512,512]{2,1,0:T(8,128)} custom-call(f32[2,4,64,128]{3,2,1,0:T(8,128)S(1)} %collective-permute-done.2.refs_0_, f32[2,4,64,128]{3,2,1,0:T(8,128)S(1)} %collective-permute-done.4.refs_1_, f32[6,4,64,128]{3,2,1,0:T(8,128)S(1)} %collective-permute-done.8.refs_2_, ...), custom_call_target="tpu_custom_call", output_to_operand_aliasing={{}: (4, {})} | custom-call | tf_op jit(solution)/shard_map/pallas_call | solution.py:118
  93.8 0.0 collective-permute-done.3.refs_0_
  93.8 0.0 collective-permute-done.5.refs_1_
  93.8 0.8 shard_map.39
  (8 shorter events, 0.1 us)
Async XLA Ops:
  0.0 42.6 %copy-start.2 = (s32[64]{0:T(128)S(1)}, s32[64]{0:T(128)}, u32[]{:S(2)}) copy-start(s32[64]{0:T(128)} %order_ref.1) | copy-start | bytes 772
  0.0 1.2 %copy-start = (f32[1,4,128,512]{3,2,1,0:T(8,128)S(1)}, f32[1,4,128,512]{3,2,1,0:T(8,128)}, u32[]{:S(2)}) copy-start(f32[1,4,128,512]{3,2,1,0:T(8,128)} %param.3) | copy-start | bytes 3145732
  1.2 41.4 %copy-start.1 = (s32[64,4]{0,1:T(4,128)S(1)}, s32[64,4]{0,1:T(4,128)}, u32[]{:S(2)}) copy-start(s32[64,4]{0,1:T(4,128)} %param.5) | copy-start | bytes 3076
  55.0 12.7 %collective-permute-start = (f32[4,64,128]{2,1,0:T(8,128)S(1)}, f32[4,64,128]{2,1,0:T(8,128)S(1)}, u32[]{:S(2)}, u32[]{:S(2)}) collective-permute-start(f32[4,64,128]{2,1,0:T(8,128)S(1)} %z_block.1), channel_id=1, source_target_pairs={{0,64},{4,5},{1,65},{5,6},{2,66},{6,7},{3,67},{7,4},{64,128},{68,6... | collective-permute-start | bytes 393224 | tf_op jit(solution)/shard_map/ppermute | solution.py:29
  56.4 11.3 %collective-permute-start.1 = (f32[4,64,128]{2,1,0:T(8,128)S(1)}, f32[4,64,128]{2,1,0:T(8,128)S(1)}, u32[]{:S(2)}, u32[]{:S(2)}) collective-permute-start(f32[4,64,128]{2,1,0:T(8,128)S(1)} %z_block.1), channel_id=1, source_target_pairs={{0,128},{4,6},{1,129},{5,7},{2,130},{6,4},{3,131},{7,5},{64,192},{... | collective-permute-start | bytes 393224 | tf_op jit(solution)/shard_map/ppermute | solution.py:29
  59.0 4.1 %collective-permute-start.6 = (f32[4,64,128]{2,1,0:T(8,128)S(1)}, f32[4,64,128]{2,1,0:T(8,128)S(1)}, u32[]{:S(2)}, u32[]{:S(2)}) collective-permute-start(f32[4,64,128]{2,1,0:T(8,128)S(1)} %z_block.1), channel_id=1, source_target_pairs={{0,192},{4,7},{1,193},{5,4},{2,194},{6,5},{3,195},{7,6},{64,0},{68... | collective-permute-start | bytes 393224 | tf_op jit(solution)/shard_map/ppermute | solution.py:29
  63.2 12.4 %collective-permute-start.10 = (f32[2,4,64,128]{3,2,1,0:T(8,128)S(1)}, f32[2,4,64,128]{3,2,1,0:T(8,128)S(1)}, u32[]{:S(2)}, u32[]{:S(2)}) collective-permute-start(f32[2,4,64,128]{3,2,1,0:T(8,128)S(1)} %pad_maximum_fusion.2.refs_0_), channel_id=1, source_target_pairs={{0,2},{4,132},{1,3},{5,133},{2,0},{6,134},{3,1},{7,135},{64,66},{6... | collective-permute-start | bytes 786440 | tf_op jit(solution)/shard_map/ppermute | solution.py:29
  65.1 15.4 %collective-permute-start.7 = (f32[2,4,64,128]{3,2,1,0:T(8,128)S(1)}, f32[2,4,64,128]{3,2,1,0:T(8,128)S(1)}, u32[]{:S(2)}, u32[]{:S(2)}) collective-permute-start(f32[2,4,64,128]{3,2,1,0:T(8,128)S(1)} %pad_maximum_fusion.2.refs_0_), channel_id=1, source_target_pairs={{0,1},{4,68},{1,2},{5,69},{2,3},{6,70},{3,0},{7,71},{64,65},{68,13... | collective-permute-start | bytes 786440 | tf_op jit(solution)/shard_map/ppermute | solution.py:29
  66.9 8.7 %collective-permute-start.9 = (f32[2,4,64,128]{3,2,1,0:T(8,128)S(1)}, f32[2,4,64,128]{3,2,1,0:T(8,128)S(1)}, u32[]{:S(2)}, u32[]{:S(2)}) collective-permute-start(f32[2,4,64,128]{3,2,1,0:T(8,128)S(1)} %pad_maximum_fusion.2.refs_0_), channel_id=1, source_target_pairs={{0,3},{4,196},{1,0},{5,197},{2,1},{6,198},{3,2},{7,199},{64,67},{6... | collective-permute-start | bytes 786440 | tf_op jit(solution)/shard_map/ppermute | solution.py:29
  67.8 7.8 %collective-permute-start.11 = (f32[2,4,64,128]{3,2,1,0:T(8,128)S(1)}, f32[2,4,64,128]{3,2,1,0:T(8,128)S(1)}, u32[]{:S(2)}, u32[]{:S(2)}) collective-permute-start(f32[2,4,64,128]{3,2,1,0:T(8,128)S(1)} %pad_maximum_fusion.1.refs_1_), channel_id=1, source_target_pairs={{0,2},{4,132},{1,3},{5,133},{2,0},{6,134},{3,1},{7,135},{64,66},{6... | collective-permute-start | bytes 786440 | tf_op jit(solution)/shard_map/ppermute | solution.py:29
  75.7 16.6 %collective-permute-start.12 = (f32[6,4,64,128]{3,2,1,0:T(8,128)S(1)}, f32[6,4,64,128]{3,2,1,0:T(8,128)S(1)}, u32[]{:S(2)}, u32[]{:S(2)}) collective-permute-start(f32[6,4,64,128]{3,2,1,0:T(8,128)S(1)} %pad_maximum_fusion), channel_id=1, source_target_pairs={{0,4},{4,0},{1,5},{5,1},{2,6},{6,2},{3,7},{7,3},{8,12},{12,8},{9,1... | collective-permute-start | bytes 2359304 | tf_op jit(solution)/shard_map/ppermute | solution.py:33
  80.5 11.8 %collective-permute-start.8 = (f32[6,4,64,128]{3,2,1,0:T(8,128)S(1)}, f32[6,4,64,128]{3,2,1,0:T(8,128)S(1)}, u32[]{:S(2)}, u32[]{:S(2)}) collective-permute-start(f32[6,4,64,128]{3,2,1,0:T(8,128)S(1)} %constant_dynamic-update-slice_fusion), channel_id=1, source_target_pairs={{0,4},{4,0},{1,5},{5,1},{2,6},{6,2},{3,7},{7,3},{8,12},{12,8},{9,1... | collective-permute-start | bytes 2359304 | tf_op jit(solution)/shard_map/ppermute | solution.py:33
  80.6 5.8 %collective-permute-start.2 = (f32[2,4,64,128]{3,2,1,0:T(8,128)S(1)}, f32[2,4,64,128]{3,2,1,0:T(8,128)S(1)}, u32[]{:S(2)}, u32[]{:S(2)}) collective-permute-start(f32[2,4,64,128]{3,2,1,0:T(8,128)S(1)} %pad_maximum_fusion.1.refs_1_), channel_id=1, source_target_pairs={{0,3},{4,196},{1,0},{5,197},{2,1},{6,198},{3,2},{7,199},{64,67},{6... | collective-permute-start | bytes 786440 | tf_op jit(solution)/shard_map/ppermute | solution.py:29
  83.1 6.7 %collective-permute-start.4 = (f32[2,4,64,128]{3,2,1,0:T(8,128)S(1)}, f32[2,4,64,128]{3,2,1,0:T(8,128)S(1)}, u32[]{:S(2)}, u32[]{:S(2)}) collective-permute-start(f32[2,4,64,128]{3,2,1,0:T(8,128)S(1)} %pad_maximum_fusion.1.refs_1_), channel_id=1, source_target_pairs={{0,1},{4,68},{1,2},{5,69},{2,3},{6,70},{3,0},{7,71},{64,65},{68,13... | collective-permute-start | bytes 786440 | tf_op jit(solution)/shard_map/ppermute | solution.py:29
  86.4 7.4 %collective-permute-start.3 = (f32[2,4,64,128]{3,2,1,0:T(8,128)S(1)}, f32[2,4,64,128]{3,2,1,0:T(8,128)S(1)}, u32[]{:S(2)}, u32[]{:S(2)}) collective-permute-start(f32[2,4,64,128]{3,2,1,0:T(8,128)S(1)} %collective-permute-done.2.refs_0_), channel_id=1, source_target_pairs={{0,4},{4,0},{1,5},{5,1},{2,6},{6,2},{3,7},{7,3},{8,12},{12,8},{9,1... | collective-permute-start | bytes 786440 | tf_op jit(solution)/shard_map/ppermute | solution.py:33
  89.8 4.0 %collective-permute-start.5 = (f32[2,4,64,128]{3,2,1,0:T(8,128)S(1)}, f32[2,4,64,128]{3,2,1,0:T(8,128)S(1)}, u32[]{:S(2)}, u32[]{:S(2)}) collective-permute-start(f32[2,4,64,128]{3,2,1,0:T(8,128)S(1)} %collective-permute-done.4.refs_1_), channel_id=1, source_target_pairs={{0,4},{4,0},{1,5},{5,1},{2,6},{6,2},{3,7},{7,3},{8,12},{12,8},{9,1... | collective-permute-start | bytes 786440 | tf_op jit(solution)/shard_map/ppermute | solution.py:33
